TPU v7x, 32 devices: a whole 2x2x4 slice. The times are simulated.
32 devices in a mesh: dp: 4 (over y, x), sp: 4 (over z), shift: 2 (over core).
Axes of the slice: x: 2, y: 2, z: 4, core: 2. Of those that a mesh axis runs over, the one named last changes fastest.
Arguments:
- query_rows: bfloat16 [8, 1024, 32, 128], P(('shift', 'dp'), 'sp'), parts along dimension 0, may hold values from -6 to 6
- key_rows: bfloat16 [8, 1024, 32, 128], P(('shift', 'dp'), 'sp'), parts along dimension 0, may hold values from -6 to 6
- value_rows: bfloat16 [8, 1024, 32, 128], P(('shift', 'dp'), 'sp'), parts along dimension 0, may hold values from -6 to 6
- out_weight: bfloat16 [8192, 4096], P(('shift', 'dp')), parts along dimension 0, may hold values from -0.09375 to 0.09375
Outputs:
- mixer_out: bfloat16 [8, 1024, 4096], P(('shift', 'dp'), 'sp'), parts along dimension 0
There are 2 independent parts, one for each index of `shift`. A program takes and returns all parts, laid end to end along the dimension named above; each array names one. Nothing has to cross between parts.
All inputs are finite; a program needn't handle non-finite values.
Results may differ from a plain program's by a relative error of at most 0.006.
Values may be sent and summed in bfloat16 or wider, within the bound.
No kernel may reach another device: no remote copies, remote signals or barrier semaphores. Data moves between devices by JAX's collectives and lax.ppermute only.
A program may use at most 128 MiB of HBM per device.

v0:
```python
import functools
import math

import jax
import jax.numpy as jnp
from jax import lax
from jax.experimental import pallas as pl
from jax.experimental.pallas import tpu as pltpu
from jax.sharding import PartitionSpec as P


F32, BF16 = jnp.float32, jnp.bfloat16
CHUNKS = 2
MIB = 1 << 20


def ring_order(n):
    side = math.isqrt(n)
    if side * side != n or side % 2:
        return list(range(n))
    order = list(range(side))
    for row in range(1, side):
        cols = range(1, side)
        order += [row * side + c for c in (reversed(cols) if row % 2 else cols)]
    order += [row * side for row in range(side - 1, 0, -1)]
    return order


def feature_map(values):
    wide = values.astype(F32)
    return jnp.where(wide > 0.0, wide + 1.0, jnp.exp(jnp.minimum(wide, 0.0))).astype(BF16)


def cost(flops, nbytes):
    return pl.CostEstimate(flops=flops, bytes_accessed=nbytes, transcendentals=0)


def split_mass(mass):
    high = mass.astype(BF16)
    low = (mass - high.astype(F32)).astype(BF16)
    return jnp.concatenate([high, low], axis=0)


def state_kernel(parts, table, here, place, key, value, *refs):
    outs, (keys, values, states) = refs[:parts], refs[parts:]
    tokens, heads, size = key.shape[1:]
    rows = heads * size // parts
    feature = feature_map(key[0]).astype(F32)
    mass = split_mass(jnp.sum(feature, axis=0))
    keys[...] = feature.reshape(tokens * heads, size)
    values[...] = value[0].astype(F32).reshape(tokens * heads, size)
    for h in range(heads):
        states[h * size : (h + 1) * size, :] = lax.dot_general(
            keys[pl.ds(h, tokens, stride=heads), :].astype(BF16),
            values[pl.ds(h, tokens, stride=heads), :].astype(BF16),
            (((0,), (0,)), ((), ())),
            preferred_element_type=F32,
        )
    for j in range(parts):
        start = pl.multiple_of(lax.rem(place[0] + j, parts) * rows, rows)
        outs[j][0, :rows, :] = states[pl.ds(start, rows), :].astype(BF16)
        outs[j][0, rows:, :] = mass


def partial_states(key, value, table, here, place, blocks, heads, parts):
    _, tokens, _, size = key.shape
    rows = heads * size // parts + 2 * heads
    block = pl.BlockSpec((1, tokens, heads, size), lambda i, t, d, p: (0, 0, t[d[0] * blocks + i], 0))
    return pl.pallas_call(
        functools.partial(state_kernel, parts),
        grid_spec=pltpu.PrefetchScalarGridSpec(
            num_scalar_prefetch=3,
            grid=(blocks,),
            in_specs=[block, block],
            out_specs=[pl.BlockSpec((1, rows, size), lambda i, t, d, p: (i, 0, 0))] * parts,
            scratch_shapes=[
                pltpu.VMEM((tokens * heads, size), F32),
                pltpu.VMEM((tokens * heads, size), F32),
                pltpu.VMEM((heads * size, size), F32),
            ],
        ),
        out_shape=[jax.ShapeDtypeStruct((blocks, rows, size), BF16)] * parts,
        cost_estimate=cost(blocks * heads * tokens * size * size * 2, blocks * heads * tokens * size * 4),
        compiler_params=pltpu.CompilerParams(vmem_limit_bytes=56 * MIB),
        name="partial_states",
    )(table, here, place, key, value)


def total_kernel(blocks, heads, count, *refs):
    takes, outs = refs[:-blocks], refs[-blocks:]
    rows = takes[0].shape[1] - 2 * heads
    for b in range(blocks):
        total = takes[0][b].astype(F32)
        for take in takes[1:]:
            total = total + take[b].astype(F32)
        total = total / count
        outs[b][:rows, :] = total[:rows].astype(BF16)
        mass = total[rows : rows + heads] + total[rows + heads :]
        outs[b][rows:, :] = split_mass(mass)


def total_states(takes, heads, count):
    blocks, rows, size = takes[0].shape
    return pl.pallas_call(
        functools.partial(total_kernel, blocks, heads, count),
        out_shape=[jax.ShapeDtypeStruct((rows, size), BF16)] * blocks,
        cost_estimate=cost(blocks * rows * size * 8, blocks * rows * size * 10),
        compiler_params=pltpu.CompilerParams(vmem_limit_bytes=8 * MIB),
        name="total_states",
    )(*takes)


def read_kernel(parts, scale, block, place, query, mass, *refs):
    pieces, (out, queries, states) = refs[:parts], refs[parts:]
    tokens, heads, size = query.shape[1:]
    rows = heads * size // parts
    for j in range(parts):
        start = pl.multiple_of(lax.rem(place[0] + parts - j, parts) * rows, rows)
        states[pl.ds(start, rows), :] = pieces[j][0, :rows, :]
    queries[...] = feature_map(query[0]).astype(F32).reshape(tokens * heads, size)
    masses = mass[...].astype(F32)
    masses = (masses[:heads] + masses[heads:]).T
    none = jnp.zeros((size, size), BF16)
    for h in range(heads):
        feature = queries[pl.ds(h, tokens, stride=heads), :].astype(BF16)
        whole = jnp.broadcast_to(masses[:, h : h + 1], (size, size))
        high = whole.astype(BF16)
        low = (whole - high.astype(F32)).astype(BF16)
        state = jnp.concatenate([states[h * size : (h + 1) * size, :], none], axis=0)
        both = jnp.concatenate([state, jnp.concatenate([high, low], axis=0)], axis=1)
        read = jnp.dot(
            jnp.concatenate([feature, feature], axis=1), both, preferred_element_type=F32
        )
        result = read[:, :size] / (read[:, size:] + 0.001) * scale
        out[:, h * size : (h + 1) * size] = result.astype(BF16)


def read_states(query, own, pieces, slot, block, heads, place, scale):
    parts = len(pieces)
    _, tokens, _, size = query.shape
    rows = own.shape[0]
    return pl.pallas_call(
        functools.partial(read_kernel, parts, scale),
        grid_spec=pltpu.PrefetchScalarGridSpec(
            num_scalar_prefetch=2,
            grid=(1,),
            in_specs=[
                pl.BlockSpec((1, tokens, heads, size), lambda i, b, p: (0, 0, b[0], 0)),
                pl.BlockSpec((2 * heads, size), lambda i, b, p: (rows // (2 * heads) - 1, 0)),
            ]
            + [pl.BlockSpec((1, rows, size), lambda i, b, p: (slot, 0, 0))] * parts,
            out_specs=pl.BlockSpec((tokens, heads * size), lambda i, b, p: (0, 0)),
            scratch_shapes=[
                pltpu.VMEM((tokens * heads, size), F32),
                pltpu.VMEM((heads * size, size), BF16),
            ],
        ),
        out_shape=jax.ShapeDtypeStruct((tokens, heads * size), BF16),
        cost_estimate=cost(heads * tokens * size * size * 8, heads * tokens * size * 4),
        compiler_params=pltpu.CompilerParams(vmem_limit_bytes=12 * MIB),
        name="read_states",
    )(block, place, query, own, *pieces)


def partial_states_plain(key, value, table, here, place, blocks, heads, parts):
    _, _, _, size = key.shape
    outs = [[] for _ in range(parts)]
    for b in range(blocks):
        start = table[here[0] * blocks + b] * heads
        key_block = feature_map(lax.dynamic_slice_in_dim(key[0], start, heads, 1))
        value_block = lax.dynamic_slice_in_dim(value[0], start, heads, 1)
        state = jnp.einsum("thd,the->hde", key_block, value_block, preferred_element_type=F32)
        state = state.reshape(heads * size, size).astype(BF16)
        mass = split_mass(jnp.sum(key_block.astype(F32), axis=0))
        rows = heads * size // parts
        for j in range(parts):
            piece = lax.dynamic_slice_in_dim(state, lax.rem(place[0] + j, parts) * rows, rows, 0)
            outs[j].append(jnp.concatenate([piece, mass]))
    return [jnp.stack(out) for out in outs]


def total_states_plain(takes, heads, count):
    total = sum(take.astype(F32) for take in takes) / count
    rows = total.shape[1] - 2 * heads
    mass = total[:, rows : rows + heads] + total[:, rows + heads :]
    return [
        jnp.concatenate([total[b, :rows].astype(BF16), split_mass(mass[b])])
        for b in range(total.shape[0])
    ]


def read_states_plain(query, own, pieces, slot, block, heads, place, scale):
    parts = len(pieces)
    _, tokens, _, size = query.shape
    query = lax.dynamic_slice_in_dim(query[0], block[0] * heads, heads, 1)
    mass = own[-2 * heads :].astype(F32)
    stack = jnp.stack([piece[slot, : -2 * heads] for piece in pieces])
    order = lax.rem(place[0] + parts - jnp.arange(parts), parts)
    state = stack[order].reshape(heads, size, size)
    feature = feature_map(query)
    top = jnp.einsum("thd,hde->the", feature, state, preferred_element_type=F32)
    bottom = jnp.einsum(
        "thd,hd->th",
        feature.astype(F32),
        mass[:heads] + mass[heads:],
        precision=lax.Precision.HIGHEST,
    )
    read = top / (bottom + 0.001)[..., None] * scale
    return read.astype(BF16).reshape(tokens, heads * size)


def layer(query_rows, key_rows, value_rows, out_weight):
    n, parts = lax.axis_size("dp"), lax.axis_size("sp")
    _, tokens, all_heads, size = query_rows.shape
    heads, width = all_heads // n, out_weight.shape[1]
    count = tokens * parts
    fits = heads % 8 == 0 and (heads * size) % (16 * parts) == 0
    make_partial = partial_states if fits else partial_states_plain
    make_total = total_states if fits else total_states_plain
    make_read = read_states if fits else read_states_plain

    ring = ring_order(n)
    to = [[ring[(ring.index(d) + o) % n] for o in range(n)] for d in range(n)]
    here = lax.axis_index("dp").reshape(1)
    place = lax.axis_index("sp").reshape(1)

    def block_of(offset):
        found = jnp.int32(to[0][offset])
        for d in range(1, n):
            found = jnp.where(here[0] == d, to[d][offset], found)
        return found

    def around(x, offset):
        return lax.ppermute(x, "dp", [(d, to[d][offset % n]) for d in range(n)])

    def along(x, offset):
        return lax.ppermute(x, "sp", [(i, (i + offset) % parts) for i in range(parts)])

    groups = [sorted({1, n - 1}), list(range(2, n - 1)) + [0]] if n > 1 else [[0]]

    takes, queries, mixed = [], {}, {}
    for group in groups:
        table = jnp.array([to[d][o] for d in range(n) for o in group], jnp.int32)
        sent = make_partial(key_rows, value_rows, table, here, place, len(group), heads, parts)
        takes.append([sent[0]] + [along(sent[j], j) for j in range(1, parts)])
        for o in group:
            if o:
                piece = lax.dynamic_slice_in_dim(query_rows, block_of(o) * heads, heads, 2)
                queries[-o % n] = around(piece, o)
    for group, take in zip(groups, takes):
        totals = make_total(take, heads, count)
        owns = [around(totals[i], o) if o else totals[i] for i, o in enumerate(group)]
        stack = jnp.stack(owns)
        pieces = [stack] + [along(stack, j) for j in range(1, parts)]
        for i, o in enumerate(group):
            slot = -o % n
            query, block = (queries[slot], jnp.zeros(1, jnp.int32)) if o else (query_rows, here)
            mixed[slot] = make_read(
                query, owns[i], pieces, i, block, heads, place, count**0.5
            )

    lanes = []
    step = width // (2 * CHUNKS)
    for c in range(2 * CHUNKS):
        way = 1 if c % 2 == 0 else -1
        lanes.append((way, out_weight[:, c * step : (c + 1) * step]))
    accs = []
    for way, weight in lanes:
        acc = jnp.dot(mixed[-way % n], weight, preferred_element_type=F32).astype(BF16)
        accs.append(acc)
    for k in range(1, n):
        for lane, (way, weight) in enumerate(lanes):
            taken = around(accs[lane], way).astype(F32)
            product = jnp.dot(mixed[-way * (k + 1) % n], weight, preferred_element_type=F32)
            accs[lane] = (product + taken).astype(BF16)
    return jnp.concatenate(accs, axis=1)[None]


def solution(mesh):
    rows = P(("shift", "dp"), "sp", None, None)
    return jax.shard_map(
        layer,
        mesh=mesh,
        in_specs=(rows, rows, rows, P(("shift", "dp"), None)),
        out_specs=P(("shift", "dp"), "sp", None),
        check_vma=False,
    )
```

profile of v0, /device:TPU:0, one launch (start us, length us, event | category | flops | bytes accessed | tf_op | source)
XLA Modules:
  0.0 152.6 jit_solution(17384033655077021638)
XLA Ops:
  0.0 4.5 %partial_states.2 = (bf16[2,272,128]{2,1,0:T(8,128)(2,1)}, bf16[2,272,128]{2,1,0:T(8,128)(2,1)}, bf16[2,272,128]{2,1,0:T(8,128)(2,1)}, bf16[2,272,128]{2,1,0:T(8,128)(2,1)}) custom-call(s32[8]{0:T(128)} %constant.28.clone.table, s32[1]{0:T(128)} %bitcast.here.block, s32[1]{0:T(128)} %bitcast.1.place, bf16[1,256,32,128]{3,2,1,0:T(8,128)(2,1)} %key.3, ...), custom_call_target="tpu_custom_call" | custom-call | flops 134217728 | bytes 2097152 | tf_op jit(solution)/shard_map/partial_states/pallas_call | solution.py:69
  4.6 3.1 %collective-permute-start = (bf16[2,272,128]{2,1,0:T(8,128)(2,1)}, bf16[2,272,128]{2,1,0:T(8,128)(2,1)S(1)}, u32[]{:S(2)}, u32[]{:S(2)}) collective-permute-start(bf16[2,272,128]{2,1,0:T(8,128)(2,1)} %get-tuple-element.18), channel_id=1, source_target_pairs={{0,2},{2,4},{4,6},{6,0},{1,3},{3,5},{5,7},{7,1},{8,10},{10,12},{12... | collective-permute-start | bytes 417800 | tf_op jit(solution)/shard_map/ppermute | solution.py:237
  7.7 4.6 %partial_states.3 = (bf16[2,272,128]{2,1,0:T(8,128)(2,1)}, bf16[2,272,128]{2,1,0:T(8,128)(2,1)}, bf16[2,272,128]{2,1,0:T(8,128)(2,1)}, bf16[2,272,128]{2,1,0:T(8,128)(2,1)}) custom-call(s32[8]{0:T(128)} %constant.27.clone.table, s32[1]{0:T(128)} %bitcast.here.block, s32[1]{0:T(128)} %bitcast.1.place, bf16[1,256,32,128]{3,2,1,0:T(8,128)(2,1)} %key.3, ...), custom_call_target="tpu_custom_call" | custom-call | flops 134217728 | bytes 2097152 | tf_op jit(solution)/shard_map/partial_states/pallas_call | solution.py:69
  12.2 2.2 %collective-permute-start.10 = (bf16[2,272,128]{2,1,0:T(8,128)(2,1)}, bf16[2,272,128]{2,1,0:T(8,128)(2,1)S(1)}, u32[]{:S(2)}, u32[]{:S(2)}) collective-permute-start(bf16[2,272,128]{2,1,0:T(8,128)(2,1)} %get-tuple-element.26), channel_id=1, source_target_pairs={{0,6},{2,0},{4,2},{6,4},{1,7},{3,1},{5,3},{7,5},{8,14},{10,8},{12,... | collective-permute-start | bytes 417800 | tf_op jit(solution)/shard_map/ppermute | solution.py:237
  14.5 2.4 %collective-permute-start.9 = (bf16[2,272,128]{2,1,0:T(8,128)(2,1)}, bf16[2,272,128]{2,1,0:T(8,128)(2,1)S(1)}, u32[]{:S(2)}, u32[]{:S(2)}) collective-permute-start(bf16[2,272,128]{2,1,0:T(8,128)(2,1)} %get-tuple-element.25), channel_id=1, source_target_pairs={{0,4},{2,6},{4,0},{6,2},{1,5},{3,7},{5,1},{7,3},{8,12},{10,14},{12... | collective-permute-start | bytes 417800 | tf_op jit(solution)/shard_map/ppermute | solution.py:237
  17.4 3.8 %collective-permute-start.2 = (bf16[2,272,128]{2,1,0:T(8,128)(2,1)S(1)}, bf16[2,272,128]{2,1,0:T(8,128)(2,1)S(1)}, u32[]{:S(2)}, u32[]{:S(2)}) collective-permute-start(bf16[2,272,128]{2,1,0:T(8,128)(2,1)S(1)} %copy-done.4), channel_id=1, source_target_pairs={{0,6},{2,0},{4,2},{6,4},{1,7},{3,1},{5,3},{7,5},{8,14},{10,8},{12,... | collective-permute-start | bytes 417800 | tf_op jit(solution)/shard_map/ppermute | solution.py:237
  21.5 13.0 %collective-permute-done.1.refs_2_ = bf16[2,272,128]{2,1,0:T(8,128)(2,1)S(1)} collective-permute-done((bf16[2,272,128]{2,1,0:T(8,128)(2,1)S(1)}, bf16[2,272,128]{2,1,0:T(8,128)(2,1)S(1)}, u32[]{:S(2)}, u32[]{:S(2)}) %collective-permute-start.1) | collective-permute-done | bytes 139296 | tf_op jit(solution)/shard_map/ppermute | solution.py:237
  34.5 1.5 collective-permute-start.17
  36.1 1.6 %collective-permute-start.3 = (bf16[272,128]{1,0:T(8,128)(2,1)S(1)}, bf16[272,128]{1,0:T(8,128)(2,1)S(1)}, u32[]{:S(2)}, u32[]{:S(2)}) collective-permute-start(bf16[272,128]{1,0:T(8,128)(2,1)S(1)} %get-tuple-element.22), channel_id=1, source_target_pairs={{0,24},{8,16},{16,8},{24,0},{1,25},{9,17},{17,9},{25,1},{2,26},{10... | collective-permute-start | bytes 208904 | tf_op jit(solution)/shard_map/ppermute | solution.py:234
  38.3 1.5 collective-permute-start.11
  39.8 10.0 %collective-permute-done.3.mass = bf16[272,128]{1,0:T(8,128)(2,1)S(1)} collective-permute-done((bf16[272,128]{1,0:T(8,128)(2,1)S(1)}, bf16[272,128]{1,0:T(8,128)(2,1)S(1)}, u32[]{:S(2)}, u32[]{:S(2)}) %collective-permute-start.3) | collective-permute-done | bytes 69664 | tf_op jit(solution)/shard_map/ppermute | solution.py:234
  49.8 3.1 %collective-permute-start.4 = (bf16[2,272,128]{2,1,0:T(8,128)(2,1)S(1)}, bf16[2,272,128]{2,1,0:T(8,128)(2,1)S(1)}, u32[]{:S(2)}, u32[]{:S(2)}) collective-permute-start(bf16[2,272,128]{2,1,0:T(8,128)(2,1)S(1)} %pad_maximum_fusion.refs_0_), channel_id=1, source_target_pairs={{0,2},{2,4},{4,6},{6,0},{1,3},{3,5},{5,7},{7,1},{8,10},{10,12},{12... | collective-permute-start | bytes 417800 | tf_op jit(solution)/shard_map/ppermute | solution.py:237
  52.9 3.4 %collective-permute-start.5 = (bf16[2,272,128]{2,1,0:T(8,128)(2,1)S(1)}, bf16[2,272,128]{2,1,0:T(8,128)(2,1)S(1)}, u32[]{:S(2)}, u32[]{:S(2)}) collective-permute-start(bf16[2,272,128]{2,1,0:T(8,128)(2,1)S(1)} %pad_maximum_fusion.refs_0_), channel_id=1, source_target_pairs={{0,4},{2,6},{4,0},{6,2},{1,5},{3,7},{5,1},{7,3},{8,12},{10,14},{12... | collective-permute-start | bytes 417800 | tf_op jit(solution)/shard_map/ppermute | solution.py:237
  57.0 3.3 %collective-permute-done.4.refs_1_ = bf16[2,272,128]{2,1,0:T(8,128)(2,1)S(1)} collective-permute-done((bf16[2,272,128]{2,1,0:T(8,128)(2,1)S(1)}, bf16[2,272,128]{2,1,0:T(8,128)(2,1)S(1)}, u32[]{:S(2)}, u32[]{:S(2)}) %collective-permute-start.4) | collective-permute-done | bytes 139296 | tf_op jit(solution)/shard_map/ppermute | solution.py:237
  60.6 7.4 %collective-permute-done.5.refs_2_ = bf16[2,272,128]{2,1,0:T(8,128)(2,1)S(1)} collective-permute-done((bf16[2,272,128]{2,1,0:T(8,128)(2,1)S(1)}, bf16[2,272,128]{2,1,0:T(8,128)(2,1)S(1)}, u32[]{:S(2)}, u32[]{:S(2)}) %collective-permute-start.5) | collective-permute-done | bytes 139296 | tf_op jit(solution)/shard_map/ppermute | solution.py:237
  69.7 1.6 %collective-permute-start.16 = (bf16[1,256,8,128]{3,2,1,0:T(8,128)(2,1)S(1)}, bf16[1,256,8,128]{3,2,1,0:T(8,128)(2,1)S(1)}, u32[]{:S(2)}, u32[]{:S(2)}) collective-permute-start(bf16[1,256,8,128]{3,2,1,0:T(8,128)(2,1)S(1)} %get-tuple-element.31), channel_id=1, source_target_pairs={{0,24},{8,16},{16,8},{24,0},{1,25},{9,17},{17,9},{25,1},{2,26},{10... | collective-permute-start | bytes 1572872 | tf_op jit(solution)/shard_map/ppermute | solution.py:234
  71.3 4.2 %collective-permute-done.14.refs_2_ = bf16[2,272,128]{2,1,0:T(8,128)(2,1)S(1)} collective-permute-done((bf16[2,272,128]{2,1,0:T(8,128)(2,1)S(1)}, bf16[2,272,128]{2,1,0:T(8,128)(2,1)S(1)}, u32[]{:S(2)}, u32[]{:S(2)}) %collective-permute-start.14) | collective-permute-done | bytes 139296 | tf_op jit(solution)/shard_map/ppermute | solution.py:237
  75.5 1.9 %collective-permute-done.15.refs_3_ = bf16[2,272,128]{2,1,0:T(8,128)(2,1)S(1)} collective-permute-done((bf16[2,272,128]{2,1,0:T(8,128)(2,1)S(1)}, bf16[2,272,128]{2,1,0:T(8,128)(2,1)S(1)}, u32[]{:S(2)}, u32[]{:S(2)}) %collective-permute-start.15) | collective-permute-done | bytes 139296 | tf_op jit(solution)/shard_map/ppermute | solution.py:237
  80.9 2.1 %collective-permute-start.21 = (bf16[256,1024]{1,0:T(8,128)(2,1)S(1)}, bf16[256,1024]{1,0:T(8,128)(2,1)S(1)}, u32[]{:S(2)}, u32[]{:S(2)}) collective-permute-start(bf16[256,1024]{1,0:T(8,128)(2,1)S(1)} %fusion.23), channel_id=1, source_target_pairs={{0,16},{8,0},{16,24},{24,8},{1,17},{9,1},{17,25},{25,9},{2,18},{10... | collective-permute-start | bytes 1572872 | tf_op jit(solution)/shard_map/ppermute | solution.py:234
  84.5 2.1 %collective-permute-start.27 = (bf16[256,1024]{1,0:T(8,128)(2,1)S(1)}, bf16[256,1024]{1,0:T(8,128)(2,1)S(1)}, u32[]{:S(2)}, u32[]{:S(2)}) collective-permute-start(bf16[256,1024]{1,0:T(8,128)(2,1)S(1)} %fusion.29), channel_id=1, source_target_pairs={{0,16},{8,0},{16,24},{24,8},{1,17},{9,1},{17,25},{25,9},{2,18},{10... | collective-permute-start | bytes 1572872 | tf_op jit(solution)/shard_map/ppermute | solution.py:234
  87.5 6.5 %collective-permute-done.18 = bf16[256,1024]{1,0:T(8,128)(2,1)S(1)} collective-permute-done((bf16[256,1024]{1,0:T(8,128)(2,1)S(1)}, bf16[256,1024]{1,0:T(8,128)(2,1)S(1)}, u32[]{:S(2)}, u32[]{:S(2)}) %collective-permute-start.18) | collective-permute-done | bytes 524320 | tf_op jit(solution)/shard_map/ppermute | solution.py:234
  96.5 2.2 %collective-permute-start.22 = (bf16[256,1024]{1,0:T(8,128)(2,1)S(1)}, bf16[256,1024]{1,0:T(8,128)(2,1)S(1)}, u32[]{:S(2)}, u32[]{:S(2)}) collective-permute-start(bf16[256,1024]{1,0:T(8,128)(2,1)S(1)} %fusion.47), channel_id=1, source_target_pairs={{0,16},{8,0},{16,24},{24,8},{1,17},{9,1},{17,25},{25,9},{2,18},{10... | collective-permute-start | bytes 1572872 | tf_op jit(solution)/shard_map/ppermute | solution.py:234
  98.7 6.5 %collective-permute-done.24 = bf16[256,1024]{1,0:T(8,128)(2,1)S(1)} collective-permute-done((bf16[256,1024]{1,0:T(8,128)(2,1)S(1)}, bf16[256,1024]{1,0:T(8,128)(2,1)S(1)}, u32[]{:S(2)}, u32[]{:S(2)}) %collective-permute-start.24) | collective-permute-done | bytes 524320 | tf_op jit(solution)/shard_map/ppermute | solution.py:234
  107.7 2.1 %collective-permute-start.28 = (bf16[256,1024]{1,0:T(8,128)(2,1)S(1)}, bf16[256,1024]{1,0:T(8,128)(2,1)S(1)}, u32[]{:S(2)}, u32[]{:S(2)}) collective-permute-start(bf16[256,1024]{1,0:T(8,128)(2,1)S(1)} %fusion.65), channel_id=1, source_target_pairs={{0,16},{8,0},{16,24},{24,8},{1,17},{9,1},{17,25},{25,9},{2,18},{10... | collective-permute-start | bytes 1572872 | tf_op jit(solution)/shard_map/ppermute | solution.py:234
  109.8 6.7 %collective-permute-done.19 = bf16[256,1024]{1,0:T(8,128)(2,1)S(1)} collective-permute-done((bf16[256,1024]{1,0:T(8,128)(2,1)S(1)}, bf16[256,1024]{1,0:T(8,128)(2,1)S(1)}, u32[]{:S(2)}, u32[]{:S(2)}) %collective-permute-start.19) | collective-permute-done | bytes 524320 | tf_op jit(solution)/shard_map/ppermute | solution.py:234
  118.9 2.1 %collective-permute-start.23 = (bf16[256,1024]{1,0:T(8,128)(2,1)S(1)}, bf16[256,1024]{1,0:T(8,128)(2,1)S(1)}, u32[]{:S(2)}, u32[]{:S(2)}) collective-permute-start(bf16[256,1024]{1,0:T(8,128)(2,1)S(1)} %fusion.44), channel_id=1, source_target_pairs={{0,16},{8,0},{16,24},{24,8},{1,17},{9,1},{17,25},{25,9},{2,18},{10... | collective-permute-start | bytes 1572872 | tf_op jit(solution)/shard_map/ppermute | solution.py:234
  121.0 6.7 %collective-permute-done.25 = bf16[256,1024]{1,0:T(8,128)(2,1)S(1)} collective-permute-done((bf16[256,1024]{1,0:T(8,128)(2,1)S(1)}, bf16[256,1024]{1,0:T(8,128)(2,1)S(1)}, u32[]{:S(2)}, u32[]{:S(2)}) %collective-permute-start.25) | collective-permute-done | bytes 524320 | tf_op jit(solution)/shard_map/ppermute | solution.py:234
  130.2 2.1 %collective-permute-start.29 = (bf16[256,1024]{1,0:T(8,128)(2,1)S(1)}, bf16[256,1024]{1,0:T(8,128)(2,1)S(1)}, u32[]{:S(2)}, u32[]{:S(2)}) collective-permute-start(bf16[256,1024]{1,0:T(8,128)(2,1)S(1)} %fusion.62), channel_id=1, source_target_pairs={{0,16},{8,0},{16,24},{24,8},{1,17},{9,1},{17,25},{25,9},{2,18},{10... | collective-permute-start | bytes 1572872 | tf_op jit(solution)/shard_map/ppermute | solution.py:234
  132.2 6.7 %collective-permute-done.20 = bf16[256,1024]{1,0:T(8,128)(2,1)S(1)} collective-permute-done((bf16[256,1024]{1,0:T(8,128)(2,1)S(1)}, bf16[256,1024]{1,0:T(8,128)(2,1)S(1)}, u32[]{:S(2)}, u32[]{:S(2)}) %collective-permute-start.20) | collective-permute-done | bytes 524320 | tf_op jit(solution)/shard_map/ppermute | solution.py:234
  141.4 7.2 %collective-permute-done.26 = bf16[256,1024]{1,0:T(8,128)(2,1)S(1)} collective-permute-done((bf16[256,1024]{1,0:T(8,128)(2,1)S(1)}, bf16[256,1024]{1,0:T(8,128)(2,1)S(1)}, u32[]{:S(2)}, u32[]{:S(2)}) %collective-permute-start.26) | collective-permute-done | bytes 524320 | tf_op jit(solution)/shard_map/ppermute | solution.py:234
  149.4 1.0 collective-permute-done.29
  151.1 1.5 maximum_bitcast_fusion
  (68 shorter events, 23.9 us)
Async XLA Ops:
  4.6 12.8 %collective-permute-start = (bf16[2,272,128]{2,1,0:T(8,128)(2,1)}, bf16[2,272,128]{2,1,0:T(8,128)(2,1)S(1)}, u32[]{:S(2)}, u32[]{:S(2)}) collective-permute-start(bf16[2,272,128]{2,1,0:T(8,128)(2,1)} %get-tuple-element.18), channel_id=1, source_target_pairs={{0,2},{2,4},{4,6},{6,0},{1,3},{3,5},{5,7},{7,1},{8,10},{10,12},{12... | collective-permute-start | bytes 417800 | tf_op jit(solution)/shard_map/ppermute | solution.py:237
  12.2 25.4 %copy-start.1 = (bf16[2,272,128]{2,1,0:T(8,128)(2,1)S(1)}, bf16[2,272,128]{2,1,0:T(8,128)(2,1)}, u32[]{:S(2)}) copy-start(bf16[2,272,128]{2,1,0:T(8,128)(2,1)} %get-tuple-element.23.refs_0_) | copy-start | bytes 417796
  12.2 25.4 %collective-permute-start.10 = (bf16[2,272,128]{2,1,0:T(8,128)(2,1)}, bf16[2,272,128]{2,1,0:T(8,128)(2,1)S(1)}, u32[]{:S(2)}, u32[]{:S(2)}) collective-permute-start(bf16[2,272,128]{2,1,0:T(8,128)(2,1)} %get-tuple-element.26), channel_id=1, source_target_pairs={{0,6},{2,0},{4,2},{6,4},{1,7},{3,1},{5,3},{7,5},{8,14},{10,8},{12,... | collective-permute-start | bytes 417800 | tf_op jit(solution)/shard_map/ppermute | solution.py:237
  14.5 23.2 %collective-permute-start.8 = (bf16[2,272,128]{2,1,0:T(8,128)(2,1)}, bf16[2,272,128]{2,1,0:T(8,128)(2,1)S(1)}, u32[]{:S(2)}, u32[]{:S(2)}) collective-permute-start(bf16[2,272,128]{2,1,0:T(8,128)(2,1)} %get-tuple-element.24), channel_id=1, source_target_pairs={{0,2},{2,4},{4,6},{6,0},{1,3},{3,5},{5,7},{7,1},{8,10},{10,12},{12... | collective-permute-start | bytes 417800 | tf_op jit(solution)/shard_map/ppermute | solution.py:237
  14.5 23.2 %collective-permute-start.9 = (bf16[2,272,128]{2,1,0:T(8,128)(2,1)}, bf16[2,272,128]{2,1,0:T(8,128)(2,1)S(1)}, u32[]{:S(2)}, u32[]{:S(2)}) collective-permute-start(bf16[2,272,128]{2,1,0:T(8,128)(2,1)} %get-tuple-element.25), channel_id=1, source_target_pairs={{0,4},{2,6},{4,0},{6,2},{1,5},{3,7},{5,1},{7,3},{8,12},{10,14},{12... | collective-permute-start | bytes 417800 | tf_op jit(solution)/shard_map/ppermute | solution.py:237
  16.9 17.6 %collective-permute-start.1 = (bf16[2,272,128]{2,1,0:T(8,128)(2,1)S(1)}, bf16[2,272,128]{2,1,0:T(8,128)(2,1)S(1)}, u32[]{:S(2)}, u32[]{:S(2)}) collective-permute-start(bf16[2,272,128]{2,1,0:T(8,128)(2,1)S(1)} %copy-done.5), channel_id=1, source_target_pairs={{0,4},{2,6},{4,0},{6,2},{1,5},{3,7},{5,1},{7,3},{8,12},{10,14},{12... | collective-permute-start | bytes 417800 | tf_op jit(solution)/shard_map/ppermute | solution.py:237
  17.4 18.6 %collective-permute-start.2 = (bf16[2,272,128]{2,1,0:T(8,128)(2,1)S(1)}, bf16[2,272,128]{2,1,0:T(8,128)(2,1)S(1)}, u32[]{:S(2)}, u32[]{:S(2)}) collective-permute-start(bf16[2,272,128]{2,1,0:T(8,128)(2,1)S(1)} %copy-done.4), channel_id=1, source_target_pairs={{0,6},{2,0},{4,2},{6,4},{1,7},{3,1},{5,3},{7,5},{8,14},{10,8},{12,... | collective-permute-start | bytes 417800 | tf_op jit(solution)/shard_map/ppermute | solution.py:237
  21.2 57.2 %copy-start.3 = (bf16[1024,4096]{1,0:T(8,128)(2,1)S(1)}, bf16[1024,4096]{1,0:T(8,128)(2,1)}, u32[]{:S(2)}) copy-start(bf16[1024,4096]{1,0:T(8,128)(2,1)} %param.9) | copy-start | bytes 25165828
  34.5 42.9 %collective-permute-start.17 = (bf16[1,256,8,128]{3,2,1,0:T(8,128)(2,1)S(1)}, bf16[1,256,8,128]{3,2,1,0:T(8,128)(2,1)S(1)}, u32[]{:S(2)}, u32[]{:S(2)}) collective-permute-start(bf16[1,256,8,128]{3,2,1,0:T(8,128)(2,1)S(1)} %get-tuple-element.30), channel_id=1, source_target_pairs={{0,8},{8,24},{16,0},{24,16},{1,9},{9,25},{17,1},{25,17},{2,10},{10... | collective-permute-start | bytes 1572872 | tf_op jit(solution)/shard_map/ppermute | solution.py:234
  36.1 13.7 %collective-permute-start.3 = (bf16[272,128]{1,0:T(8,128)(2,1)S(1)}, bf16[272,128]{1,0:T(8,128)(2,1)S(1)}, u32[]{:S(2)}, u32[]{:S(2)}) collective-permute-start(bf16[272,128]{1,0:T(8,128)(2,1)S(1)} %get-tuple-element.22), channel_id=1, source_target_pairs={{0,24},{8,16},{16,8},{24,0},{1,25},{9,17},{17,9},{25,1},{2,26},{10... | collective-permute-start | bytes 208904 | tf_op jit(solution)/shard_map/ppermute | solution.py:234
  37.7 18.5 %collective-permute-start.12 = (bf16[272,128]{1,0:T(8,128)(2,1)S(1)}, bf16[272,128]{1,0:T(8,128)(2,1)S(1)}, u32[]{:S(2)}, u32[]{:S(2)}) collective-permute-start(bf16[272,128]{1,0:T(8,128)(2,1)S(1)} %get-tuple-element.28), channel_id=1, source_target_pairs={{0,8},{8,24},{16,0},{24,16},{1,9},{9,25},{17,1},{25,17},{2,10},{10... | collective-permute-start | bytes 208904 | tf_op jit(solution)/shard_map/ppermute | solution.py:234
  38.3 18.0 %collective-permute-start.11 = (bf16[272,128]{1,0:T(8,128)(2,1)S(1)}, bf16[272,128]{1,0:T(8,128)(2,1)S(1)}, u32[]{:S(2)}, u32[]{:S(2)}) collective-permute-start(bf16[272,128]{1,0:T(8,128)(2,1)S(1)} %get-tuple-element.27), channel_id=1, source_target_pairs={{0,16},{8,0},{16,24},{24,8},{1,17},{9,1},{17,25},{25,9},{2,18},{10... | collective-permute-start | bytes 208904 | tf_op jit(solution)/shard_map/ppermute | solution.py:234
  49.8 10.5 %collective-permute-start.4 = (bf16[2,272,128]{2,1,0:T(8,128)(2,1)S(1)}, bf16[2,272,128]{2,1,0:T(8,128)(2,1)S(1)}, u32[]{:S(2)}, u32[]{:S(2)}) collective-permute-start(bf16[2,272,128]{2,1,0:T(8,128)(2,1)S(1)} %pad_maximum_fusion.refs_0_), channel_id=1, source_target_pairs={{0,2},{2,4},{4,6},{6,0},{1,3},{3,5},{5,7},{7,1},{8,10},{10,12},{12... | collective-permute-start | bytes 417800 | tf_op jit(solution)/shard_map/ppermute | solution.py:237
  52.9 15.1 %collective-permute-start.5 = (bf16[2,272,128]{2,1,0:T(8,128)(2,1)S(1)}, bf16[2,272,128]{2,1,0:T(8,128)(2,1)S(1)}, u32[]{:S(2)}, u32[]{:S(2)}) collective-permute-start(bf16[2,272,128]{2,1,0:T(8,128)(2,1)S(1)} %pad_maximum_fusion.refs_0_), channel_id=1, source_target_pairs={{0,4},{2,6},{4,0},{6,2},{1,5},{3,7},{5,1},{7,3},{8,12},{10,14},{12... | collective-permute-start | bytes 417800 | tf_op jit(solution)/shard_map/ppermute | solution.py:237
  56.3 11.8 %collective-permute-start.6 = (bf16[2,272,128]{2,1,0:T(8,128)(2,1)S(1)}, bf16[2,272,128]{2,1,0:T(8,128)(2,1)S(1)}, u32[]{:S(2)}, u32[]{:S(2)}) collective-permute-start(bf16[2,272,128]{2,1,0:T(8,128)(2,1)S(1)} %pad_maximum_fusion.refs_0_), channel_id=1, source_target_pairs={{0,6},{2,0},{4,2},{6,4},{1,7},{3,1},{5,3},{7,5},{8,14},{10,8},{12,... | collective-permute-start | bytes 417800 | tf_op jit(solution)/shard_map/ppermute | solution.py:237
  56.3 22.9 %collective-permute-start.7 = (bf16[1,256,8,128]{3,2,1,0:T(8,128)(2,1)S(1)}, bf16[1,256,8,128]{3,2,1,0:T(8,128)(2,1)S(1)}, u32[]{:S(2)}, u32[]{:S(2)}) collective-permute-start(bf16[1,256,8,128]{3,2,1,0:T(8,128)(2,1)S(1)} %get-tuple-element.29), channel_id=1, source_target_pairs={{0,16},{8,0},{16,24},{24,8},{1,17},{9,1},{17,25},{25,9},{2,18},{10... | collective-permute-start | bytes 1572872 | tf_op jit(solution)/shard_map/ppermute | solution.py:234
  60.3 9.4 %collective-permute-start.13 = (bf16[2,272,128]{2,1,0:T(8,128)(2,1)S(1)}, bf16[2,272,128]{2,1,0:T(8,128)(2,1)S(1)}, u32[]{:S(2)}, u32[]{:S(2)}) collective-permute-start(bf16[2,272,128]{2,1,0:T(8,128)(2,1)S(1)} %pad_maximum_fusion.1.refs_0_), channel_id=1, source_target_pairs={{0,2},{2,4},{4,6},{6,0},{1,3},{3,5},{5,7},{7,1},{8,10},{10,12},{12... | collective-permute-start | bytes 417800 | tf_op jit(solution)/shard_map/ppermute | solution.py:237
  68.0 7.5 %collective-permute-start.14 = (bf16[2,272,128]{2,1,0:T(8,128)(2,1)S(1)}, bf16[2,272,128]{2,1,0:T(8,128)(2,1)S(1)}, u32[]{:S(2)}, u32[]{:S(2)}) collective-permute-start(bf16[2,272,128]{2,1,0:T(8,128)(2,1)S(1)} %pad_maximum_fusion.1.refs_0_), channel_id=1, source_target_pairs={{0,4},{2,6},{4,0},{6,2},{1,5},{3,7},{5,1},{7,3},{8,12},{10,14},{12... | collective-permute-start | bytes 417800 | tf_op jit(solution)/shard_map/ppermute | solution.py:237
  68.0 9.4 %collective-permute-start.15 = (bf16[2,272,128]{2,1,0:T(8,128)(2,1)S(1)}, bf16[2,272,128]{2,1,0:T(8,128)(2,1)S(1)}, u32[]{:S(2)}, u32[]{:S(2)}) collective-permute-start(bf16[2,272,128]{2,1,0:T(8,128)(2,1)S(1)} %pad_maximum_fusion.1.refs_0_), channel_id=1, source_target_pairs={{0,6},{2,0},{4,2},{6,4},{1,7},{3,1},{5,3},{7,5},{8,14},{10,8},{12,... | collective-permute-start | bytes 417800 | tf_op jit(solution)/shard_map/ppermute | solution.py:237
  69.7 16.8 %collective-permute-start.16 = (bf16[1,256,8,128]{3,2,1,0:T(8,128)(2,1)S(1)}, bf16[1,256,8,128]{3,2,1,0:T(8,128)(2,1)S(1)}, u32[]{:S(2)}, u32[]{:S(2)}) collective-permute-start(bf16[1,256,8,128]{3,2,1,0:T(8,128)(2,1)S(1)} %get-tuple-element.31), channel_id=1, source_target_pairs={{0,24},{8,16},{16,8},{24,0},{1,25},{9,17},{17,9},{25,1},{2,26},{10... | collective-permute-start | bytes 1572872 | tf_op jit(solution)/shard_map/ppermute | solution.py:234
  79.1 14.8 %collective-permute-start.18 = (bf16[256,1024]{1,0:T(8,128)(2,1)S(1)}, bf16[256,1024]{1,0:T(8,128)(2,1)S(1)}, u32[]{:S(2)}, u32[]{:S(2)}) collective-permute-start(bf16[256,1024]{1,0:T(8,128)(2,1)S(1)} %fusion.20), channel_id=1, source_target_pairs={{0,8},{8,24},{16,0},{24,16},{1,9},{9,25},{17,1},{25,17},{2,10},{10... | collective-permute-start | bytes 1572872 | tf_op jit(solution)/shard_map/ppermute | solution.py:234
  80.9 14.8 %collective-permute-start.21 = (bf16[256,1024]{1,0:T(8,128)(2,1)S(1)}, bf16[256,1024]{1,0:T(8,128)(2,1)S(1)}, u32[]{:S(2)}, u32[]{:S(2)}) collective-permute-start(bf16[256,1024]{1,0:T(8,128)(2,1)S(1)} %fusion.23), channel_id=1, source_target_pairs={{0,16},{8,0},{16,24},{24,8},{1,17},{9,1},{17,25},{25,9},{2,18},{10... | collective-permute-start | bytes 1572872 | tf_op jit(solution)/shard_map/ppermute | solution.py:234
  83.7 21.5 %collective-permute-start.24 = (bf16[256,1024]{1,0:T(8,128)(2,1)S(1)}, bf16[256,1024]{1,0:T(8,128)(2,1)S(1)}, u32[]{:S(2)}, u32[]{:S(2)}) collective-permute-start(bf16[256,1024]{1,0:T(8,128)(2,1)S(1)} %fusion.26), channel_id=1, source_target_pairs={{0,8},{8,24},{16,0},{24,16},{1,9},{9,25},{17,1},{25,17},{2,10},{10... | collective-permute-start | bytes 1572872 | tf_op jit(solution)/shard_map/ppermute | solution.py:234
  84.5 22.5 %collective-permute-start.27 = (bf16[256,1024]{1,0:T(8,128)(2,1)S(1)}, bf16[256,1024]{1,0:T(8,128)(2,1)S(1)}, u32[]{:S(2)}, u32[]{:S(2)}) collective-permute-start(bf16[256,1024]{1,0:T(8,128)(2,1)S(1)} %fusion.29), channel_id=1, source_target_pairs={{0,16},{8,0},{16,24},{24,8},{1,17},{9,1},{17,25},{25,9},{2,18},{10... | collective-permute-start | bytes 1572872 | tf_op jit(solution)/shard_map/ppermute | solution.py:234
  94.7 21.7 %collective-permute-start.19 = (bf16[256,1024]{1,0:T(8,128)(2,1)S(1)}, bf16[256,1024]{1,0:T(8,128)(2,1)S(1)}, u32[]{:S(2)}, u32[]{:S(2)}) collective-permute-start(bf16[256,1024]{1,0:T(8,128)(2,1)S(1)} %fusion.38), channel_id=1, source_target_pairs={{0,8},{8,24},{16,0},{24,16},{1,9},{9,25},{17,1},{25,17},{2,10},{10... | collective-permute-start | bytes 1572872 | tf_op jit(solution)/shard_map/ppermute | solution.py:234
  96.5 21.7 %collective-permute-start.22 = (bf16[256,1024]{1,0:T(8,128)(2,1)S(1)}, bf16[256,1024]{1,0:T(8,128)(2,1)S(1)}, u32[]{:S(2)}, u32[]{:S(2)}) collective-permute-start(bf16[256,1024]{1,0:T(8,128)(2,1)S(1)} %fusion.47), channel_id=1, source_target_pairs={{0,16},{8,0},{16,24},{24,8},{1,17},{9,1},{17,25},{25,9},{2,18},{10... | collective-permute-start | bytes 1572872 | tf_op jit(solution)/shard_map/ppermute | solution.py:234
  106.0 21.7 %collective-permute-start.25 = (bf16[256,1024]{1,0:T(8,128)(2,1)S(1)}, bf16[256,1024]{1,0:T(8,128)(2,1)S(1)}, u32[]{:S(2)}, u32[]{:S(2)}) collective-permute-start(bf16[256,1024]{1,0:T(8,128)(2,1)S(1)} %fusion.56), channel_id=1, source_target_pairs={{0,8},{8,24},{16,0},{24,16},{1,9},{9,25},{17,1},{25,17},{2,10},{10... | collective-permute-start | bytes 1572872 | tf_op jit(solution)/shard_map/ppermute | solution.py:234
  107.7 21.7 %collective-permute-start.28 = (bf16[256,1024]{1,0:T(8,128)(2,1)S(1)}, bf16[256,1024]{1,0:T(8,128)(2,1)S(1)}, u32[]{:S(2)}, u32[]{:S(2)}) collective-permute-start(bf16[256,1024]{1,0:T(8,128)(2,1)S(1)} %fusion.65), channel_id=1, source_target_pairs={{0,16},{8,0},{16,24},{24,8},{1,17},{9,1},{17,25},{25,9},{2,18},{10... | collective-permute-start | bytes 1572872 | tf_op jit(solution)/shard_map/ppermute | solution.py:234
  117.2 21.7 %collective-permute-start.20 = (bf16[256,1024]{1,0:T(8,128)(2,1)S(1)}, bf16[256,1024]{1,0:T(8,128)(2,1)S(1)}, u32[]{:S(2)}, u32[]{:S(2)}) collective-permute-start(bf16[256,1024]{1,0:T(8,128)(2,1)S(1)} %fusion.35), channel_id=1, source_target_pairs={{0,8},{8,24},{16,0},{24,16},{1,9},{9,25},{17,1},{25,17},{2,10},{10... | collective-permute-start | bytes 1572872 | tf_op jit(solution)/shard_map/ppermute | solution.py:234
  118.9 21.7 %collective-permute-start.23 = (bf16[256,1024]{1,0:T(8,128)(2,1)S(1)}, bf16[256,1024]{1,0:T(8,128)(2,1)S(1)}, u32[]{:S(2)}, u32[]{:S(2)}) collective-permute-start(bf16[256,1024]{1,0:T(8,128)(2,1)S(1)} %fusion.44), channel_id=1, source_target_pairs={{0,16},{8,0},{16,24},{24,8},{1,17},{9,1},{17,25},{25,9},{2,18},{10... | collective-permute-start | bytes 1572872 | tf_op jit(solution)/shard_map/ppermute | solution.py:234
  128.4 20.2 %collective-permute-start.26 = (bf16[256,1024]{1,0:T(8,128)(2,1)S(1)}, bf16[256,1024]{1,0:T(8,128)(2,1)S(1)}, u32[]{:S(2)}, u32[]{:S(2)}) collective-permute-start(bf16[256,1024]{1,0:T(8,128)(2,1)S(1)} %fusion.53), channel_id=1, source_target_pairs={{0,8},{8,24},{16,0},{24,16},{1,9},{9,25},{17,1},{25,17},{2,10},{10... | collective-permute-start | bytes 1572872 | tf_op jit(solution)/shard_map/ppermute | solution.py:234
  130.2 20.2 %collective-permute-start.29 = (bf16[256,1024]{1,0:T(8,128)(2,1)S(1)}, bf16[256,1024]{1,0:T(8,128)(2,1)S(1)}, u32[]{:S(2)}, u32[]{:S(2)}) collective-permute-start(bf16[256,1024]{1,0:T(8,128)(2,1)S(1)} %fusion.62), channel_id=1, source_target_pairs={{0,16},{8,0},{16,24},{24,8},{1,17},{9,1},{17,25},{25,9},{2,18},{10... | collective-permute-start | bytes 1572872 | tf_op jit(solution)/shard_map/ppermute | solution.py:234
  (4 other events, 65.7 us)
where the time goes:
time: 154 us; the launch traced here: 153 us
  waiting for transfers between devices  86 us (56%)
  starting transfers between devices  39.8 us (26%)
  Pallas kernels  13.1 us (9%)
  matrix products  11.6 us (8%)
    ppermute x18, waiting for transfers between devices, around(): return lax.ppermute(x, 'dp', [(d, to[d][offset % n]) for d in range(n)])  56.1 us
    ppermute x12, waiting for transfers between devices, along(): lax.ppermute(x, 'sp', [(i, (i + offset) % parts) for i in range(parts)])  29.8 us
    ppermute x18, starting transfers between devices, around(): return lax.ppermute(x, 'dp', [(d, to[d][offset % n]) for d in range(n)])  20.3 us
    ppermute x12, starting transfers between devices, along(): lax.ppermute(x, 'sp', [(i, (i + offset) % parts) for i in range(parts)])  19.5 us
    pallas_call x2, Pallas kernels, partial_states(): pl.pallas_call(functools.partial(state_kernel, parts), grid_spec=pltpu.Pr...  9.11 us
    dot_general x12, matrix products, layer(): jnp.dot(mixed[-way * (k + 1) % n], weight, preferred_element_type=F32)  8.74 us
    pallas_call x4, Pallas kernels, read_states(): pl.pallas_call(functools.partial(read_kernel, parts, scale), grid_spec=pl...  3.78 us
  transfers between devices with their start and end apart: 30, of which 18 were waited for; matrix products, arithmetic and copies ran while one was open for 7% of the time, Pallas kernels for 6%

commit v1 on v0

--- a/solution.py
+++ b/solution.py
@@ -31,6 +31,10 @@
     return jnp.where(wide > 0.0, wide + 1.0, jnp.exp(jnp.minimum(wide, 0.0))).astype(BF16)
 
 
+def weight_bytes(weight):
+    return weight.size * weight.dtype.itemsize
+
+
 def cost(flops, nbytes):
     return pl.CostEstimate(flops=flops, bytes_accessed=nbytes, transcendentals=0)
 
@@ -42,7 +46,7 @@
 
 
 def state_kernel(parts, table, here, place, key, value, *refs):
-    outs, (keys, values, states) = refs[:parts], refs[parts:]
+    outs, (keys, values, states) = refs[:-3], refs[-3:]
     tokens, heads, size = key.shape[1:]
     rows = heads * size // parts
     feature = feature_map(key[0]).astype(F32)
@@ -58,13 +62,20 @@
         )
     for j in range(parts):
         start = pl.multiple_of(lax.rem(place[0] + j, parts) * rows, rows)
-        outs[j][0, :rows, :] = states[pl.ds(start, rows), :].astype(BF16)
-        outs[j][0, rows:, :] = mass
-
-
-def partial_states(key, value, table, here, place, blocks, heads, parts):
+        out = outs[j].at[0] if len(outs) == parts else outs[0].at[0, j]
+        out[:rows, :] = states[pl.ds(start, rows), :].astype(BF16)
+        out[rows:, :] = mass
+
+
+def partial_states(key, value, table, here, place, blocks, heads, parts, grant, joined):
     _, tokens, _, size = key.shape
     rows = heads * size // parts + 2 * heads
+    if joined:
+        outs = [jax.ShapeDtypeStruct((blocks, parts, rows, size), BF16)]
+        out_specs = [pl.BlockSpec((1, parts, rows, size), lambda i, t, d, p: (i, 0, 0, 0))]
+    else:
+        outs = [jax.ShapeDtypeStruct((blocks, rows, size), BF16)] * parts
+        out_specs = [pl.BlockSpec((1, rows, size), lambda i, t, d, p: (i, 0, 0))] * parts
     block = pl.BlockSpec((1, tokens, heads, size), lambda i, t, d, p: (0, 0, t[d[0] * blocks + i], 0))
     return pl.pallas_call(
         functools.partial(state_kernel, parts),
@@ -72,16 +83,16 @@
             num_scalar_prefetch=3,
             grid=(blocks,),
             in_specs=[block, block],
-            out_specs=[pl.BlockSpec((1, rows, size), lambda i, t, d, p: (i, 0, 0))] * parts,
+            out_specs=out_specs,
             scratch_shapes=[
                 pltpu.VMEM((tokens * heads, size), F32),
                 pltpu.VMEM((tokens * heads, size), F32),
                 pltpu.VMEM((heads * size, size), F32),
             ],
         ),
-        out_shape=[jax.ShapeDtypeStruct((blocks, rows, size), BF16)] * parts,
+        out_shape=outs,
         cost_estimate=cost(blocks * heads * tokens * size * size * 2, blocks * heads * tokens * size * 4),
-        compiler_params=pltpu.CompilerParams(vmem_limit_bytes=56 * MIB),
+        compiler_params=pltpu.CompilerParams(vmem_limit_bytes=grant * MIB),
         name="partial_states",
     )(table, here, place, key, value)
 
@@ -162,7 +173,25 @@
     )(block, place, query, own, *pieces)
 
 
-def partial_states_plain(key, value, table, here, place, blocks, heads, parts):
+def hold_kernel(weight, out, sem):
+    copy = pltpu.make_async_copy(weight, out, sem)
+    copy.start()
+    copy.wait()
+
+
+def hold(weight):
+    return pl.pallas_call(
+        hold_kernel,
+        in_specs=[pl.BlockSpec(memory_space=pl.ANY)],
+        out_specs=pl.BlockSpec(memory_space=pltpu.VMEM),
+        scratch_shapes=[pltpu.SemaphoreType.DMA],
+        out_shape=jax.ShapeDtypeStruct(weight.shape, weight.dtype),
+        compiler_params=pltpu.CompilerParams(vmem_limit_bytes=weight_bytes(weight) + MIB),
+        name="hold",
+    )(weight)
+
+
+def partial_states_plain(key, value, table, here, place, blocks, heads, parts, grant, joined):
     _, _, _, size = key.shape
     outs = [[] for _ in range(parts)]
     for b in range(blocks):
@@ -176,7 +205,8 @@
         for j in range(parts):
             piece = lax.dynamic_slice_in_dim(state, lax.rem(place[0] + j, parts) * rows, rows, 0)
             outs[j].append(jnp.concatenate([piece, mass]))
-    return [jnp.stack(out) for out in outs]
+    outs = [jnp.stack(out) for out in outs]
+    return [jnp.stack(outs, axis=1)] if joined else outs
 
 
 def total_states_plain(takes, heads, count):
@@ -236,21 +266,28 @@
     def along(x, offset):
         return lax.ppermute(x, "sp", [(i, (i + offset) % parts) for i in range(parts)])
 
-    groups = [sorted({1, n - 1}), list(range(2, n - 1)) + [0]] if n > 1 else [[0]]
+    groups = [g for g in (sorted({1, n - 1} - {n, 0}), list(range(2, n - 1)), [0]) if g]
 
     takes, queries, mixed = [], {}, {}
-    for group in groups:
+    step = width // (2 * CHUNKS)
+    for g, group in enumerate(groups):
         table = jnp.array([to[d][o] for d in range(n) for o in group], jnp.int32)
-        sent = make_partial(key_rows, value_rows, table, here, place, len(group), heads, parts)
+        size_of = (len(group), heads, parts, 16 if g else 56)
+        far = g > 0 and group[0] > 0
+        sent = make_partial(key_rows, value_rows, table, here, place, *size_of, far)
+        if far:
+            moved = [around(sent[0][i], o) for i, o in enumerate(group)]
+            sent = [jnp.stack([x[j] for x in moved]) for j in range(parts)]
         takes.append([sent[0]] + [along(sent[j], j) for j in range(1, parts)])
         for o in group:
             if o:
                 piece = lax.dynamic_slice_in_dim(query_rows, block_of(o) * heads, heads, 2)
                 queries[-o % n] = around(piece, o)
-    for group, take in zip(groups, takes):
-        totals = make_total(take, heads, count)
-        owns = [around(totals[i], o) if o else totals[i] for i, o in enumerate(group)]
-        stack = jnp.stack(owns)
+    for g, (group, take) in enumerate(zip(groups, takes)):
+        owns = list(make_total(take, heads, count))
+        if g == 0:
+            owns = [around(own, o) if o else own for own, o in zip(owns, group)]
+        stack = jnp.stack(owns) if len(owns) > 1 else owns[0][None]
         pieces = [stack] + [along(stack, j) for j in range(1, parts)]
         for i, o in enumerate(group):
             slot = -o % n
@@ -259,8 +296,10 @@
                 query, owns[i], pieces, i, block, heads, place, count**0.5
             )
 
+    if fits and weight_bytes(out_weight) <= 16 * MIB:
+        out_weight = hold(out_weight)
+
     lanes = []
-    step = width // (2 * CHUNKS)
     for c in range(2 * CHUNKS):
         way = 1 if c % 2 == 0 else -1
         lanes.append((way, out_weight[:, c * step : (c + 1) * step]))
@@ -270,10 +309,13 @@
         accs.append(acc)
     for k in range(1, n):
         for lane, (way, weight) in enumerate(lanes):
-            taken = around(accs[lane], way).astype(F32)
-            product = jnp.dot(mixed[-way * (k + 1) % n], weight, preferred_element_type=F32)
-            accs[lane] = (product + taken).astype(BF16)
-    return jnp.concatenate(accs, axis=1)[None]
+            accs[lane] = around(accs[lane], way).astype(F32)
+            if k < n - 1:
+                product = jnp.dot(mixed[-way * (k + 1) % n], weight, preferred_element_type=F32)
+                accs[lane] = (product + accs[lane]).astype(BF16)
+    product = jnp.dot(mixed[0], out_weight, preferred_element_type=F32)
+    product = lax.optimization_barrier(product)
+    return (product + jnp.concatenate(accs, axis=1)).astype(BF16)[None]
 
 
 def solution(mesh):

time: 154 us -> 141 us (0.916)
  waiting for transfers between devices: 86 us -> 61.8 us
  local copies, waits for them, and re-layouts: 0.3 us -> 8.42 us
  starting transfers between devices: 39.8 us -> 44.4 us
    ppermute x12 -> x18, waiting for transfers between devices: 29.8 us -> 15.5 us  [along(): lax.ppermute(x, 'sp', [(i, (i + offset) % parts) for i in range(parts)])]
    ppermute x18, waiting for transfers between devices: 56.1 us -> 46.3 us  [around(): return lax.ppermute(x, 'dp', [(d, to[d][offset % n]) for d in range(n)])]
    unnamed x12 -> x14, local copies, waits for them, and re-layouts: 0.02 us -> 8.13 us
    ppermute x12 -> x18, starting transfers between devices: 19.5 us -> 23.5 us  [along(): lax.ppermute(x, 'sp', [(i, (i + offset) % parts) for i in range(parts)])]
    dot_general x12 -> x8, matrix products: 8.74 us -> 5.84 us  [layer(): jnp.dot(mixed[-way * (k + 1) % n], weight, preferred_element_type=F32)]
    dot_general x0 -> x1, matrix products: none -> 2.38 us  [layer(): product = jnp.dot(mixed[0], out_weight, preferred_element_type=F32)]
    pallas_call x2 -> x3, Pallas kernels: 9.11 us -> 7.84 us  [partial_states(): pl.pallas_call(functools.partial(state_kernel, parts), grid_spec=pltpu.Pr...]
  transfers between devices with their start and end apart: 30 -> 36, of which waited for: 18 -> 14; matrix products, arithmetic and copies ran while one was open for 7% -> 8% of each run, Pallas kernels for 6% -> 8%
where the time goes in v1:
time: 141 us; the launch traced here: 140 us
  waiting for transfers between devices  61.8 us (44%)
  starting transfers between devices  44.4 us (31%)
  Pallas kernels  12.4 us (9%)
  matrix products  11.1 us (8%)
  local copies, waits for them, and re-layouts  8.42 us (6%)
  other arithmetic  1.91 us (1%)
    ppermute x18, waiting for transfers between devices, around(): return lax.ppermute(x, 'dp', [(d, to[d][offset % n]) for d in range(n)])  46.3 us
    ppermute x18, starting transfers between devices, along(): lax.ppermute(x, 'sp', [(i, (i + offset) % parts) for i in range(parts)])  23.5 us
    ppermute x18, starting transfers between devices, around(): return lax.ppermute(x, 'dp', [(d, to[d][offset % n]) for d in range(n)])  20.9 us
    ppermute x18, waiting for transfers between devices, along(): lax.ppermute(x, 'sp', [(i, (i + offset) % parts) for i in range(parts)])  15.5 us
    unnamed x14, local copies, waits for them, and re-layouts  8.13 us
    pallas_call x3, Pallas kernels, partial_states(): pl.pallas_call(functools.partial(state_kernel, parts), grid_spec=pltpu.Pr...  7.84 us
    dot_general x8, matrix products, layer(): jnp.dot(mixed[-way * (k + 1) % n], weight, preferred_element_type=F32)  5.84 us
    pallas_call x4, Pallas kernels, read_states(): pl.pallas_call(functools.partial(read_kernel, parts, scale), grid_spec=pl...  3.78 us
  transfers between devices with their start and end apart: 36, of which 14 were waited for; matrix products, arithmetic and copies ran while one was open for 8% of the time, Pallas kernels for 8%

profile of v1, /device:TPU:0, one launch (start us, length us, event | category | flops | bytes accessed | tf_op | source)
XLA Modules:
  0.0 140.3 jit_solution(11351836894386008327)
XLA Ops:
  0.0 1.6 %copy-done = bf16[1,256,32,128]{3,2,1,0:T(8,128)(2,1)S(1)} copy-done((bf16[1,256,32,128]{3,2,1,0:T(8,128)(2,1)S(1)}, bf16[1,256,32,128]{3,2,1,0:T(8,128)(2,1)}, u32[]{:S(2)}) %copy-start) | copy-done | bytes 2097176
  1.6 1.6 %copy-done.2 = bf16[1,256,32,128]{3,2,1,0:T(8,128)(2,1)S(1)} copy-done((bf16[1,256,32,128]{3,2,1,0:T(8,128)(2,1)S(1)}, bf16[1,256,32,128]{3,2,1,0:T(8,128)(2,1)}, u32[]{:S(2)}) %copy-start.2) | copy-done | bytes 2097176
  3.8 1.6 %partial_states.5 = bf16[1,4,272,128]{3,2,1,0:T(8,128)(2,1)S(1)} custom-call(s32[4]{0:T(128)S(1)} %copy-done.6, s32[1]{0:T(128)} %bitcast.here.block, s32[1]{0:T(128)} %bitcast.1.place, bf16[1,256,32,128]{3,2,1,0:T(8,128)(2,1)S(1)} %copy-done, bf16[1,256,32,128]{3,2,1,0:T(8,128)(2,1)S(1)} %copy-done.2), custom_call_target="tpu_custom_call" | custom-call | flops 67108864 | bytes 1048576 | tf_op jit(solution)/shard_map/partial_states/pallas_call | solution.py:80
  5.5 4.0 %collective-permute-start.16 = (bf16[4,272,128]{2,1,0:T(8,128)(2,1)S(1)}, bf16[4,272,128]{2,1,0:T(8,128)(2,1)S(1)}, u32[]{:S(2)}, u32[]{:S(2)}) collective-permute-start(bf16[4,272,128]{2,1,0:T(8,128)(2,1)S(1)} %bitcast.33), channel_id=1, source_target_pairs={{0,24},{8,16},{16,8},{24,0},{1,25},{9,17},{17,9},{25,1},{2,26},{10... | collective-permute-start | bytes 835592 | tf_op jit(solution)/shard_map/ppermute | solution.py:264
  9.5 1.6 %partial_states.3 = (bf16[1,272,128]{2,1,0:T(8,128)(2,1)S(1)}, bf16[1,272,128]{2,1,0:T(8,128)(2,1)S(1)}, bf16[1,272,128]{2,1,0:T(8,128)(2,1)S(1)}, bf16[1,272,128]{2,1,0:T(8,128)(2,1)S(1)}) custom-call(s32[4]{0:T(128)S(1)} %call_exported.0.table, s32[1]{0:T(128)} %bitcast.here.block, s32[1]{0:T(128)} %bitcast.1.place, ...), custom_call_target="tpu_custom_call" | custom-call | flops 67108864 | bytes 1048576 | tf_op jit(solution)/shard_map/partial_states/pallas_call | solution.py:80
  11.1 1.6 %collective-permute-start = (bf16[1,272,128]{2,1,0:T(8,128)(2,1)S(1)}, bf16[1,272,128]{2,1,0:T(8,128)(2,1)S(1)}, u32[]{:S(2)}, u32[]{:S(2)}) collective-permute-start(bf16[1,272,128]{2,1,0:T(8,128)(2,1)S(1)} %get-tuple-element.16), channel_id=1, source_target_pairs={{0,2},{2,4},{4,6},{6,0},{1,3},{3,5},{5,7},{7,1},{8,10},{10,12},{12... | collective-permute-start | bytes 208904 | tf_op jit(solution)/shard_map/ppermute | solution.py:267
  12.8 2.6 %collective-permute-start.1 = (bf16[1,272,128]{2,1,0:T(8,128)(2,1)S(1)}, bf16[1,272,128]{2,1,0:T(8,128)(2,1)S(1)}, u32[]{:S(2)}, u32[]{:S(2)}) collective-permute-start(bf16[1,272,128]{2,1,0:T(8,128)(2,1)S(1)} %get-tuple-element.17), channel_id=1, source_target_pairs={{0,4},{2,6},{4,0},{6,2},{1,5},{3,7},{5,1},{7,3},{8,12},{10,14},{12... | collective-permute-start | bytes 208904 | tf_op jit(solution)/shard_map/ppermute | solution.py:267
  15.4 1.3 collective-permute-start.2
  16.7 4.5 %partial_states.4 = (bf16[2,272,128]{2,1,0:T(8,128)(2,1)}, bf16[2,272,128]{2,1,0:T(8,128)(2,1)}, bf16[2,272,128]{2,1,0:T(8,128)(2,1)}, bf16[2,272,128]{2,1,0:T(8,128)(2,1)}) custom-call(s32[8]{0:T(128)} %constant.29.clone.table, s32[1]{0:T(128)} %bitcast.here.block, s32[1]{0:T(128)} %bitcast.1.place, bf16[1,256,32,128]{3,2,1,0:T(8,128)(2,1)} %key.5, ...), custom_call_target="tpu_custom_call" | custom-call | flops 134217728 | bytes 2097152 | tf_op jit(solution)/shard_map/partial_states/pallas_call | solution.py:80
  22.3 2.9 %collective-permute-start.9 = (bf16[2,272,128]{2,1,0:T(8,128)(2,1)}, bf16[2,272,128]{2,1,0:T(8,128)(2,1)S(1)}, u32[]{:S(2)}, u32[]{:S(2)}) collective-permute-start(bf16[2,272,128]{2,1,0:T(8,128)(2,1)} %get-tuple-element.22), channel_id=1, source_target_pairs={{0,6},{2,0},{4,2},{6,4},{1,7},{3,1},{5,3},{7,5},{8,14},{10,8},{12,... | collective-permute-start | bytes 417800 | tf_op jit(solution)/shard_map/ppermute | solution.py:267
  25.2 1.2 collective-permute-start.5
  26.7 3.2 %collective-permute-done.7.refs_1_ = bf16[2,272,128]{2,1,0:T(8,128)(2,1)S(1)} collective-permute-done((bf16[2,272,128]{2,1,0:T(8,128)(2,1)}, bf16[2,272,128]{2,1,0:T(8,128)(2,1)S(1)}, u32[]{:S(2)}, u32[]{:S(2)}) %collective-permute-start.7) | collective-permute-done | bytes 139296 | tf_op jit(solution)/shard_map/ppermute | solution.py:267
  30.4 3.3 %collective-permute-done.8.refs_2_ = bf16[2,272,128]{2,1,0:T(8,128)(2,1)S(1)} collective-permute-done((bf16[2,272,128]{2,1,0:T(8,128)(2,1)}, bf16[2,272,128]{2,1,0:T(8,128)(2,1)S(1)}, u32[]{:S(2)}, u32[]{:S(2)}) %collective-permute-start.8) | collective-permute-done | bytes 139296 | tf_op jit(solution)/shard_map/ppermute | solution.py:267
  33.7 2.1 %collective-permute-start.4 = (bf16[1,272,128]{2,1,0:T(8,128)(2,1)S(1)}, bf16[1,272,128]{2,1,0:T(8,128)(2,1)S(1)}, u32[]{:S(2)}, u32[]{:S(2)}) collective-permute-start(bf16[1,272,128]{2,1,0:T(8,128)(2,1)S(1)} %bitcast.24), channel_id=1, source_target_pairs={{0,4},{2,6},{4,0},{6,2},{1,5},{3,7},{5,1},{7,3},{8,12},{10,14},{12... | collective-permute-start | bytes 208904 | tf_op jit(solution)/shard_map/ppermute | solution.py:267
  35.8 3.7 %collective-permute-start.3 = (bf16[1,272,128]{2,1,0:T(8,128)(2,1)S(1)}, bf16[1,272,128]{2,1,0:T(8,128)(2,1)S(1)}, u32[]{:S(2)}, u32[]{:S(2)}) collective-permute-start(bf16[1,272,128]{2,1,0:T(8,128)(2,1)S(1)} %bitcast.25), channel_id=1, source_target_pairs={{0,2},{2,4},{4,6},{6,0},{1,3},{3,5},{5,7},{7,1},{8,10},{10,12},{12... | collective-permute-start | bytes 208904 | tf_op jit(solution)/shard_map/ppermute | solution.py:267
  41.1 1.5 %collective-permute-start.11 = (bf16[272,128]{1,0:T(8,128)(2,1)S(1)}, bf16[272,128]{1,0:T(8,128)(2,1)S(1)}, u32[]{:S(2)}, u32[]{:S(2)}) collective-permute-start(bf16[272,128]{1,0:T(8,128)(2,1)S(1)} %get-tuple-element.24), channel_id=1, source_target_pairs={{0,8},{8,24},{16,0},{24,16},{1,9},{9,25},{17,1},{25,17},{2,10},{10... | collective-permute-start | bytes 208904 | tf_op jit(solution)/shard_map/ppermute | solution.py:264
  43.2 1.9 %collective-permute-start.19 = (bf16[1,272,128]{2,1,0:T(8,128)(2,1)S(1)}, bf16[1,272,128]{2,1,0:T(8,128)(2,1)S(1)}, u32[]{:S(2)}, u32[]{:S(2)}) collective-permute-start(bf16[1,272,128]{2,1,0:T(8,128)(2,1)S(1)} %get-tuple-element.28), channel_id=1, source_target_pairs={{0,6},{2,0},{4,2},{6,4},{1,7},{3,1},{5,3},{7,5},{8,14},{10,8},{12,... | collective-permute-start | bytes 208904 | tf_op jit(solution)/shard_map/ppermute | solution.py:267
  46.1 3.3 %collective-permute-done.19.refs_3_ = bf16[1,272,128]{2,1,0:T(8,128)(2,1)S(1)} collective-permute-done((bf16[1,272,128]{2,1,0:T(8,128)(2,1)S(1)}, bf16[1,272,128]{2,1,0:T(8,128)(2,1)S(1)}, u32[]{:S(2)}, u32[]{:S(2)}) %collective-permute-start.19) | collective-permute-done | bytes 69664 | tf_op jit(solution)/shard_map/ppermute | solution.py:267
  49.4 2.0 %collective-permute-start.14 = (bf16[2,272,128]{2,1,0:T(8,128)(2,1)S(1)}, bf16[2,272,128]{2,1,0:T(8,128)(2,1)S(1)}, u32[]{:S(2)}, u32[]{:S(2)}) collective-permute-start(bf16[2,272,128]{2,1,0:T(8,128)(2,1)S(1)} %pad_maximum_fusion.refs_0_), channel_id=1, source_target_pairs={{0,6},{2,0},{4,2},{6,4},{1,7},{3,1},{5,3},{7,5},{8,14},{10,8},{12,... | collective-permute-start | bytes 417800 | tf_op jit(solution)/shard_map/ppermute | solution.py:267
  51.4 2.7 %collective-permute-done.18.refs_2_ = bf16[1,272,128]{2,1,0:T(8,128)(2,1)S(1)} collective-permute-done((bf16[1,272,128]{2,1,0:T(8,128)(2,1)S(1)}, bf16[1,272,128]{2,1,0:T(8,128)(2,1)S(1)}, u32[]{:S(2)}, u32[]{:S(2)}) %collective-permute-start.18) | collective-permute-done | bytes 69664 | tf_op jit(solution)/shard_map/ppermute | solution.py:267
  54.6 3.4 %copy-done.3 = bf16[1024,4096]{1,0:T(8,128)(2,1)S(1)} copy-done((bf16[1024,4096]{1,0:T(8,128)(2,1)S(1)}, bf16[1024,4096]{1,0:T(8,128)(2,1)}, u32[]{:S(2)}) %copy-start.3) | copy-done | bytes 8388632
  60.6 3.1 %collective-permute-done.13.refs_2_ = bf16[2,272,128]{2,1,0:T(8,128)(2,1)S(1)} collective-permute-done((bf16[2,272,128]{2,1,0:T(8,128)(2,1)S(1)}, bf16[2,272,128]{2,1,0:T(8,128)(2,1)S(1)}, u32[]{:S(2)}, u32[]{:S(2)}) %collective-permute-start.13) | collective-permute-done | bytes 139296 | tf_op jit(solution)/shard_map/ppermute | solution.py:267
  75.8 8.2 %collective-permute-done.33 = bf16[256,1024]{1,0:T(8,128)(2,1)S(1)} collective-permute-done((bf16[256,1024]{1,0:T(8,128)(2,1)S(1)}, bf16[256,1024]{1,0:T(8,128)(2,1)S(1)}, u32[]{:S(2)}, u32[]{:S(2)}) %collective-permute-start.33) | collective-permute-done | bytes 524320 | tf_op jit(solution)/shard_map/ppermute | solution.py:264
  87.6 7.6 %collective-permute-done.27 = bf16[256,1024]{1,0:T(8,128)(2,1)S(1)} collective-permute-done((bf16[256,1024]{1,0:T(8,128)(2,1)S(1)}, bf16[256,1024]{1,0:T(8,128)(2,1)S(1)}, u32[]{:S(2)}, u32[]{:S(2)}) %collective-permute-start.27) | collective-permute-done | bytes 524320 | tf_op jit(solution)/shard_map/ppermute | solution.py:264
  98.8 7.6 %collective-permute-done.34 = bf16[256,1024]{1,0:T(8,128)(2,1)S(1)} collective-permute-done((bf16[256,1024]{1,0:T(8,128)(2,1)S(1)}, bf16[256,1024]{1,0:T(8,128)(2,1)S(1)}, u32[]{:S(2)}, u32[]{:S(2)}) %collective-permute-start.34) | collective-permute-done | bytes 524320 | tf_op jit(solution)/shard_map/ppermute | solution.py:264
  110.1 7.6 %collective-permute-done.28 = bf16[256,1024]{1,0:T(8,128)(2,1)S(1)} collective-permute-done((bf16[256,1024]{1,0:T(8,128)(2,1)S(1)}, bf16[256,1024]{1,0:T(8,128)(2,1)S(1)}, u32[]{:S(2)}, u32[]{:S(2)}) %collective-permute-start.28) | collective-permute-done | bytes 524320 | tf_op jit(solution)/shard_map/ppermute | solution.py:264
  121.3 2.4 %fusion.86 = f32[256,4096]{1,0:T(8,128)S(1)} fusion(bf16[256,1024]{1,0:T(8,128)(2,1)S(1)} %read_states.4, bf16[1024,4096]{1,0:T(8,128)(2,1)S(1)} %hold.1), kind=kOutput, calls=%fused_computation.51 | convolution fusion | flops 2147483648 | bytes 13107200 | tf_op jit(solution)/shard_map/dot_general | solution.py:316
  123.7 5.2 %collective-permute-done.35 = bf16[256,1024]{1,0:T(8,128)(2,1)S(1)} collective-permute-done((bf16[256,1024]{1,0:T(8,128)(2,1)S(1)}, bf16[256,1024]{1,0:T(8,128)(2,1)S(1)}, u32[]{:S(2)}, u32[]{:S(2)}) %collective-permute-start.35) | collective-permute-done | bytes 524320 | tf_op jit(solution)/shard_map/ppermute | solution.py:264
  128.9 1.9 %collective-permute-done.32 = bf16[256,1024]{1,0:T(8,128)(2,1)S(1)} collective-permute-done((bf16[256,1024]{1,0:T(8,128)(2,1)S(1)}, bf16[256,1024]{1,0:T(8,128)(2,1)S(1)}, u32[]{:S(2)}, u32[]{:S(2)}) %collective-permute-start.32) | collective-permute-done | bytes 524320 | tf_op jit(solution)/shard_map/ppermute | solution.py:264
  130.8 6.3 %collective-permute-done.29 = bf16[256,1024]{1,0:T(8,128)(2,1)S(1)} collective-permute-done((bf16[256,1024]{1,0:T(8,128)(2,1)S(1)}, bf16[256,1024]{1,0:T(8,128)(2,1)S(1)}, u32[]{:S(2)}, u32[]{:S(2)}) %collective-permute-start.29) | collective-permute-done | bytes 524320 | tf_op jit(solution)/shard_map/ppermute | solution.py:264
  137.1 1.3 collective-permute-done.26
  138.4 1.9 %fusion = bf16[1,256,4096]{2,1,0:T(8,128)(2,1)} fusion(f32[256,4096]{1,0:T(8,128)S(1)} %fusion.86, bf16[256,1024]{1,0:T(8,128)(2,1)S(1)} %collective-permute-done.35, bf16[256,1024]{1,0:T(8,128)(2,1)S(1)} %collective-permute-done.32, bf16[256,1024]{1,0:T(8,128)(2,1)S(1)} %collective-permute-done.29, bf16[256,1024]{1,0:T(8,128)(2,1)S(1)} %collective-permute-done.26), kind=kLoop, calls=%fused_computation.1 | loop fusion | flops 10485760 | bytes 8388608 | tf_op jit(solution)/shard_map/broadcast_in_dim | solution.py:318
  (83 shorter events, 35.2 us)
Async XLA Ops:
  5.5 35.6 %collective-permute-start.16 = (bf16[4,272,128]{2,1,0:T(8,128)(2,1)S(1)}, bf16[4,272,128]{2,1,0:T(8,128)(2,1)S(1)}, u32[]{:S(2)}, u32[]{:S(2)}) collective-permute-start(bf16[4,272,128]{2,1,0:T(8,128)(2,1)S(1)} %bitcast.33), channel_id=1, source_target_pairs={{0,24},{8,16},{16,8},{24,0},{1,25},{9,17},{17,9},{25,1},{2,26},{10... | collective-permute-start | bytes 835592 | tf_op jit(solution)/shard_map/ppermute | solution.py:264
  11.1 10.8 %collective-permute-start = (bf16[1,272,128]{2,1,0:T(8,128)(2,1)S(1)}, bf16[1,272,128]{2,1,0:T(8,128)(2,1)S(1)}, u32[]{:S(2)}, u32[]{:S(2)}) collective-permute-start(bf16[1,272,128]{2,1,0:T(8,128)(2,1)S(1)} %get-tuple-element.16), channel_id=1, source_target_pairs={{0,2},{2,4},{4,6},{6,0},{1,3},{3,5},{5,7},{7,1},{8,10},{10,12},{12... | collective-permute-start | bytes 208904 | tf_op jit(solution)/shard_map/ppermute | solution.py:267
  12.8 9.5 %collective-permute-start.1 = (bf16[1,272,128]{2,1,0:T(8,128)(2,1)S(1)}, bf16[1,272,128]{2,1,0:T(8,128)(2,1)S(1)}, u32[]{:S(2)}, u32[]{:S(2)}) collective-permute-start(bf16[1,272,128]{2,1,0:T(8,128)(2,1)S(1)} %get-tuple-element.17), channel_id=1, source_target_pairs={{0,4},{2,6},{4,0},{6,2},{1,5},{3,7},{5,1},{7,3},{8,12},{10,14},{12... | collective-permute-start | bytes 208904 | tf_op jit(solution)/shard_map/ppermute | solution.py:267
  15.4 9.8 %collective-permute-start.2 = (bf16[1,272,128]{2,1,0:T(8,128)(2,1)S(1)}, bf16[1,272,128]{2,1,0:T(8,128)(2,1)S(1)}, u32[]{:S(2)}, u32[]{:S(2)}) collective-permute-start(bf16[1,272,128]{2,1,0:T(8,128)(2,1)S(1)} %get-tuple-element.18), channel_id=1, source_target_pairs={{0,6},{2,0},{4,2},{6,4},{1,7},{3,1},{5,3},{7,5},{8,14},{10,8},{12,... | collective-permute-start | bytes 208904 | tf_op jit(solution)/shard_map/ppermute | solution.py:267
  21.3 8.6 %collective-permute-start.7 = (bf16[2,272,128]{2,1,0:T(8,128)(2,1)}, bf16[2,272,128]{2,1,0:T(8,128)(2,1)S(1)}, u32[]{:S(2)}, u32[]{:S(2)}) collective-permute-start(bf16[2,272,128]{2,1,0:T(8,128)(2,1)} %get-tuple-element.20), channel_id=1, source_target_pairs={{0,2},{2,4},{4,6},{6,0},{1,3},{3,5},{5,7},{7,1},{8,10},{10,12},{12... | collective-permute-start | bytes 417800 | tf_op jit(solution)/shard_map/ppermute | solution.py:267
  22.0 11.7 %collective-permute-start.8 = (bf16[2,272,128]{2,1,0:T(8,128)(2,1)}, bf16[2,272,128]{2,1,0:T(8,128)(2,1)S(1)}, u32[]{:S(2)}, u32[]{:S(2)}) collective-permute-start(bf16[2,272,128]{2,1,0:T(8,128)(2,1)} %get-tuple-element.21), channel_id=1, source_target_pairs={{0,4},{2,6},{4,0},{6,2},{1,5},{3,7},{5,1},{7,3},{8,12},{10,14},{12... | collective-permute-start | bytes 417800 | tf_op jit(solution)/shard_map/ppermute | solution.py:267
  22.3 13.5 %collective-permute-start.9 = (bf16[2,272,128]{2,1,0:T(8,128)(2,1)}, bf16[2,272,128]{2,1,0:T(8,128)(2,1)S(1)}, u32[]{:S(2)}, u32[]{:S(2)}) collective-permute-start(bf16[2,272,128]{2,1,0:T(8,128)(2,1)} %get-tuple-element.22), channel_id=1, source_target_pairs={{0,6},{2,0},{4,2},{6,4},{1,7},{3,1},{5,3},{7,5},{8,14},{10,8},{12,... | collective-permute-start | bytes 417800 | tf_op jit(solution)/shard_map/ppermute | solution.py:267
  25.2 15.3 %collective-permute-start.5 = (bf16[1,272,128]{2,1,0:T(8,128)(2,1)S(1)}, bf16[1,272,128]{2,1,0:T(8,128)(2,1)S(1)}, u32[]{:S(2)}, u32[]{:S(2)}) collective-permute-start(bf16[1,272,128]{2,1,0:T(8,128)(2,1)S(1)} %bitcast.23), channel_id=1, source_target_pairs={{0,6},{2,0},{4,2},{6,4},{1,7},{3,1},{5,3},{7,5},{8,14},{10,8},{12,... | collective-permute-start | bytes 208904 | tf_op jit(solution)/shard_map/ppermute | solution.py:267
  29.9 35.7 %collective-permute-start.23 = (bf16[1,256,8,128]{3,2,1,0:T(8,128)(2,1)S(1)}, bf16[1,256,8,128]{3,2,1,0:T(8,128)(2,1)S(1)}, u32[]{:S(2)}, u32[]{:S(2)}) collective-permute-start(bf16[1,256,8,128]{3,2,1,0:T(8,128)(2,1)S(1)} %get-tuple-element.26), channel_id=1, source_target_pairs={{0,8},{8,24},{16,0},{24,16},{1,9},{9,25},{17,1},{25,17},{2,10},{10... | collective-permute-start | bytes 1572872 | tf_op jit(solution)/shard_map/ppermute | solution.py:264
  33.7 9.0 %collective-permute-start.4 = (bf16[1,272,128]{2,1,0:T(8,128)(2,1)S(1)}, bf16[1,272,128]{2,1,0:T(8,128)(2,1)S(1)}, u32[]{:S(2)}, u32[]{:S(2)}) collective-permute-start(bf16[1,272,128]{2,1,0:T(8,128)(2,1)S(1)} %bitcast.24), channel_id=1, source_target_pairs={{0,4},{2,6},{4,0},{6,2},{1,5},{3,7},{5,1},{7,3},{8,12},{10,14},{12... | collective-permute-start | bytes 208904 | tf_op jit(solution)/shard_map/ppermute | solution.py:267
  35.8 7.4 %collective-permute-start.3 = (bf16[1,272,128]{2,1,0:T(8,128)(2,1)S(1)}, bf16[1,272,128]{2,1,0:T(8,128)(2,1)S(1)}, u32[]{:S(2)}, u32[]{:S(2)}) collective-permute-start(bf16[1,272,128]{2,1,0:T(8,128)(2,1)S(1)} %bitcast.25), channel_id=1, source_target_pairs={{0,2},{2,4},{4,6},{6,0},{1,3},{3,5},{5,7},{7,1},{8,10},{10,12},{12... | collective-permute-start | bytes 208904 | tf_op jit(solution)/shard_map/ppermute | solution.py:267
  42.7 24.8 %collective-permute-start.6 = (bf16[1,256,8,128]{3,2,1,0:T(8,128)(2,1)S(1)}, bf16[1,256,8,128]{3,2,1,0:T(8,128)(2,1)S(1)}, u32[]{:S(2)}, u32[]{:S(2)}) collective-permute-start(bf16[1,256,8,128]{3,2,1,0:T(8,128)(2,1)S(1)} %get-tuple-element.25), channel_id=1, source_target_pairs={{0,16},{8,0},{16,24},{24,8},{1,17},{9,1},{17,25},{25,9},{2,18},{10... | collective-permute-start | bytes 1572872 | tf_op jit(solution)/shard_map/ppermute | solution.py:264
  45.7 8.4 %collective-permute-start.18 = (bf16[1,272,128]{2,1,0:T(8,128)(2,1)S(1)}, bf16[1,272,128]{2,1,0:T(8,128)(2,1)S(1)}, u32[]{:S(2)}, u32[]{:S(2)}) collective-permute-start(bf16[1,272,128]{2,1,0:T(8,128)(2,1)S(1)} %get-tuple-element.29), channel_id=1, source_target_pairs={{0,4},{2,6},{4,0},{6,2},{1,5},{3,7},{5,1},{7,3},{8,12},{10,14},{12... | collective-permute-start | bytes 208904 | tf_op jit(solution)/shard_map/ppermute | solution.py:267
  45.7 8.4 %collective-permute-start.17 = (bf16[1,272,128]{2,1,0:T(8,128)(2,1)S(1)}, bf16[1,272,128]{2,1,0:T(8,128)(2,1)S(1)}, u32[]{:S(2)}, u32[]{:S(2)}) collective-permute-start(bf16[1,272,128]{2,1,0:T(8,128)(2,1)S(1)} %get-tuple-element.30), channel_id=1, source_target_pairs={{0,2},{2,4},{4,6},{6,0},{1,3},{3,5},{5,7},{7,1},{8,10},{10,12},{12... | collective-permute-start | bytes 208904 | tf_op jit(solution)/shard_map/ppermute | solution.py:267
  49.4 10.2 %collective-permute-start.14 = (bf16[2,272,128]{2,1,0:T(8,128)(2,1)S(1)}, bf16[2,272,128]{2,1,0:T(8,128)(2,1)S(1)}, u32[]{:S(2)}, u32[]{:S(2)}) collective-permute-start(bf16[2,272,128]{2,1,0:T(8,128)(2,1)S(1)} %pad_maximum_fusion.refs_0_), channel_id=1, source_target_pairs={{0,6},{2,0},{4,2},{6,4},{1,7},{3,1},{5,3},{7,5},{8,14},{10,8},{12,... | collective-permute-start | bytes 417800 | tf_op jit(solution)/shard_map/ppermute | solution.py:267
  54.0 9.7 %collective-permute-start.13 = (bf16[2,272,128]{2,1,0:T(8,128)(2,1)S(1)}, bf16[2,272,128]{2,1,0:T(8,128)(2,1)S(1)}, u32[]{:S(2)}, u32[]{:S(2)}) collective-permute-start(bf16[2,272,128]{2,1,0:T(8,128)(2,1)S(1)} %pad_maximum_fusion.refs_0_), channel_id=1, source_target_pairs={{0,4},{2,6},{4,0},{6,2},{1,5},{3,7},{5,1},{7,3},{8,12},{10,14},{12... | collective-permute-start | bytes 417800 | tf_op jit(solution)/shard_map/ppermute | solution.py:267
  54.0 10.4 %collective-permute-start.12 = (bf16[2,272,128]{2,1,0:T(8,128)(2,1)S(1)}, bf16[2,272,128]{2,1,0:T(8,128)(2,1)S(1)}, u32[]{:S(2)}, u32[]{:S(2)}) collective-permute-start(bf16[2,272,128]{2,1,0:T(8,128)(2,1)S(1)} %pad_maximum_fusion.refs_0_), channel_id=1, source_target_pairs={{0,2},{2,4},{4,6},{6,0},{1,3},{3,5},{5,7},{7,1},{8,10},{10,12},{12... | collective-permute-start | bytes 417800 | tf_op jit(solution)/shard_map/ppermute | solution.py:267
  59.6 15.2 %collective-permute-start.15 = (bf16[1,256,8,128]{3,2,1,0:T(8,128)(2,1)S(1)}, bf16[1,256,8,128]{3,2,1,0:T(8,128)(2,1)S(1)}, u32[]{:S(2)}, u32[]{:S(2)}) collective-permute-start(bf16[1,256,8,128]{3,2,1,0:T(8,128)(2,1)S(1)} %get-tuple-element.27), channel_id=1, source_target_pairs={{0,24},{8,16},{16,8},{24,0},{1,25},{9,17},{17,9},{25,1},{2,26},{10... | collective-permute-start | bytes 1572872 | tf_op jit(solution)/shard_map/ppermute | solution.py:264
  64.4 8.3 %collective-permute-start.21 = (bf16[1,272,128]{2,1,0:T(8,128)(2,1)S(1)}, bf16[1,272,128]{2,1,0:T(8,128)(2,1)S(1)}, u32[]{:S(2)}, u32[]{:S(2)}) collective-permute-start(bf16[1,272,128]{2,1,0:T(8,128)(2,1)S(1)} %bitcast.28), channel_id=1, source_target_pairs={{0,4},{2,6},{4,0},{6,2},{1,5},{3,7},{5,1},{7,3},{8,12},{10,14},{12... | collective-permute-start | bytes 208904 | tf_op jit(solution)/shard_map/ppermute | solution.py:267
  65.6 8.3 %collective-permute-start.20 = (bf16[1,272,128]{2,1,0:T(8,128)(2,1)S(1)}, bf16[1,272,128]{2,1,0:T(8,128)(2,1)S(1)}, u32[]{:S(2)}, u32[]{:S(2)}) collective-permute-start(bf16[1,272,128]{2,1,0:T(8,128)(2,1)S(1)} %bitcast.29), channel_id=1, source_target_pairs={{0,2},{2,4},{4,6},{6,0},{1,3},{3,5},{5,7},{7,1},{8,10},{10,12},{12... | collective-permute-start | bytes 208904 | tf_op jit(solution)/shard_map/ppermute | solution.py:267
  69.1 14.8 %collective-permute-start.33 = (bf16[256,1024]{1,0:T(8,128)(2,1)S(1)}, bf16[256,1024]{1,0:T(8,128)(2,1)S(1)}, u32[]{:S(2)}, u32[]{:S(2)}) collective-permute-start(bf16[256,1024]{1,0:T(8,128)(2,1)S(1)} %fusion.58), channel_id=1, source_target_pairs={{0,16},{8,0},{16,24},{24,8},{1,17},{9,1},{17,25},{25,9},{2,18},{10... | collective-permute-start | bytes 1572872 | tf_op jit(solution)/shard_map/ppermute | solution.py:264
  71.0 14.9 %collective-permute-start.30 = (bf16[256,1024]{1,0:T(8,128)(2,1)S(1)}, bf16[256,1024]{1,0:T(8,128)(2,1)S(1)}, u32[]{:S(2)}, u32[]{:S(2)}) collective-permute-start(bf16[256,1024]{1,0:T(8,128)(2,1)S(1)} %fusion.55), channel_id=1, source_target_pairs={{0,8},{8,24},{16,0},{24,16},{1,9},{9,25},{17,1},{25,17},{2,10},{10... | collective-permute-start | bytes 1572872 | tf_op jit(solution)/shard_map/ppermute | solution.py:264
  72.7 22.5 %collective-permute-start.27 = (bf16[256,1024]{1,0:T(8,128)(2,1)S(1)}, bf16[256,1024]{1,0:T(8,128)(2,1)S(1)}, u32[]{:S(2)}, u32[]{:S(2)}) collective-permute-start(bf16[256,1024]{1,0:T(8,128)(2,1)S(1)} %fusion.52), channel_id=1, source_target_pairs={{0,16},{8,0},{16,24},{24,8},{1,17},{9,1},{17,25},{25,9},{2,18},{10... | collective-permute-start | bytes 1572872 | tf_op jit(solution)/shard_map/ppermute | solution.py:264
  73.8 23.2 %collective-permute-start.24 = (bf16[256,1024]{1,0:T(8,128)(2,1)S(1)}, bf16[256,1024]{1,0:T(8,128)(2,1)S(1)}, u32[]{:S(2)}, u32[]{:S(2)}) collective-permute-start(bf16[256,1024]{1,0:T(8,128)(2,1)S(1)} %fusion.49), channel_id=1, source_target_pairs={{0,8},{8,24},{16,0},{24,16},{1,9},{9,25},{17,1},{25,17},{2,10},{10... | collective-permute-start | bytes 1572872 | tf_op jit(solution)/shard_map/ppermute | solution.py:264
  84.7 21.7 %collective-permute-start.34 = (bf16[256,1024]{1,0:T(8,128)(2,1)S(1)}, bf16[256,1024]{1,0:T(8,128)(2,1)S(1)}, u32[]{:S(2)}, u32[]{:S(2)}) collective-permute-start(bf16[256,1024]{1,0:T(8,128)(2,1)S(1)} %fusion.61), channel_id=1, source_target_pairs={{0,16},{8,0},{16,24},{24,8},{1,17},{9,1},{17,25},{25,9},{2,18},{10... | collective-permute-start | bytes 1572872 | tf_op jit(solution)/shard_map/ppermute | solution.py:264
  86.6 21.7 %collective-permute-start.31 = (bf16[256,1024]{1,0:T(8,128)(2,1)S(1)}, bf16[256,1024]{1,0:T(8,128)(2,1)S(1)}, u32[]{:S(2)}, u32[]{:S(2)}) collective-permute-start(bf16[256,1024]{1,0:T(8,128)(2,1)S(1)} %fusion.67), channel_id=1, source_target_pairs={{0,8},{8,24},{16,0},{24,16},{1,9},{9,25},{17,1},{25,17},{2,10},{10... | collective-permute-start | bytes 1572872 | tf_op jit(solution)/shard_map/ppermute | solution.py:264
  96.0 21.7 %collective-permute-start.28 = (bf16[256,1024]{1,0:T(8,128)(2,1)S(1)}, bf16[256,1024]{1,0:T(8,128)(2,1)S(1)}, u32[]{:S(2)}, u32[]{:S(2)}) collective-permute-start(bf16[256,1024]{1,0:T(8,128)(2,1)S(1)} %fusion.73), channel_id=1, source_target_pairs={{0,16},{8,0},{16,24},{24,8},{1,17},{9,1},{17,25},{25,9},{2,18},{10... | collective-permute-start | bytes 1572872 | tf_op jit(solution)/shard_map/ppermute | solution.py:264
  97.8 21.7 %collective-permute-start.25 = (bf16[256,1024]{1,0:T(8,128)(2,1)S(1)}, bf16[256,1024]{1,0:T(8,128)(2,1)S(1)}, u32[]{:S(2)}, u32[]{:S(2)}) collective-permute-start(bf16[256,1024]{1,0:T(8,128)(2,1)S(1)} %fusion.79), channel_id=1, source_target_pairs={{0,8},{8,24},{16,0},{24,16},{1,9},{9,25},{17,1},{25,17},{2,10},{10... | collective-permute-start | bytes 1572872 | tf_op jit(solution)/shard_map/ppermute | solution.py:264
  107.2 21.7 %collective-permute-start.35 = (bf16[256,1024]{1,0:T(8,128)(2,1)S(1)}, bf16[256,1024]{1,0:T(8,128)(2,1)S(1)}, u32[]{:S(2)}, u32[]{:S(2)}) collective-permute-start(bf16[256,1024]{1,0:T(8,128)(2,1)S(1)} %fusion.64), channel_id=1, source_target_pairs={{0,16},{8,0},{16,24},{24,8},{1,17},{9,1},{17,25},{25,9},{2,18},{10... | collective-permute-start | bytes 1572872 | tf_op jit(solution)/shard_map/ppermute | solution.py:264
  109.1 21.7 %collective-permute-start.32 = (bf16[256,1024]{1,0:T(8,128)(2,1)S(1)}, bf16[256,1024]{1,0:T(8,128)(2,1)S(1)}, u32[]{:S(2)}, u32[]{:S(2)}) collective-permute-start(bf16[256,1024]{1,0:T(8,128)(2,1)S(1)} %fusion.70), channel_id=1, source_target_pairs={{0,8},{8,24},{16,0},{24,16},{1,9},{9,25},{17,1},{25,17},{2,10},{10... | collective-permute-start | bytes 1572872 | tf_op jit(solution)/shard_map/ppermute | solution.py:264
  118.4 18.7 %collective-permute-start.29 = (bf16[256,1024]{1,0:T(8,128)(2,1)S(1)}, bf16[256,1024]{1,0:T(8,128)(2,1)S(1)}, u32[]{:S(2)}, u32[]{:S(2)}) collective-permute-start(bf16[256,1024]{1,0:T(8,128)(2,1)S(1)} %fusion.76), channel_id=1, source_target_pairs={{0,16},{8,0},{16,24},{24,8},{1,17},{9,1},{17,25},{25,9},{2,18},{10... | collective-permute-start | bytes 1572872 | tf_op jit(solution)/shard_map/ppermute | solution.py:264
  120.3 18.1 %collective-permute-start.26 = (bf16[256,1024]{1,0:T(8,128)(2,1)S(1)}, bf16[256,1024]{1,0:T(8,128)(2,1)S(1)}, u32[]{:S(2)}, u32[]{:S(2)}) collective-permute-start(bf16[256,1024]{1,0:T(8,128)(2,1)S(1)} %fusion.82), channel_id=1, source_target_pairs={{0,8},{8,24},{16,0},{24,16},{1,9},{9,25},{17,1},{25,17},{2,10},{10... | collective-permute-start | bytes 1572872 | tf_op jit(solution)/shard_map/ppermute | solution.py:264
  (11 other events, 53.8 us)

commit v2 on v1

--- a/solution.py
+++ b/solution.py
@@ -121,14 +121,19 @@
     )(*takes)
 
 
-def read_kernel(parts, scale, block, place, query, mass, *refs):
-    pieces, (out, queries, states) = refs[:parts], refs[parts:]
-    tokens, heads, size = query.shape[1:]
+def read_kernel(parts, scale, block, place, mass, *refs):
+    pieces, asked, (out, queries, states) = refs[:parts], refs[parts:-3], refs[-3:]
+    heads, size = asked[0].shape[2:]
+    tokens = out.shape[0]
     rows = heads * size // parts
     for j in range(parts):
         start = pl.multiple_of(lax.rem(place[0] + parts - j, parts) * rows, rows)
         states[pl.ds(start, rows), :] = pieces[j][0, :rows, :]
-    queries[...] = feature_map(query[0]).astype(F32).reshape(tokens * heads, size)
+    done = 0
+    for query in asked:
+        some = query.shape[1] * heads
+        queries[done : done + some, :] = feature_map(query[0]).astype(F32).reshape(some, size)
+        done += some
     masses = mass[...].astype(F32)
     masses = (masses[:heads] + masses[heads:]).T
     none = jnp.zeros((size, size), BF16)
@@ -146,20 +151,21 @@
         out[:, h * size : (h + 1) * size] = result.astype(BF16)
 
 
-def read_states(query, own, pieces, slot, block, heads, place, scale):
+def read_states(queries, own, pieces, slot, block, heads, place, scale):
     parts = len(pieces)
-    _, tokens, _, size = query.shape
+    tokens, size = sum(query.shape[1] for query in queries), own.shape[1]
     rows = own.shape[0]
     return pl.pallas_call(
         functools.partial(read_kernel, parts, scale),
         grid_spec=pltpu.PrefetchScalarGridSpec(
             num_scalar_prefetch=2,
             grid=(1,),
-            in_specs=[
-                pl.BlockSpec((1, tokens, heads, size), lambda i, b, p: (0, 0, b[0], 0)),
-                pl.BlockSpec((2 * heads, size), lambda i, b, p: (rows // (2 * heads) - 1, 0)),
-            ]
-            + [pl.BlockSpec((1, rows, size), lambda i, b, p: (slot, 0, 0))] * parts,
+            in_specs=[pl.BlockSpec((2 * heads, size), lambda i, b, p: (rows // (2 * heads) - 1, 0))]
+            + [pl.BlockSpec((1, rows, size), lambda i, b, p: (slot, 0, 0))] * parts
+            + [
+                pl.BlockSpec((1, query.shape[1], heads, size), lambda i, b, p: (0, 0, b[0], 0))
+                for query in queries
+            ],
             out_specs=pl.BlockSpec((tokens, heads * size), lambda i, b, p: (0, 0)),
             scratch_shapes=[
                 pltpu.VMEM((tokens * heads, size), F32),
@@ -170,7 +176,7 @@
         cost_estimate=cost(heads * tokens * size * size * 8, heads * tokens * size * 4),
         compiler_params=pltpu.CompilerParams(vmem_limit_bytes=12 * MIB),
         name="read_states",
-    )(block, place, query, own, *pieces)
+    )(block, place, own, *pieces, *queries)
 
 
 def hold_kernel(weight, out, sem):
@@ -219,10 +225,11 @@
     ]
 
 
-def read_states_plain(query, own, pieces, slot, block, heads, place, scale):
+def read_states_plain(queries, own, pieces, slot, block, heads, place, scale):
     parts = len(pieces)
-    _, tokens, _, size = query.shape
-    query = lax.dynamic_slice_in_dim(query[0], block[0] * heads, heads, 1)
+    query = jnp.concatenate(queries, axis=1)[0]
+    tokens, _, size = query.shape
+    query = lax.dynamic_slice_in_dim(query, block[0] * heads, heads, 1)
     mass = own[-2 * heads :].astype(F32)
     stack = jnp.stack([piece[slot, : -2 * heads] for piece in pieces])
     order = lax.rem(place[0] + parts - jnp.arange(parts), parts)
@@ -279,10 +286,14 @@
             moved = [around(sent[0][i], o) for i, o in enumerate(group)]
             sent = [jnp.stack([x[j] for x in moved]) for j in range(parts)]
         takes.append([sent[0]] + [along(sent[j], j) for j in range(1, parts)])
+        halves = [tokens // 4] if far else 1
         for o in group:
             if o:
                 piece = lax.dynamic_slice_in_dim(query_rows, block_of(o) * heads, heads, 2)
-                queries[-o % n] = around(piece, o)
+                cuts = jnp.split(piece, halves, axis=1)
+                for c, cut in enumerate(cuts):
+                    cuts[c] = around(cut, o)
+                queries[-o % n] = cuts
     for g, (group, take) in enumerate(zip(groups, takes)):
         owns = list(make_total(take, heads, count))
         if g == 0:
@@ -291,7 +302,7 @@
         pieces = [stack] + [along(stack, j) for j in range(1, parts)]
         for i, o in enumerate(group):
             slot = -o % n
-            query, block = (queries[slot], jnp.zeros(1, jnp.int32)) if o else (query_rows, here)
+            query, block = (queries[slot], jnp.zeros(1, jnp.int32)) if o else ([query_rows], here)
             mixed[slot] = make_read(
                 query, owns[i], pieces, i, block, heads, place, count**0.5
             )

time: 141 us -> 144 us (1.021)
  starting transfers between devices: 44.4 us -> 55.4 us
  waiting for transfers between devices: 61.8 us -> 53.6 us
    ppermute x18, starting transfers between devices: 23.5 us -> 29.4 us  [along(): lax.ppermute(x, 'sp', [(i, (i + offset) % parts) for i in range(parts)])]
    ppermute x18 -> x19, starting transfers between devices: 20.9 us -> 26 us  [around(): return lax.ppermute(x, 'dp', [(d, to[d][offset % n]) for d in range(n)])]
    ppermute x18 -> x19, waiting for transfers between devices: 46.3 us -> 42.2 us  [around(): return lax.ppermute(x, 'dp', [(d, to[d][offset % n]) for d in range(n)])]
    ppermute x18, waiting for transfers between devices: 15.5 us -> 11.5 us  [along(): lax.ppermute(x, 'sp', [(i, (i + offset) % parts) for i in range(parts)])]
  transfers between devices with their start and end apart: 36 -> 37, of which waited for: 14 -> 16; matrix products, arithmetic and copies ran while one was open for 8% -> 7% of each run, Pallas kernels for 8% -> 8%
where the time goes in v2:
time: 144 us
  starting transfers between devices  55.4 us (38%)
  waiting for transfers between devices  53.6 us (37%)
  Pallas kernels  12.4 us (9%)
  matrix products  11.2 us (8%)
  local copies, waits for them, and re-layouts  9.25 us (6%)
  other arithmetic  1.91 us (1%)
    ppermute x19, waiting for transfers between devices, around(): return lax.ppermute(x, 'dp', [(d, to[d][offset % n]) for d in range(n)])  42.2 us
    ppermute x18, starting transfers between devices, along(): lax.ppermute(x, 'sp', [(i, (i + offset) % parts) for i in range(parts)])  29.4 us
    ppermute x19, starting transfers between devices, around(): return lax.ppermute(x, 'dp', [(d, to[d][offset % n]) for d in range(n)])  26 us
    ppermute x18, waiting for transfers between devices, along(): lax.ppermute(x, 'sp', [(i, (i + offset) % parts) for i in range(parts)])  11.5 us
    unnamed x14, local copies, waits for them, and re-layouts  8.13 us
    pallas_call x3, Pallas kernels, partial_states(): pl.pallas_call(functools.partial(state_kernel, parts), grid_spec=pltpu.Pr...  7.83 us
    dot_general x8, matrix products, layer(): jnp.dot(mixed[-way * (k + 1) % n], weight, preferred_element_type=F32)  5.89 us
    pallas_call x4, Pallas kernels, read_states(): pl.pallas_call(functools.partial(read_kernel, parts, scale), grid_spec=pl...  3.79 us
  transfers between devices with their start and end apart: 37, of which 16 were waited for; matrix products, arithmetic and copies ran while one was open for 7% of the time, Pallas kernels for 8%

profile of v2, /device:TPU:0, one launch (start us, length us, event | category | flops | bytes accessed | tf_op | source)
XLA Modules:
  0.0 144.0 jit_solution(8512588349214230256)
XLA Ops:
  0.9 4.0 %collective-permute-start.22 = (bf16[1,64,8,128]{3,2,1,0:T(8,128)(2,1)S(1)}, bf16[1,64,8,128]{3,2,1,0:T(8,128)(2,1)S(1)}, u32[]{:S(2)}, u32[]{:S(2)}) collective-permute-start(bf16[1,64,8,128]{3,2,1,0:T(8,128)(2,1)S(1)} %constant_dynamic-slice_fusion), channel_id=1, source_target_pairs={{0,24},{8,16},{16,8},{24,0},{1,25},{9,17},{17,9},{25,1},{2,26},{10... | collective-permute-start | bytes 393224 | tf_op jit(solution)/shard_map/ppermute | solution.py:271
  8.7 1.7 %partial_states.5 = bf16[1,4,272,128]{3,2,1,0:T(8,128)(2,1)S(1)} custom-call(s32[4]{0:T(128)S(1)} %copy-done.6, s32[1]{0:T(128)} %bitcast.here.block, s32[1]{0:T(128)} %bitcast.1.place, bf16[1,256,32,128]{3,2,1,0:T(8,128)(2,1)S(1)} %copy-done, bf16[1,256,32,128]{3,2,1,0:T(8,128)(2,1)S(1)} %copy-done.2), custom_call_target="tpu_custom_call" | custom-call | flops 67108864 | bytes 1048576 | tf_op jit(solution)/shard_map/partial_states/pallas_call | solution.py:80
  12.1 2.1 %collective-permute-start = (bf16[1,272,128]{2,1,0:T(8,128)(2,1)S(1)}, bf16[1,272,128]{2,1,0:T(8,128)(2,1)S(1)}, u32[]{:S(2)}, u32[]{:S(2)}) collective-permute-start(bf16[1,272,128]{2,1,0:T(8,128)(2,1)S(1)} %get-tuple-element.16), channel_id=1, source_target_pairs={{0,2},{2,4},{4,6},{6,0},{1,3},{3,5},{5,7},{7,1},{8,10},{10,12},{12... | collective-permute-start | bytes 208904 | tf_op jit(solution)/shard_map/ppermute | solution.py:274
  14.2 2.6 %collective-permute-start.1 = (bf16[1,272,128]{2,1,0:T(8,128)(2,1)S(1)}, bf16[1,272,128]{2,1,0:T(8,128)(2,1)S(1)}, u32[]{:S(2)}, u32[]{:S(2)}) collective-permute-start(bf16[1,272,128]{2,1,0:T(8,128)(2,1)S(1)} %get-tuple-element.17), channel_id=1, source_target_pairs={{0,4},{2,6},{4,0},{6,2},{1,5},{3,7},{5,1},{7,3},{8,12},{10,14},{12... | collective-permute-start | bytes 208904 | tf_op jit(solution)/shard_map/ppermute | solution.py:274
  19.4 2.6 %collective-permute-start.23 = (bf16[1,192,8,128]{3,2,1,0:T(8,128)(2,1)S(1)}, bf16[1,192,8,128]{3,2,1,0:T(8,128)(2,1)S(1)}, u32[]{:S(2)}, u32[]{:S(2)}) collective-permute-start(bf16[1,192,8,128]{3,2,1,0:T(8,128)(2,1)S(1)} %constant_dynamic-slice_fusion.2), channel_id=1, source_target_pairs={{0,24},{8,16},{16,8},{24,0},{1,25},{9,17},{17,9},{25,1},{2,26},{10... | collective-permute-start | bytes 1179656 | tf_op jit(solution)/shard_map/ppermute | solution.py:271
  22.1 2.3 %collective-permute-start.5 = (bf16[1,272,128]{2,1,0:T(8,128)(2,1)S(1)}, bf16[1,272,128]{2,1,0:T(8,128)(2,1)S(1)}, u32[]{:S(2)}, u32[]{:S(2)}) collective-permute-start(bf16[1,272,128]{2,1,0:T(8,128)(2,1)S(1)} %bitcast.23), channel_id=1, source_target_pairs={{0,6},{2,0},{4,2},{6,4},{1,7},{3,1},{5,3},{7,5},{8,14},{10,8},{12,... | collective-permute-start | bytes 208904 | tf_op jit(solution)/shard_map/ppermute | solution.py:274
  24.6 4.5 %partial_states.4 = (bf16[2,272,128]{2,1,0:T(8,128)(2,1)}, bf16[2,272,128]{2,1,0:T(8,128)(2,1)}, bf16[2,272,128]{2,1,0:T(8,128)(2,1)}, bf16[2,272,128]{2,1,0:T(8,128)(2,1)}) custom-call(s32[8]{0:T(128)} %constant.29.clone.table, s32[1]{0:T(128)} %bitcast.here.block, s32[1]{0:T(128)} %bitcast.1.place, bf16[1,256,32,128]{3,2,1,0:T(8,128)(2,1)} %key.5, ...), custom_call_target="tpu_custom_call" | custom-call | flops 134217728 | bytes 2097152 | tf_op jit(solution)/shard_map/partial_states/pallas_call | solution.py:80
  32.1 2.8 %collective-permute-start.8 = (bf16[2,272,128]{2,1,0:T(8,128)(2,1)}, bf16[2,272,128]{2,1,0:T(8,128)(2,1)S(1)}, u32[]{:S(2)}, u32[]{:S(2)}) collective-permute-start(bf16[2,272,128]{2,1,0:T(8,128)(2,1)} %get-tuple-element.22), channel_id=1, source_target_pairs={{0,6},{2,0},{4,2},{6,4},{1,7},{3,1},{5,3},{7,5},{8,14},{10,8},{12,... | collective-permute-start | bytes 417800 | tf_op jit(solution)/shard_map/ppermute | solution.py:274
  37.8 1.7 %collective-permute-start.18 = (bf16[1,272,128]{2,1,0:T(8,128)(2,1)S(1)}, bf16[1,272,128]{2,1,0:T(8,128)(2,1)S(1)}, u32[]{:S(2)}, u32[]{:S(2)}) collective-permute-start(bf16[1,272,128]{2,1,0:T(8,128)(2,1)S(1)} %get-tuple-element.27), channel_id=1, source_target_pairs={{0,6},{2,0},{4,2},{6,4},{1,7},{3,1},{5,3},{7,5},{8,14},{10,8},{12,... | collective-permute-start | bytes 208904 | tf_op jit(solution)/shard_map/ppermute | solution.py:274
  39.5 2.2 %collective-permute-done.7.refs_2_ = bf16[2,272,128]{2,1,0:T(8,128)(2,1)S(1)} collective-permute-done((bf16[2,272,128]{2,1,0:T(8,128)(2,1)}, bf16[2,272,128]{2,1,0:T(8,128)(2,1)S(1)}, u32[]{:S(2)}, u32[]{:S(2)}) %collective-permute-start.7) | collective-permute-done | bytes 139296 | tf_op jit(solution)/shard_map/ppermute | solution.py:274
  41.7 2.2 %collective-permute-start.17 = (bf16[1,272,128]{2,1,0:T(8,128)(2,1)S(1)}, bf16[1,272,128]{2,1,0:T(8,128)(2,1)S(1)}, u32[]{:S(2)}, u32[]{:S(2)}) collective-permute-start(bf16[1,272,128]{2,1,0:T(8,128)(2,1)S(1)} %get-tuple-element.28), channel_id=1, source_target_pairs={{0,4},{2,6},{4,0},{6,2},{1,5},{3,7},{5,1},{7,3},{8,12},{10,14},{12... | collective-permute-start | bytes 208904 | tf_op jit(solution)/shard_map/ppermute | solution.py:274
  44.0 4.0 %collective-permute-start.16 = (bf16[1,272,128]{2,1,0:T(8,128)(2,1)S(1)}, bf16[1,272,128]{2,1,0:T(8,128)(2,1)S(1)}, u32[]{:S(2)}, u32[]{:S(2)}) collective-permute-start(bf16[1,272,128]{2,1,0:T(8,128)(2,1)S(1)} %get-tuple-element.29), channel_id=1, source_target_pairs={{0,2},{2,4},{4,6},{6,0},{1,3},{3,5},{5,7},{7,1},{8,10},{10,12},{12... | collective-permute-start | bytes 208904 | tf_op jit(solution)/shard_map/ppermute | solution.py:274
  49.1 1.7 %collective-permute-start.9 = (bf16[272,128]{1,0:T(8,128)(2,1)S(1)}, bf16[272,128]{1,0:T(8,128)(2,1)S(1)}, u32[]{:S(2)}, u32[]{:S(2)}) collective-permute-start(bf16[272,128]{1,0:T(8,128)(2,1)S(1)} %get-tuple-element.23), channel_id=1, source_target_pairs={{0,16},{8,0},{16,24},{24,8},{1,17},{9,1},{17,25},{25,9},{2,18},{10... | collective-permute-start | bytes 208904 | tf_op jit(solution)/shard_map/ppermute | solution.py:271
  52.5 2.7 %collective-permute-done.3.refs_1_ = bf16[1,272,128]{2,1,0:T(8,128)(2,1)S(1)} collective-permute-done((bf16[1,272,128]{2,1,0:T(8,128)(2,1)S(1)}, bf16[1,272,128]{2,1,0:T(8,128)(2,1)S(1)}, u32[]{:S(2)}, u32[]{:S(2)}) %collective-permute-start.3) | collective-permute-done | bytes 69664 | tf_op jit(solution)/shard_map/ppermute | solution.py:274
  55.2 1.7 %collective-permute-start.14 = (bf16[1,256,8,128]{3,2,1,0:T(8,128)(2,1)S(1)}, bf16[1,256,8,128]{3,2,1,0:T(8,128)(2,1)S(1)}, u32[]{:S(2)}, u32[]{:S(2)}) collective-permute-start(bf16[1,256,8,128]{3,2,1,0:T(8,128)(2,1)S(1)} %get-tuple-element.25), channel_id=1, source_target_pairs={{0,16},{8,0},{16,24},{24,8},{1,17},{9,1},{17,25},{25,9},{2,18},{10... | collective-permute-start | bytes 1572872 | tf_op jit(solution)/shard_map/ppermute | solution.py:271
  59.5 1.8 %collective-permute-done.21.refs_3_ = bf16[1,272,128]{2,1,0:T(8,128)(2,1)S(1)} collective-permute-done((bf16[1,272,128]{2,1,0:T(8,128)(2,1)S(1)}, bf16[1,272,128]{2,1,0:T(8,128)(2,1)S(1)}, u32[]{:S(2)}, u32[]{:S(2)}) %collective-permute-start.21) | collective-permute-done | bytes 69664 | tf_op jit(solution)/shard_map/ppermute | solution.py:274
  61.3 3.6 %collective-permute-start.13 = (bf16[2,272,128]{2,1,0:T(8,128)(2,1)S(1)}, bf16[2,272,128]{2,1,0:T(8,128)(2,1)S(1)}, u32[]{:S(2)}, u32[]{:S(2)}) collective-permute-start(bf16[2,272,128]{2,1,0:T(8,128)(2,1)S(1)} %pad_maximum_fusion.refs_0_), channel_id=1, source_target_pairs={{0,6},{2,0},{4,2},{6,4},{1,7},{3,1},{5,3},{7,5},{8,14},{10,8},{12,... | collective-permute-start | bytes 417800 | tf_op jit(solution)/shard_map/ppermute | solution.py:274
  67.5 3.4 %copy-done.3 = bf16[1024,4096]{1,0:T(8,128)(2,1)S(1)} copy-done((bf16[1024,4096]{1,0:T(8,128)(2,1)S(1)}, bf16[1024,4096]{1,0:T(8,128)(2,1)}, u32[]{:S(2)}) %copy-start.3) | copy-done | bytes 8388632
  77.3 1.7 %collective-permute-start.34 = (bf16[256,1024]{1,0:T(8,128)(2,1)S(1)}, bf16[256,1024]{1,0:T(8,128)(2,1)S(1)}, u32[]{:S(2)}, u32[]{:S(2)}) collective-permute-start(bf16[256,1024]{1,0:T(8,128)(2,1)S(1)} %fusion.58), channel_id=1, source_target_pairs={{0,16},{8,0},{16,24},{24,8},{1,17},{9,1},{17,25},{25,9},{2,18},{10... | collective-permute-start | bytes 1572872 | tf_op jit(solution)/shard_map/ppermute | solution.py:271
  80.1 1.7 %collective-permute-start.28 = (bf16[256,1024]{1,0:T(8,128)(2,1)S(1)}, bf16[256,1024]{1,0:T(8,128)(2,1)S(1)}, u32[]{:S(2)}, u32[]{:S(2)}) collective-permute-start(bf16[256,1024]{1,0:T(8,128)(2,1)S(1)} %fusion.52), channel_id=1, source_target_pairs={{0,16},{8,0},{16,24},{24,8},{1,17},{9,1},{17,25},{25,9},{2,18},{10... | collective-permute-start | bytes 1572872 | tf_op jit(solution)/shard_map/ppermute | solution.py:271
  83.1 9.0 %collective-permute-done.34 = bf16[256,1024]{1,0:T(8,128)(2,1)S(1)} collective-permute-done((bf16[256,1024]{1,0:T(8,128)(2,1)S(1)}, bf16[256,1024]{1,0:T(8,128)(2,1)S(1)}, u32[]{:S(2)}, u32[]{:S(2)}) %collective-permute-start.34) | collective-permute-done | bytes 524320 | tf_op jit(solution)/shard_map/ppermute | solution.py:271
  92.8 1.7 %collective-permute-start.35 = (bf16[256,1024]{1,0:T(8,128)(2,1)S(1)}, bf16[256,1024]{1,0:T(8,128)(2,1)S(1)}, u32[]{:S(2)}, u32[]{:S(2)}) collective-permute-start(bf16[256,1024]{1,0:T(8,128)(2,1)S(1)} %fusion.61), channel_id=1, source_target_pairs={{0,16},{8,0},{16,24},{24,8},{1,17},{9,1},{17,25},{25,9},{2,18},{10... | collective-permute-start | bytes 1572872 | tf_op jit(solution)/shard_map/ppermute | solution.py:271
  95.7 7.6 %collective-permute-done.28 = bf16[256,1024]{1,0:T(8,128)(2,1)S(1)} collective-permute-done((bf16[256,1024]{1,0:T(8,128)(2,1)S(1)}, bf16[256,1024]{1,0:T(8,128)(2,1)S(1)}, u32[]{:S(2)}, u32[]{:S(2)}) %collective-permute-start.28) | collective-permute-done | bytes 524320 | tf_op jit(solution)/shard_map/ppermute | solution.py:271
  104.1 1.7 %collective-permute-start.29 = (bf16[256,1024]{1,0:T(8,128)(2,1)S(1)}, bf16[256,1024]{1,0:T(8,128)(2,1)S(1)}, u32[]{:S(2)}, u32[]{:S(2)}) collective-permute-start(bf16[256,1024]{1,0:T(8,128)(2,1)S(1)} %fusion.73), channel_id=1, source_target_pairs={{0,16},{8,0},{16,24},{24,8},{1,17},{9,1},{17,25},{25,9},{2,18},{10... | collective-permute-start | bytes 1572872 | tf_op jit(solution)/shard_map/ppermute | solution.py:271
  107.0 7.6 %collective-permute-done.35 = bf16[256,1024]{1,0:T(8,128)(2,1)S(1)} collective-permute-done((bf16[256,1024]{1,0:T(8,128)(2,1)S(1)}, bf16[256,1024]{1,0:T(8,128)(2,1)S(1)}, u32[]{:S(2)}, u32[]{:S(2)}) %collective-permute-start.35) | collective-permute-done | bytes 524320 | tf_op jit(solution)/shard_map/ppermute | solution.py:271
  115.3 1.7 %collective-permute-start.36 = (bf16[256,1024]{1,0:T(8,128)(2,1)S(1)}, bf16[256,1024]{1,0:T(8,128)(2,1)S(1)}, u32[]{:S(2)}, u32[]{:S(2)}) collective-permute-start(bf16[256,1024]{1,0:T(8,128)(2,1)S(1)} %fusion.64), channel_id=1, source_target_pairs={{0,16},{8,0},{16,24},{24,8},{1,17},{9,1},{17,25},{25,9},{2,18},{10... | collective-permute-start | bytes 1572872 | tf_op jit(solution)/shard_map/ppermute | solution.py:271
  118.2 7.6 %collective-permute-done.29 = bf16[256,1024]{1,0:T(8,128)(2,1)S(1)} collective-permute-done((bf16[256,1024]{1,0:T(8,128)(2,1)S(1)}, bf16[256,1024]{1,0:T(8,128)(2,1)S(1)}, u32[]{:S(2)}, u32[]{:S(2)}) %collective-permute-start.29) | collective-permute-done | bytes 524320 | tf_op jit(solution)/shard_map/ppermute | solution.py:271
  126.6 1.7 %collective-permute-start.30 = (bf16[256,1024]{1,0:T(8,128)(2,1)S(1)}, bf16[256,1024]{1,0:T(8,128)(2,1)S(1)}, u32[]{:S(2)}, u32[]{:S(2)}) collective-permute-start(bf16[256,1024]{1,0:T(8,128)(2,1)S(1)} %fusion.76), channel_id=1, source_target_pairs={{0,16},{8,0},{16,24},{24,8},{1,17},{9,1},{17,25},{25,9},{2,18},{10... | collective-permute-start | bytes 1572872 | tf_op jit(solution)/shard_map/ppermute | solution.py:271
  129.4 2.4 %fusion.86 = f32[256,4096]{1,0:T(8,128)S(1)} fusion(bf16[256,1024]{1,0:T(8,128)(2,1)S(1)} %read_states.4, bf16[1024,4096]{1,0:T(8,128)(2,1)S(1)} %hold.1), kind=kOutput, calls=%fused_computation.52 | convolution fusion | flops 2147483648 | bytes 13107200 | tf_op jit(solution)/shard_map/dot_general | solution.py:327
  131.8 3.4 %collective-permute-done.36 = bf16[256,1024]{1,0:T(8,128)(2,1)S(1)} collective-permute-done((bf16[256,1024]{1,0:T(8,128)(2,1)S(1)}, bf16[256,1024]{1,0:T(8,128)(2,1)S(1)}, u32[]{:S(2)}, u32[]{:S(2)}) %collective-permute-start.36) | collective-permute-done | bytes 524320 | tf_op jit(solution)/shard_map/ppermute | solution.py:271
  136.5 4.4 %collective-permute-done.30 = bf16[256,1024]{1,0:T(8,128)(2,1)S(1)} collective-permute-done((bf16[256,1024]{1,0:T(8,128)(2,1)S(1)}, bf16[256,1024]{1,0:T(8,128)(2,1)S(1)}, u32[]{:S(2)}, u32[]{:S(2)}) %collective-permute-start.30) | collective-permute-done | bytes 524320 | tf_op jit(solution)/shard_map/ppermute | solution.py:271
  142.1 1.9 %fusion = bf16[1,256,4096]{2,1,0:T(8,128)(2,1)} fusion(f32[256,4096]{1,0:T(8,128)S(1)} %fusion.86, bf16[256,1024]{1,0:T(8,128)(2,1)S(1)} %collective-permute-done.36, bf16[256,1024]{1,0:T(8,128)(2,1)S(1)} %collective-permute-done.33, bf16[256,1024]{1,0:T(8,128)(2,1)S(1)} %collective-permute-done.30, bf16[256,1024]{1,0:T(8,128)(2,1)S(1)} %collective-permute-done.27), kind=kLoop, calls=%fused_computation.1 | loop fusion | flops 10485760 | bytes 8388608 | tf_op jit(solution)/shard_map/broadcast_in_dim | solution.py:329
  (87 shorter events, 41.9 us)
Async XLA Ops:
  0.9 28.2 %collective-permute-start.22 = (bf16[1,64,8,128]{3,2,1,0:T(8,128)(2,1)S(1)}, bf16[1,64,8,128]{3,2,1,0:T(8,128)(2,1)S(1)}, u32[]{:S(2)}, u32[]{:S(2)}) collective-permute-start(bf16[1,64,8,128]{3,2,1,0:T(8,128)(2,1)S(1)} %constant_dynamic-slice_fusion), channel_id=1, source_target_pairs={{0,24},{8,16},{16,8},{24,0},{1,25},{9,17},{17,9},{25,1},{2,26},{10... | collective-permute-start | bytes 393224 | tf_op jit(solution)/shard_map/ppermute | solution.py:271
  10.4 24.6 %collective-permute-start.15 = (bf16[4,272,128]{2,1,0:T(8,128)(2,1)S(1)}, bf16[4,272,128]{2,1,0:T(8,128)(2,1)S(1)}, u32[]{:S(2)}, u32[]{:S(2)}) collective-permute-start(bf16[4,272,128]{2,1,0:T(8,128)(2,1)S(1)} %bitcast.33), channel_id=1, source_target_pairs={{0,24},{8,16},{16,8},{24,0},{1,25},{9,17},{17,9},{25,1},{2,26},{10... | collective-permute-start | bytes 835592 | tf_op jit(solution)/shard_map/ppermute | solution.py:271
  12.1 7.3 %collective-permute-start = (bf16[1,272,128]{2,1,0:T(8,128)(2,1)S(1)}, bf16[1,272,128]{2,1,0:T(8,128)(2,1)S(1)}, u32[]{:S(2)}, u32[]{:S(2)}) collective-permute-start(bf16[1,272,128]{2,1,0:T(8,128)(2,1)S(1)} %get-tuple-element.16), channel_id=1, source_target_pairs={{0,2},{2,4},{4,6},{6,0},{1,3},{3,5},{5,7},{7,1},{8,10},{10,12},{12... | collective-permute-start | bytes 208904 | tf_op jit(solution)/shard_map/ppermute | solution.py:274
  14.2 7.9 %collective-permute-start.1 = (bf16[1,272,128]{2,1,0:T(8,128)(2,1)S(1)}, bf16[1,272,128]{2,1,0:T(8,128)(2,1)S(1)}, u32[]{:S(2)}, u32[]{:S(2)}) collective-permute-start(bf16[1,272,128]{2,1,0:T(8,128)(2,1)S(1)} %get-tuple-element.17), channel_id=1, source_target_pairs={{0,4},{2,6},{4,0},{6,2},{1,5},{3,7},{5,1},{7,3},{8,12},{10,14},{12... | collective-permute-start | bytes 208904 | tf_op jit(solution)/shard_map/ppermute | solution.py:274
  19.4 38.6 %collective-permute-start.23 = (bf16[1,192,8,128]{3,2,1,0:T(8,128)(2,1)S(1)}, bf16[1,192,8,128]{3,2,1,0:T(8,128)(2,1)S(1)}, u32[]{:S(2)}, u32[]{:S(2)}) collective-permute-start(bf16[1,192,8,128]{3,2,1,0:T(8,128)(2,1)S(1)} %constant_dynamic-slice_fusion.2), channel_id=1, source_target_pairs={{0,24},{8,16},{16,8},{24,0},{1,25},{9,17},{17,9},{25,1},{2,26},{10... | collective-permute-start | bytes 1179656 | tf_op jit(solution)/shard_map/ppermute | solution.py:271
  22.1 8.4 %collective-permute-start.5 = (bf16[1,272,128]{2,1,0:T(8,128)(2,1)S(1)}, bf16[1,272,128]{2,1,0:T(8,128)(2,1)S(1)}, u32[]{:S(2)}, u32[]{:S(2)}) collective-permute-start(bf16[1,272,128]{2,1,0:T(8,128)(2,1)S(1)} %bitcast.23), channel_id=1, source_target_pairs={{0,6},{2,0},{4,2},{6,4},{1,7},{3,1},{5,3},{7,5},{8,14},{10,8},{12,... | collective-permute-start | bytes 208904 | tf_op jit(solution)/shard_map/ppermute | solution.py:274
  24.4 7.8 %collective-permute-start.4 = (bf16[1,272,128]{2,1,0:T(8,128)(2,1)S(1)}, bf16[1,272,128]{2,1,0:T(8,128)(2,1)S(1)}, u32[]{:S(2)}, u32[]{:S(2)}) collective-permute-start(bf16[1,272,128]{2,1,0:T(8,128)(2,1)S(1)} %bitcast.24), channel_id=1, source_target_pairs={{0,4},{2,6},{4,0},{6,2},{1,5},{3,7},{5,1},{7,3},{8,12},{10,14},{12... | collective-permute-start | bytes 208904 | tf_op jit(solution)/shard_map/ppermute | solution.py:274
  29.1 8.7 %collective-permute-start.6 = (bf16[2,272,128]{2,1,0:T(8,128)(2,1)}, bf16[2,272,128]{2,1,0:T(8,128)(2,1)S(1)}, u32[]{:S(2)}, u32[]{:S(2)}) collective-permute-start(bf16[2,272,128]{2,1,0:T(8,128)(2,1)} %get-tuple-element.20), channel_id=1, source_target_pairs={{0,2},{2,4},{4,6},{6,0},{1,3},{3,5},{5,7},{7,1},{8,10},{10,12},{12... | collective-permute-start | bytes 417800 | tf_op jit(solution)/shard_map/ppermute | solution.py:274
  30.5 11.2 %collective-permute-start.7 = (bf16[2,272,128]{2,1,0:T(8,128)(2,1)}, bf16[2,272,128]{2,1,0:T(8,128)(2,1)S(1)}, u32[]{:S(2)}, u32[]{:S(2)}) collective-permute-start(bf16[2,272,128]{2,1,0:T(8,128)(2,1)} %get-tuple-element.21), channel_id=1, source_target_pairs={{0,4},{2,6},{4,0},{6,2},{1,5},{3,7},{5,1},{7,3},{8,12},{10,14},{12... | collective-permute-start | bytes 417800 | tf_op jit(solution)/shard_map/ppermute | solution.py:274
  32.1 11.8 %collective-permute-start.8 = (bf16[2,272,128]{2,1,0:T(8,128)(2,1)}, bf16[2,272,128]{2,1,0:T(8,128)(2,1)S(1)}, u32[]{:S(2)}, u32[]{:S(2)}) collective-permute-start(bf16[2,272,128]{2,1,0:T(8,128)(2,1)} %get-tuple-element.22), channel_id=1, source_target_pairs={{0,6},{2,0},{4,2},{6,4},{1,7},{3,1},{5,3},{7,5},{8,14},{10,8},{12,... | collective-permute-start | bytes 417800 | tf_op jit(solution)/shard_map/ppermute | solution.py:274
  35.0 38.9 %collective-permute-start.24 = (bf16[1,256,8,128]{3,2,1,0:T(8,128)(2,1)S(1)}, bf16[1,256,8,128]{3,2,1,0:T(8,128)(2,1)S(1)}, u32[]{:S(2)}, u32[]{:S(2)}) collective-permute-start(bf16[1,256,8,128]{3,2,1,0:T(8,128)(2,1)S(1)} %get-tuple-element.26), channel_id=1, source_target_pairs={{0,8},{8,24},{16,0},{24,16},{1,9},{9,25},{17,1},{25,17},{2,10},{10... | collective-permute-start | bytes 1572872 | tf_op jit(solution)/shard_map/ppermute | solution.py:271
  37.8 11.2 %collective-permute-start.18 = (bf16[1,272,128]{2,1,0:T(8,128)(2,1)S(1)}, bf16[1,272,128]{2,1,0:T(8,128)(2,1)S(1)}, u32[]{:S(2)}, u32[]{:S(2)}) collective-permute-start(bf16[1,272,128]{2,1,0:T(8,128)(2,1)S(1)} %get-tuple-element.27), channel_id=1, source_target_pairs={{0,6},{2,0},{4,2},{6,4},{1,7},{3,1},{5,3},{7,5},{8,14},{10,8},{12,... | collective-permute-start | bytes 208904 | tf_op jit(solution)/shard_map/ppermute | solution.py:274
  41.7 7.4 %collective-permute-start.17 = (bf16[1,272,128]{2,1,0:T(8,128)(2,1)S(1)}, bf16[1,272,128]{2,1,0:T(8,128)(2,1)S(1)}, u32[]{:S(2)}, u32[]{:S(2)}) collective-permute-start(bf16[1,272,128]{2,1,0:T(8,128)(2,1)S(1)} %get-tuple-element.28), channel_id=1, source_target_pairs={{0,4},{2,6},{4,0},{6,2},{1,5},{3,7},{5,1},{7,3},{8,12},{10,14},{12... | collective-permute-start | bytes 208904 | tf_op jit(solution)/shard_map/ppermute | solution.py:274
  49.1 7.8 %collective-permute-start.9 = (bf16[272,128]{1,0:T(8,128)(2,1)S(1)}, bf16[272,128]{1,0:T(8,128)(2,1)S(1)}, u32[]{:S(2)}, u32[]{:S(2)}) collective-permute-start(bf16[272,128]{1,0:T(8,128)(2,1)S(1)} %get-tuple-element.23), channel_id=1, source_target_pairs={{0,16},{8,0},{16,24},{24,8},{1,17},{9,1},{17,25},{25,9},{2,18},{10... | collective-permute-start | bytes 208904 | tf_op jit(solution)/shard_map/ppermute | solution.py:271
  55.2 20.4 %collective-permute-start.14 = (bf16[1,256,8,128]{3,2,1,0:T(8,128)(2,1)S(1)}, bf16[1,256,8,128]{3,2,1,0:T(8,128)(2,1)S(1)}, u32[]{:S(2)}, u32[]{:S(2)}) collective-permute-start(bf16[1,256,8,128]{3,2,1,0:T(8,128)(2,1)S(1)} %get-tuple-element.25), channel_id=1, source_target_pairs={{0,16},{8,0},{16,24},{24,8},{1,17},{9,1},{17,25},{25,9},{2,18},{10... | collective-permute-start | bytes 1572872 | tf_op jit(solution)/shard_map/ppermute | solution.py:271
  58.0 8.4 %collective-permute-start.20 = (bf16[1,272,128]{2,1,0:T(8,128)(2,1)S(1)}, bf16[1,272,128]{2,1,0:T(8,128)(2,1)S(1)}, u32[]{:S(2)}, u32[]{:S(2)}) collective-permute-start(bf16[1,272,128]{2,1,0:T(8,128)(2,1)S(1)} %bitcast.28), channel_id=1, source_target_pairs={{0,4},{2,6},{4,0},{6,2},{1,5},{3,7},{5,1},{7,3},{8,12},{10,14},{12... | collective-permute-start | bytes 208904 | tf_op jit(solution)/shard_map/ppermute | solution.py:274
  58.0 8.4 %collective-permute-start.19 = (bf16[1,272,128]{2,1,0:T(8,128)(2,1)S(1)}, bf16[1,272,128]{2,1,0:T(8,128)(2,1)S(1)}, u32[]{:S(2)}, u32[]{:S(2)}) collective-permute-start(bf16[1,272,128]{2,1,0:T(8,128)(2,1)S(1)} %bitcast.29), channel_id=1, source_target_pairs={{0,2},{2,4},{4,6},{6,0},{1,3},{3,5},{5,7},{7,1},{8,10},{10,12},{12... | collective-permute-start | bytes 208904 | tf_op jit(solution)/shard_map/ppermute | solution.py:274
  61.3 12.1 %collective-permute-start.13 = (bf16[2,272,128]{2,1,0:T(8,128)(2,1)S(1)}, bf16[2,272,128]{2,1,0:T(8,128)(2,1)S(1)}, u32[]{:S(2)}, u32[]{:S(2)}) collective-permute-start(bf16[2,272,128]{2,1,0:T(8,128)(2,1)S(1)} %pad_maximum_fusion.refs_0_), channel_id=1, source_target_pairs={{0,6},{2,0},{4,2},{6,4},{1,7},{3,1},{5,3},{7,5},{8,14},{10,8},{12,... | collective-permute-start | bytes 417800 | tf_op jit(solution)/shard_map/ppermute | solution.py:274
  66.4 7.4 %collective-permute-start.12 = (bf16[2,272,128]{2,1,0:T(8,128)(2,1)S(1)}, bf16[2,272,128]{2,1,0:T(8,128)(2,1)S(1)}, u32[]{:S(2)}, u32[]{:S(2)}) collective-permute-start(bf16[2,272,128]{2,1,0:T(8,128)(2,1)S(1)} %pad_maximum_fusion.refs_0_), channel_id=1, source_target_pairs={{0,4},{2,6},{4,0},{6,2},{1,5},{3,7},{5,1},{7,3},{8,12},{10,14},{12... | collective-permute-start | bytes 417800 | tf_op jit(solution)/shard_map/ppermute | solution.py:274
  66.4 7.4 %collective-permute-start.11 = (bf16[2,272,128]{2,1,0:T(8,128)(2,1)S(1)}, bf16[2,272,128]{2,1,0:T(8,128)(2,1)S(1)}, u32[]{:S(2)}, u32[]{:S(2)}) collective-permute-start(bf16[2,272,128]{2,1,0:T(8,128)(2,1)S(1)} %pad_maximum_fusion.refs_0_), channel_id=1, source_target_pairs={{0,2},{2,4},{4,6},{6,0},{1,3},{3,5},{5,7},{7,1},{8,10},{10,12},{12... | collective-permute-start | bytes 417800 | tf_op jit(solution)/shard_map/ppermute | solution.py:274
  77.3 14.8 %collective-permute-start.34 = (bf16[256,1024]{1,0:T(8,128)(2,1)S(1)}, bf16[256,1024]{1,0:T(8,128)(2,1)S(1)}, u32[]{:S(2)}, u32[]{:S(2)}) collective-permute-start(bf16[256,1024]{1,0:T(8,128)(2,1)S(1)} %fusion.58), channel_id=1, source_target_pairs={{0,16},{8,0},{16,24},{24,8},{1,17},{9,1},{17,25},{25,9},{2,18},{10... | collective-permute-start | bytes 1572872 | tf_op jit(solution)/shard_map/ppermute | solution.py:271
  79.0 15.6 %collective-permute-start.31 = (bf16[256,1024]{1,0:T(8,128)(2,1)S(1)}, bf16[256,1024]{1,0:T(8,128)(2,1)S(1)}, u32[]{:S(2)}, u32[]{:S(2)}) collective-permute-start(bf16[256,1024]{1,0:T(8,128)(2,1)S(1)} %fusion.55), channel_id=1, source_target_pairs={{0,8},{8,24},{16,0},{24,16},{1,9},{9,25},{17,1},{25,17},{2,10},{10... | collective-permute-start | bytes 1572872 | tf_op jit(solution)/shard_map/ppermute | solution.py:271
  80.1 23.3 %collective-permute-start.28 = (bf16[256,1024]{1,0:T(8,128)(2,1)S(1)}, bf16[256,1024]{1,0:T(8,128)(2,1)S(1)}, u32[]{:S(2)}, u32[]{:S(2)}) collective-permute-start(bf16[256,1024]{1,0:T(8,128)(2,1)S(1)} %fusion.52), channel_id=1, source_target_pairs={{0,16},{8,0},{16,24},{24,8},{1,17},{9,1},{17,25},{25,9},{2,18},{10... | collective-permute-start | bytes 1572872 | tf_op jit(solution)/shard_map/ppermute | solution.py:271
  82.5 23.3 %collective-permute-start.25 = (bf16[256,1024]{1,0:T(8,128)(2,1)S(1)}, bf16[256,1024]{1,0:T(8,128)(2,1)S(1)}, u32[]{:S(2)}, u32[]{:S(2)}) collective-permute-start(bf16[256,1024]{1,0:T(8,128)(2,1)S(1)} %fusion.49), channel_id=1, source_target_pairs={{0,8},{8,24},{16,0},{24,16},{1,9},{9,25},{17,1},{25,17},{2,10},{10... | collective-permute-start | bytes 1572872 | tf_op jit(solution)/shard_map/ppermute | solution.py:271
  92.8 21.7 %collective-permute-start.35 = (bf16[256,1024]{1,0:T(8,128)(2,1)S(1)}, bf16[256,1024]{1,0:T(8,128)(2,1)S(1)}, u32[]{:S(2)}, u32[]{:S(2)}) collective-permute-start(bf16[256,1024]{1,0:T(8,128)(2,1)S(1)} %fusion.61), channel_id=1, source_target_pairs={{0,16},{8,0},{16,24},{24,8},{1,17},{9,1},{17,25},{25,9},{2,18},{10... | collective-permute-start | bytes 1572872 | tf_op jit(solution)/shard_map/ppermute | solution.py:271
  95.3 21.7 %collective-permute-start.32 = (bf16[256,1024]{1,0:T(8,128)(2,1)S(1)}, bf16[256,1024]{1,0:T(8,128)(2,1)S(1)}, u32[]{:S(2)}, u32[]{:S(2)}) collective-permute-start(bf16[256,1024]{1,0:T(8,128)(2,1)S(1)} %fusion.67), channel_id=1, source_target_pairs={{0,8},{8,24},{16,0},{24,16},{1,9},{9,25},{17,1},{25,17},{2,10},{10... | collective-permute-start | bytes 1572872 | tf_op jit(solution)/shard_map/ppermute | solution.py:271
  104.1 21.7 %collective-permute-start.29 = (bf16[256,1024]{1,0:T(8,128)(2,1)S(1)}, bf16[256,1024]{1,0:T(8,128)(2,1)S(1)}, u32[]{:S(2)}, u32[]{:S(2)}) collective-permute-start(bf16[256,1024]{1,0:T(8,128)(2,1)S(1)} %fusion.73), channel_id=1, source_target_pairs={{0,16},{8,0},{16,24},{24,8},{1,17},{9,1},{17,25},{25,9},{2,18},{10... | collective-permute-start | bytes 1572872 | tf_op jit(solution)/shard_map/ppermute | solution.py:271
  106.6 21.7 %collective-permute-start.26 = (bf16[256,1024]{1,0:T(8,128)(2,1)S(1)}, bf16[256,1024]{1,0:T(8,128)(2,1)S(1)}, u32[]{:S(2)}, u32[]{:S(2)}) collective-permute-start(bf16[256,1024]{1,0:T(8,128)(2,1)S(1)} %fusion.79), channel_id=1, source_target_pairs={{0,8},{8,24},{16,0},{24,16},{1,9},{9,25},{17,1},{25,17},{2,10},{10... | collective-permute-start | bytes 1572872 | tf_op jit(solution)/shard_map/ppermute | solution.py:271
  115.3 19.9 %collective-permute-start.36 = (bf16[256,1024]{1,0:T(8,128)(2,1)S(1)}, bf16[256,1024]{1,0:T(8,128)(2,1)S(1)}, u32[]{:S(2)}, u32[]{:S(2)}) collective-permute-start(bf16[256,1024]{1,0:T(8,128)(2,1)S(1)} %fusion.64), channel_id=1, source_target_pairs={{0,16},{8,0},{16,24},{24,8},{1,17},{9,1},{17,25},{25,9},{2,18},{10... | collective-permute-start | bytes 1572872 | tf_op jit(solution)/shard_map/ppermute | solution.py:271
  117.8 18.7 %collective-permute-start.33 = (bf16[256,1024]{1,0:T(8,128)(2,1)S(1)}, bf16[256,1024]{1,0:T(8,128)(2,1)S(1)}, u32[]{:S(2)}, u32[]{:S(2)}) collective-permute-start(bf16[256,1024]{1,0:T(8,128)(2,1)S(1)} %fusion.70), channel_id=1, source_target_pairs={{0,8},{8,24},{16,0},{24,16},{1,9},{9,25},{17,1},{25,17},{2,10},{10... | collective-permute-start | bytes 1572872 | tf_op jit(solution)/shard_map/ppermute | solution.py:271
  126.6 14.3 %collective-permute-start.30 = (bf16[256,1024]{1,0:T(8,128)(2,1)S(1)}, bf16[256,1024]{1,0:T(8,128)(2,1)S(1)}, u32[]{:S(2)}, u32[]{:S(2)}) collective-permute-start(bf16[256,1024]{1,0:T(8,128)(2,1)S(1)} %fusion.76), channel_id=1, source_target_pairs={{0,16},{8,0},{16,24},{24,8},{1,17},{9,1},{17,25},{25,9},{2,18},{10... | collective-permute-start | bytes 1572872 | tf_op jit(solution)/shard_map/ppermute | solution.py:271
  129.0 13.1 %collective-permute-start.27 = (bf16[256,1024]{1,0:T(8,128)(2,1)S(1)}, bf16[256,1024]{1,0:T(8,128)(2,1)S(1)}, u32[]{:S(2)}, u32[]{:S(2)}) collective-permute-start(bf16[256,1024]{1,0:T(8,128)(2,1)S(1)} %fusion.82), channel_id=1, source_target_pairs={{0,8},{8,24},{16,0},{24,16},{1,9},{9,25},{17,1},{25,17},{2,10},{10... | collective-permute-start | bytes 1572872 | tf_op jit(solution)/shard_map/ppermute | solution.py:271
  (12 other events, 49.0 us)

commit v3 on v2

--- a/solution.py
+++ b/solution.py
@@ -10,7 +10,7 @@
 
 
 F32, BF16 = jnp.float32, jnp.bfloat16
-CHUNKS = 2
+SHARES = (1, 1)
 MIB = 1 << 20
 
 
@@ -197,6 +197,31 @@
     )(weight)
 
 
+def finish_kernel(product, *refs):
+    first, second, out = refs[-3:]
+    half = first.shape[1]
+    out[0, :, :half] = (product[:, :half] + first[...].astype(F32)).astype(BF16)
+    out[0, :, half:] = (product[:, half:] + second[...].astype(F32)).astype(BF16)
+
+
+def finish(result, product, first, second, shape, start):
+    tokens, width = product.shape
+    whole = pl.BlockSpec((tokens, width // 2), lambda i: (0, 0))
+    given = [] if result is None else [result]
+    return pl.pallas_call(
+        finish_kernel,
+        grid=(1,),
+        in_specs=[pl.BlockSpec((tokens, width), lambda i: (0, 0))]
+        + [pl.BlockSpec(memory_space=pl.ANY)] * len(given)
+        + [whole, whole],
+        out_specs=pl.BlockSpec((1, tokens, width), lambda i: (0, 0, start // width)),
+        out_shape=jax.ShapeDtypeStruct(shape, BF16),
+        input_output_aliases={1: 0} if given else {},
+        compiler_params=pltpu.CompilerParams(vmem_limit_bytes=24 * MIB),
+        name="finish",
+    )(product, *given, first, second)
+
+
 def partial_states_plain(key, value, table, here, place, blocks, heads, parts, grant, joined):
     _, _, _, size = key.shape
     outs = [[] for _ in range(parts)]
@@ -276,7 +301,6 @@
     groups = [g for g in (sorted({1, n - 1} - {n, 0}), list(range(2, n - 1)), [0]) if g]
 
     takes, queries, mixed = [], {}, {}
-    step = width // (2 * CHUNKS)
     for g, group in enumerate(groups):
         table = jnp.array([to[d][o] for d in range(n) for o in group], jnp.int32)
         size_of = (len(group), heads, parts, 16 if g else 56)
@@ -311,22 +335,34 @@
         out_weight = hold(out_weight)
 
     lanes = []
-    for c in range(2 * CHUNKS):
-        way = 1 if c % 2 == 0 else -1
-        lanes.append((way, out_weight[:, c * step : (c + 1) * step]))
+    start, unit = 0, width // (2 * sum(SHARES))
+    for share in SHARES:
+        for way in (1, -1):
+            lanes.append((way, out_weight[:, start : start + share * unit]))
+            start += share * unit
     accs = []
     for way, weight in lanes:
         acc = jnp.dot(mixed[-way % n], weight, preferred_element_type=F32).astype(BF16)
         accs.append(acc)
     for k in range(1, n):
         for lane, (way, weight) in enumerate(lanes):
-            accs[lane] = around(accs[lane], way).astype(F32)
+            accs[lane] = around(accs[lane], way)
             if k < n - 1:
                 product = jnp.dot(mixed[-way * (k + 1) % n], weight, preferred_element_type=F32)
-                accs[lane] = (product + accs[lane]).astype(BF16)
-    product = jnp.dot(mixed[0], out_weight, preferred_element_type=F32)
-    product = lax.optimization_barrier(product)
-    return (product + jnp.concatenate(accs, axis=1)).astype(BF16)[None]
+                accs[lane] = (product + accs[lane].astype(F32)).astype(BF16)
+    result, start = None, 0
+    for lane in range(0, len(lanes), 2):
+        stop = start + 2 * lanes[lane][1].shape[1]
+        weight = out_weight[:, start:stop]
+        product = jnp.dot(mixed[0], weight, preferred_element_type=F32)
+        pair = accs[lane : lane + 2]
+        if fits:
+            result = finish(result, product, *pair, (1, tokens, width), start)
+        else:
+            part = (product + jnp.concatenate(pair, axis=1).astype(F32)).astype(BF16)[None]
+            result = part if result is None else jnp.concatenate([result, part], axis=2)
+        start = stop
+    return result
 
 
 def solution(mesh):

time: 144 us -> 146 us (1.014)
  local copies, waits for them, and re-layouts: 9.25 us -> 12.4 us
  Pallas kernels: 12.4 us -> 14.7 us
  waiting for transfers between devices: 53.6 us -> 51.5 us
  other arithmetic: 1.91 us -> 0.01 us
    pallas_call x0 -> x2, Pallas kernels: none -> 2.28 us  [finish(): pl.pallas_call(finish_kernel, grid=(1,), in_specs=[pl.BlockSpec((tokens,...]
    broadcast_in_dim x1 -> x0, other arithmetic: 1.89 us -> none  [layer(): return (product + jnp.concatenate(accs, axis=1)).astype(BF16)[None]]
  transfers between devices with their start and end apart: 37 -> 37, of which waited for: 16 -> 13; matrix products, arithmetic and copies ran while one was open for 7% -> 9% of each run, Pallas kernels for 8% -> 9%
where the time goes in v3:
time: 146 us
  starting transfers between devices  55.3 us (38%)
  waiting for transfers between devices  51.5 us (35%)
  Pallas kernels  14.7 us (10%)
  local copies, waits for them, and re-layouts  12.4 us (8%)
  matrix products  11.3 us (8%)
    ppermute x19, waiting for transfers between devices, around(): return lax.ppermute(x, 'dp', [(d, to[d][offset % n]) for d in range(n)])  41.5 us
    ppermute x18, starting transfers between devices, along(): lax.ppermute(x, 'sp', [(i, (i + offset) % parts) for i in range(parts)])  29.5 us
    ppermute x19, starting transfers between devices, around(): return lax.ppermute(x, 'dp', [(d, to[d][offset % n]) for d in range(n)])  25.8 us
    ppermute x18, waiting for transfers between devices, along(): lax.ppermute(x, 'sp', [(i, (i + offset) % parts) for i in range(parts)])  10.1 us
    unnamed x14, local copies, waits for them, and re-layouts  9.14 us
    pallas_call x3, Pallas kernels, partial_states(): pl.pallas_call(functools.partial(state_kernel, parts), grid_spec=pltpu.Pr...  7.84 us
    dot_general x8, matrix products, layer(): jnp.dot(mixed[-way * (k + 1) % n], weight, preferred_element_type=F32)  5.87 us
    pallas_call x4, Pallas kernels, read_states(): pl.pallas_call(functools.partial(read_kernel, parts, scale), grid_spec=pl...  3.79 us
  transfers between devices with their start and end apart: 37, of which 13 were waited for; matrix products, arithmetic and copies ran while one was open for 9% of the time, Pallas kernels for 9%

profile of v3, /device:TPU:0, one launch (start us, length us, event | category | flops | bytes accessed | tf_op | source)
XLA Modules:
  0.0 145.6 jit_solution(2793591765369960319)
XLA Ops:
  0.9 4.0 %collective-permute-start.22 = (bf16[1,64,8,128]{3,2,1,0:T(8,128)(2,1)S(1)}, bf16[1,64,8,128]{3,2,1,0:T(8,128)(2,1)S(1)}, u32[]{:S(2)}, u32[]{:S(2)}) collective-permute-start(bf16[1,64,8,128]{3,2,1,0:T(8,128)(2,1)S(1)} %constant_dynamic-slice_fusion), channel_id=1, source_target_pairs={{0,24},{8,16},{16,8},{24,0},{1,25},{9,17},{17,9},{25,1},{2,26},{10... | collective-permute-start | bytes 393224 | tf_op jit(solution)/shard_map/ppermute | solution.py:296
  4.9 1.6 %copy-done = bf16[1,256,32,128]{3,2,1,0:T(8,128)(2,1)S(1)} copy-done((bf16[1,256,32,128]{3,2,1,0:T(8,128)(2,1)S(1)}, bf16[1,256,32,128]{3,2,1,0:T(8,128)(2,1)}, u32[]{:S(2)}) %copy-start) | copy-done | bytes 2097176
  6.5 1.6 %copy-done.2 = bf16[1,256,32,128]{3,2,1,0:T(8,128)(2,1)S(1)} copy-done((bf16[1,256,32,128]{3,2,1,0:T(8,128)(2,1)S(1)}, bf16[1,256,32,128]{3,2,1,0:T(8,128)(2,1)}, u32[]{:S(2)}) %copy-start.2) | copy-done | bytes 2097176
  8.7 1.6 %partial_states.5 = bf16[1,4,272,128]{3,2,1,0:T(8,128)(2,1)S(1)} custom-call(s32[4]{0:T(128)S(1)} %copy-done.6, s32[1]{0:T(128)} %bitcast.here.block, s32[1]{0:T(128)} %bitcast.1.place, bf16[1,256,32,128]{3,2,1,0:T(8,128)(2,1)S(1)} %copy-done, bf16[1,256,32,128]{3,2,1,0:T(8,128)(2,1)S(1)} %copy-done.2), custom_call_target="tpu_custom_call" | custom-call | flops 67108864 | bytes 1048576 | tf_op jit(solution)/shard_map/partial_states/pallas_call | solution.py:80
  10.5 1.6 %partial_states.3 = (bf16[1,272,128]{2,1,0:T(8,128)(2,1)S(1)}, bf16[1,272,128]{2,1,0:T(8,128)(2,1)S(1)}, bf16[1,272,128]{2,1,0:T(8,128)(2,1)S(1)}, bf16[1,272,128]{2,1,0:T(8,128)(2,1)S(1)}) custom-call(s32[4]{0:T(128)S(1)} %call_exported.0.table, s32[1]{0:T(128)} %bitcast.here.block, s32[1]{0:T(128)} %bitcast.1.place, ...), custom_call_target="tpu_custom_call" | custom-call | flops 67108864 | bytes 1048576 | tf_op jit(solution)/shard_map/partial_states/pallas_call | solution.py:80
  12.2 2.1 %collective-permute-start = (bf16[1,272,128]{2,1,0:T(8,128)(2,1)S(1)}, bf16[1,272,128]{2,1,0:T(8,128)(2,1)S(1)}, u32[]{:S(2)}, u32[]{:S(2)}) collective-permute-start(bf16[1,272,128]{2,1,0:T(8,128)(2,1)S(1)} %get-tuple-element.16), channel_id=1, source_target_pairs={{0,2},{2,4},{4,6},{6,0},{1,3},{3,5},{5,7},{7,1},{8,10},{10,12},{12... | collective-permute-start | bytes 208904 | tf_op jit(solution)/shard_map/ppermute | solution.py:299
  14.2 2.6 %collective-permute-start.1 = (bf16[1,272,128]{2,1,0:T(8,128)(2,1)S(1)}, bf16[1,272,128]{2,1,0:T(8,128)(2,1)S(1)}, u32[]{:S(2)}, u32[]{:S(2)}) collective-permute-start(bf16[1,272,128]{2,1,0:T(8,128)(2,1)S(1)} %get-tuple-element.17), channel_id=1, source_target_pairs={{0,4},{2,6},{4,0},{6,2},{1,5},{3,7},{5,1},{7,3},{8,12},{10,14},{12... | collective-permute-start | bytes 208904 | tf_op jit(solution)/shard_map/ppermute | solution.py:299
  19.4 2.6 %collective-permute-start.23 = (bf16[1,192,8,128]{3,2,1,0:T(8,128)(2,1)S(1)}, bf16[1,192,8,128]{3,2,1,0:T(8,128)(2,1)S(1)}, u32[]{:S(2)}, u32[]{:S(2)}) collective-permute-start(bf16[1,192,8,128]{3,2,1,0:T(8,128)(2,1)S(1)} %constant_dynamic-slice_fusion.2), channel_id=1, source_target_pairs={{0,24},{8,16},{16,8},{24,0},{1,25},{9,17},{17,9},{25,1},{2,26},{10... | collective-permute-start | bytes 1179656 | tf_op jit(solution)/shard_map/ppermute | solution.py:296
  22.1 2.3 %collective-permute-start.5 = (bf16[1,272,128]{2,1,0:T(8,128)(2,1)S(1)}, bf16[1,272,128]{2,1,0:T(8,128)(2,1)S(1)}, u32[]{:S(2)}, u32[]{:S(2)}) collective-permute-start(bf16[1,272,128]{2,1,0:T(8,128)(2,1)S(1)} %bitcast.21), channel_id=1, source_target_pairs={{0,6},{2,0},{4,2},{6,4},{1,7},{3,1},{5,3},{7,5},{8,14},{10,8},{12,... | collective-permute-start | bytes 208904 | tf_op jit(solution)/shard_map/ppermute | solution.py:299
  25.8 4.5 %partial_states.4 = (bf16[2,272,128]{2,1,0:T(8,128)(2,1)}, bf16[2,272,128]{2,1,0:T(8,128)(2,1)}, bf16[2,272,128]{2,1,0:T(8,128)(2,1)}, bf16[2,272,128]{2,1,0:T(8,128)(2,1)}) custom-call(s32[8]{0:T(128)} %constant.29.clone.table, s32[1]{0:T(128)} %bitcast.here.block, s32[1]{0:T(128)} %bitcast.1.place, bf16[1,256,32,128]{3,2,1,0:T(8,128)(2,1)} %key.5, ...), custom_call_target="tpu_custom_call" | custom-call | flops 134217728 | bytes 2097152 | tf_op jit(solution)/shard_map/partial_states/pallas_call | solution.py:80
  31.7 1.7 %collective-permute-start.7 = (bf16[2,272,128]{2,1,0:T(8,128)(2,1)}, bf16[2,272,128]{2,1,0:T(8,128)(2,1)S(1)}, u32[]{:S(2)}, u32[]{:S(2)}) collective-permute-start(bf16[2,272,128]{2,1,0:T(8,128)(2,1)} %get-tuple-element.21), channel_id=1, source_target_pairs={{0,4},{2,6},{4,0},{6,2},{1,5},{3,7},{5,1},{7,3},{8,12},{10,14},{12... | collective-permute-start | bytes 417800 | tf_op jit(solution)/shard_map/ppermute | solution.py:299
  33.3 2.8 %collective-permute-start.8 = (bf16[2,272,128]{2,1,0:T(8,128)(2,1)}, bf16[2,272,128]{2,1,0:T(8,128)(2,1)S(1)}, u32[]{:S(2)}, u32[]{:S(2)}) collective-permute-start(bf16[2,272,128]{2,1,0:T(8,128)(2,1)} %get-tuple-element.22), channel_id=1, source_target_pairs={{0,6},{2,0},{4,2},{6,4},{1,7},{3,1},{5,3},{7,5},{8,14},{10,8},{12,... | collective-permute-start | bytes 417800 | tf_op jit(solution)/shard_map/ppermute | solution.py:299
  39.0 1.7 %collective-permute-start.18 = (bf16[1,272,128]{2,1,0:T(8,128)(2,1)S(1)}, bf16[1,272,128]{2,1,0:T(8,128)(2,1)S(1)}, u32[]{:S(2)}, u32[]{:S(2)}) collective-permute-start(bf16[1,272,128]{2,1,0:T(8,128)(2,1)S(1)} %get-tuple-element.27), channel_id=1, source_target_pairs={{0,6},{2,0},{4,2},{6,4},{1,7},{3,1},{5,3},{7,5},{8,14},{10,8},{12,... | collective-permute-start | bytes 208904 | tf_op jit(solution)/shard_map/ppermute | solution.py:299
  40.7 2.2 %collective-permute-done.7.refs_2_ = bf16[2,272,128]{2,1,0:T(8,128)(2,1)S(1)} collective-permute-done((bf16[2,272,128]{2,1,0:T(8,128)(2,1)}, bf16[2,272,128]{2,1,0:T(8,128)(2,1)S(1)}, u32[]{:S(2)}, u32[]{:S(2)}) %collective-permute-start.7) | collective-permute-done | bytes 139296 | tf_op jit(solution)/shard_map/ppermute | solution.py:299
  42.9 3.0 %collective-permute-start.17 = (bf16[1,272,128]{2,1,0:T(8,128)(2,1)S(1)}, bf16[1,272,128]{2,1,0:T(8,128)(2,1)S(1)}, u32[]{:S(2)}, u32[]{:S(2)}) collective-permute-start(bf16[1,272,128]{2,1,0:T(8,128)(2,1)S(1)} %get-tuple-element.28), channel_id=1, source_target_pairs={{0,4},{2,6},{4,0},{6,2},{1,5},{3,7},{5,1},{7,3},{8,12},{10,14},{12... | collective-permute-start | bytes 208904 | tf_op jit(solution)/shard_map/ppermute | solution.py:299
  45.9 3.3 %collective-permute-start.16 = (bf16[1,272,128]{2,1,0:T(8,128)(2,1)S(1)}, bf16[1,272,128]{2,1,0:T(8,128)(2,1)S(1)}, u32[]{:S(2)}, u32[]{:S(2)}) collective-permute-start(bf16[1,272,128]{2,1,0:T(8,128)(2,1)S(1)} %get-tuple-element.29), channel_id=1, source_target_pairs={{0,2},{2,4},{4,6},{6,0},{1,3},{3,5},{5,7},{7,1},{8,10},{10,12},{12... | collective-permute-start | bytes 208904 | tf_op jit(solution)/shard_map/ppermute | solution.py:299
  50.3 1.7 %collective-permute-start.9 = (bf16[272,128]{1,0:T(8,128)(2,1)S(1)}, bf16[272,128]{1,0:T(8,128)(2,1)S(1)}, u32[]{:S(2)}, u32[]{:S(2)}) collective-permute-start(bf16[272,128]{1,0:T(8,128)(2,1)S(1)} %get-tuple-element.23), channel_id=1, source_target_pairs={{0,16},{8,0},{16,24},{24,8},{1,17},{9,1},{17,25},{25,9},{2,18},{10... | collective-permute-start | bytes 208904 | tf_op jit(solution)/shard_map/ppermute | solution.py:296
  53.7 2.7 %collective-permute-done.3.refs_1_ = bf16[1,272,128]{2,1,0:T(8,128)(2,1)S(1)} collective-permute-done((bf16[1,272,128]{2,1,0:T(8,128)(2,1)S(1)}, bf16[1,272,128]{2,1,0:T(8,128)(2,1)S(1)}, u32[]{:S(2)}, u32[]{:S(2)}) %collective-permute-start.3) | collective-permute-done | bytes 69664 | tf_op jit(solution)/shard_map/ppermute | solution.py:299
  56.4 1.6 %collective-permute-start.14 = (bf16[1,256,8,128]{3,2,1,0:T(8,128)(2,1)S(1)}, bf16[1,256,8,128]{3,2,1,0:T(8,128)(2,1)S(1)}, u32[]{:S(2)}, u32[]{:S(2)}) collective-permute-start(bf16[1,256,8,128]{3,2,1,0:T(8,128)(2,1)S(1)} %get-tuple-element.26), channel_id=1, source_target_pairs={{0,16},{8,0},{16,24},{24,8},{1,17},{9,1},{17,25},{25,9},{2,18},{10... | collective-permute-start | bytes 1572872 | tf_op jit(solution)/shard_map/ppermute | solution.py:296
  60.6 1.8 %collective-permute-done.21.refs_3_ = bf16[1,272,128]{2,1,0:T(8,128)(2,1)S(1)} collective-permute-done((bf16[1,272,128]{2,1,0:T(8,128)(2,1)S(1)}, bf16[1,272,128]{2,1,0:T(8,128)(2,1)S(1)}, u32[]{:S(2)}, u32[]{:S(2)}) %collective-permute-start.21) | collective-permute-done | bytes 69664 | tf_op jit(solution)/shard_map/ppermute | solution.py:299
  62.4 3.6 %collective-permute-start.13 = (bf16[2,272,128]{2,1,0:T(8,128)(2,1)S(1)}, bf16[2,272,128]{2,1,0:T(8,128)(2,1)S(1)}, u32[]{:S(2)}, u32[]{:S(2)}) collective-permute-start(bf16[2,272,128]{2,1,0:T(8,128)(2,1)S(1)} %pad_maximum_fusion.refs_0_), channel_id=1, source_target_pairs={{0,6},{2,0},{4,2},{6,4},{1,7},{3,1},{5,3},{7,5},{8,14},{10,8},{12,... | collective-permute-start | bytes 417800 | tf_op jit(solution)/shard_map/ppermute | solution.py:299
  66.0 1.6 %collective-permute-done.20.refs_2_ = bf16[1,272,128]{2,1,0:T(8,128)(2,1)S(1)} collective-permute-done((bf16[1,272,128]{2,1,0:T(8,128)(2,1)S(1)}, bf16[1,272,128]{2,1,0:T(8,128)(2,1)S(1)}, u32[]{:S(2)}, u32[]{:S(2)}) %collective-permute-start.20) | collective-permute-done | bytes 69664 | tf_op jit(solution)/shard_map/ppermute | solution.py:299
  68.6 3.4 %copy-done.3 = bf16[1024,4096]{1,0:T(8,128)(2,1)S(1)} copy-done((bf16[1024,4096]{1,0:T(8,128)(2,1)S(1)}, bf16[1024,4096]{1,0:T(8,128)(2,1)}, u32[]{:S(2)}) %copy-start.3) | copy-done | bytes 8388632
  84.8 9.0 %collective-permute-done.34 = bf16[256,1024]{1,0:T(8,128)(2,1)S(1)} collective-permute-done((bf16[256,1024]{1,0:T(8,128)(2,1)S(1)}, bf16[256,1024]{1,0:T(8,128)(2,1)S(1)}, u32[]{:S(2)}, u32[]{:S(2)}) %collective-permute-start.34) | collective-permute-done | bytes 524320 | tf_op jit(solution)/shard_map/ppermute | solution.py:296
  94.6 1.5 %collective-permute-start.35 = (bf16[256,1024]{1,0:T(8,128)(2,1)S(1)}, bf16[256,1024]{1,0:T(8,128)(2,1)S(1)}, u32[]{:S(2)}, u32[]{:S(2)}) collective-permute-start(bf16[256,1024]{1,0:T(8,128)(2,1)S(1)} %fusion.64), channel_id=1, source_target_pairs={{0,16},{8,0},{16,24},{24,8},{1,17},{9,1},{17,25},{25,9},{2,18},{10... | collective-permute-start | bytes 1572872 | tf_op jit(solution)/shard_map/ppermute | solution.py:296
  97.4 7.6 %collective-permute-done.28 = bf16[256,1024]{1,0:T(8,128)(2,1)S(1)} collective-permute-done((bf16[256,1024]{1,0:T(8,128)(2,1)S(1)}, bf16[256,1024]{1,0:T(8,128)(2,1)S(1)}, u32[]{:S(2)}, u32[]{:S(2)}) %collective-permute-start.28) | collective-permute-done | bytes 524320 | tf_op jit(solution)/shard_map/ppermute | solution.py:296
  105.8 1.5 %collective-permute-start.29 = (bf16[256,1024]{1,0:T(8,128)(2,1)S(1)}, bf16[256,1024]{1,0:T(8,128)(2,1)S(1)}, u32[]{:S(2)}, u32[]{:S(2)}) collective-permute-start(bf16[256,1024]{1,0:T(8,128)(2,1)S(1)} %fusion.76), channel_id=1, source_target_pairs={{0,16},{8,0},{16,24},{24,8},{1,17},{9,1},{17,25},{25,9},{2,18},{10... | collective-permute-start | bytes 1572872 | tf_op jit(solution)/shard_map/ppermute | solution.py:296
  108.7 7.6 %collective-permute-done.35 = bf16[256,1024]{1,0:T(8,128)(2,1)S(1)} collective-permute-done((bf16[256,1024]{1,0:T(8,128)(2,1)S(1)}, bf16[256,1024]{1,0:T(8,128)(2,1)S(1)}, u32[]{:S(2)}, u32[]{:S(2)}) %collective-permute-start.35) | collective-permute-done | bytes 524320 | tf_op jit(solution)/shard_map/ppermute | solution.py:296
  117.0 1.5 %collective-permute-start.36 = (bf16[256,1024]{1,0:T(8,128)(2,1)S(1)}, bf16[256,1024]{1,0:T(8,128)(2,1)S(1)}, u32[]{:S(2)}, u32[]{:S(2)}) collective-permute-start(bf16[256,1024]{1,0:T(8,128)(2,1)S(1)} %fusion.67), channel_id=1, source_target_pairs={{0,16},{8,0},{16,24},{24,8},{1,17},{9,1},{17,25},{25,9},{2,18},{10... | collective-permute-start | bytes 1572872 | tf_op jit(solution)/shard_map/ppermute | solution.py:296
  119.9 7.6 %collective-permute-done.29 = bf16[256,1024]{1,0:T(8,128)(2,1)S(1)} collective-permute-done((bf16[256,1024]{1,0:T(8,128)(2,1)S(1)}, bf16[256,1024]{1,0:T(8,128)(2,1)S(1)}, u32[]{:S(2)}, u32[]{:S(2)}) %collective-permute-start.29) | collective-permute-done | bytes 524320 | tf_op jit(solution)/shard_map/ppermute | solution.py:296
  128.3 1.5 %collective-permute-start.30 = (bf16[256,1024]{1,0:T(8,128)(2,1)S(1)}, bf16[256,1024]{1,0:T(8,128)(2,1)S(1)}, u32[]{:S(2)}, u32[]{:S(2)}) collective-permute-start(bf16[256,1024]{1,0:T(8,128)(2,1)S(1)} %fusion.79), channel_id=1, source_target_pairs={{0,16},{8,0},{16,24},{24,8},{1,17},{9,1},{17,25},{25,9},{2,18},{10... | collective-permute-start | bytes 1572872 | tf_op jit(solution)/shard_map/ppermute | solution.py:296
  133.7 8.4 %collective-permute-done.30.refs_1_ = bf16[256,1024]{1,0:T(8,128)(2,1)S(1)} collective-permute-done((bf16[256,1024]{1,0:T(8,128)(2,1)S(1)}, bf16[256,1024]{1,0:T(8,128)(2,1)S(1)}, u32[]{:S(2)}, u32[]{:S(2)}) %collective-permute-start.30) | collective-permute-done | bytes 524320 | tf_op jit(solution)/shard_map/ppermute | solution.py:296
  (89 shorter events, 43.4 us)
Async XLA Ops:
  0.9 29.4 %collective-permute-start.22 = (bf16[1,64,8,128]{3,2,1,0:T(8,128)(2,1)S(1)}, bf16[1,64,8,128]{3,2,1,0:T(8,128)(2,1)S(1)}, u32[]{:S(2)}, u32[]{:S(2)}) collective-permute-start(bf16[1,64,8,128]{3,2,1,0:T(8,128)(2,1)S(1)} %constant_dynamic-slice_fusion), channel_id=1, source_target_pairs={{0,24},{8,16},{16,8},{24,0},{1,25},{9,17},{17,9},{25,1},{2,26},{10... | collective-permute-start | bytes 393224 | tf_op jit(solution)/shard_map/ppermute | solution.py:296
  10.4 25.8 %collective-permute-start.15 = (bf16[4,272,128]{2,1,0:T(8,128)(2,1)S(1)}, bf16[4,272,128]{2,1,0:T(8,128)(2,1)S(1)}, u32[]{:S(2)}, u32[]{:S(2)}) collective-permute-start(bf16[4,272,128]{2,1,0:T(8,128)(2,1)S(1)} %bitcast.31), channel_id=1, source_target_pairs={{0,24},{8,16},{16,8},{24,0},{1,25},{9,17},{17,9},{25,1},{2,26},{10... | collective-permute-start | bytes 835592 | tf_op jit(solution)/shard_map/ppermute | solution.py:296
  12.2 7.3 %collective-permute-start = (bf16[1,272,128]{2,1,0:T(8,128)(2,1)S(1)}, bf16[1,272,128]{2,1,0:T(8,128)(2,1)S(1)}, u32[]{:S(2)}, u32[]{:S(2)}) collective-permute-start(bf16[1,272,128]{2,1,0:T(8,128)(2,1)S(1)} %get-tuple-element.16), channel_id=1, source_target_pairs={{0,2},{2,4},{4,6},{6,0},{1,3},{3,5},{5,7},{7,1},{8,10},{10,12},{12... | collective-permute-start | bytes 208904 | tf_op jit(solution)/shard_map/ppermute | solution.py:299
  14.2 7.8 %collective-permute-start.1 = (bf16[1,272,128]{2,1,0:T(8,128)(2,1)S(1)}, bf16[1,272,128]{2,1,0:T(8,128)(2,1)S(1)}, u32[]{:S(2)}, u32[]{:S(2)}) collective-permute-start(bf16[1,272,128]{2,1,0:T(8,128)(2,1)S(1)} %get-tuple-element.17), channel_id=1, source_target_pairs={{0,4},{2,6},{4,0},{6,2},{1,5},{3,7},{5,1},{7,3},{8,12},{10,14},{12... | collective-permute-start | bytes 208904 | tf_op jit(solution)/shard_map/ppermute | solution.py:299
  19.4 39.7 %collective-permute-start.23 = (bf16[1,192,8,128]{3,2,1,0:T(8,128)(2,1)S(1)}, bf16[1,192,8,128]{3,2,1,0:T(8,128)(2,1)S(1)}, u32[]{:S(2)}, u32[]{:S(2)}) collective-permute-start(bf16[1,192,8,128]{3,2,1,0:T(8,128)(2,1)S(1)} %constant_dynamic-slice_fusion.2), channel_id=1, source_target_pairs={{0,24},{8,16},{16,8},{24,0},{1,25},{9,17},{17,9},{25,1},{2,26},{10... | collective-permute-start | bytes 1179656 | tf_op jit(solution)/shard_map/ppermute | solution.py:296
  22.1 9.6 %collective-permute-start.5 = (bf16[1,272,128]{2,1,0:T(8,128)(2,1)S(1)}, bf16[1,272,128]{2,1,0:T(8,128)(2,1)S(1)}, u32[]{:S(2)}, u32[]{:S(2)}) collective-permute-start(bf16[1,272,128]{2,1,0:T(8,128)(2,1)S(1)} %bitcast.21), channel_id=1, source_target_pairs={{0,6},{2,0},{4,2},{6,4},{1,7},{3,1},{5,3},{7,5},{8,14},{10,8},{12,... | collective-permute-start | bytes 208904 | tf_op jit(solution)/shard_map/ppermute | solution.py:299
  24.4 8.9 %collective-permute-start.4 = (bf16[1,272,128]{2,1,0:T(8,128)(2,1)S(1)}, bf16[1,272,128]{2,1,0:T(8,128)(2,1)S(1)}, u32[]{:S(2)}, u32[]{:S(2)}) collective-permute-start(bf16[1,272,128]{2,1,0:T(8,128)(2,1)S(1)} %bitcast.22), channel_id=1, source_target_pairs={{0,4},{2,6},{4,0},{6,2},{1,5},{3,7},{5,1},{7,3},{8,12},{10,14},{12... | collective-permute-start | bytes 208904 | tf_op jit(solution)/shard_map/ppermute | solution.py:299
  30.3 8.7 %collective-permute-start.6 = (bf16[2,272,128]{2,1,0:T(8,128)(2,1)}, bf16[2,272,128]{2,1,0:T(8,128)(2,1)S(1)}, u32[]{:S(2)}, u32[]{:S(2)}) collective-permute-start(bf16[2,272,128]{2,1,0:T(8,128)(2,1)} %get-tuple-element.20), channel_id=1, source_target_pairs={{0,2},{2,4},{4,6},{6,0},{1,3},{3,5},{5,7},{7,1},{8,10},{10,12},{12... | collective-permute-start | bytes 417800 | tf_op jit(solution)/shard_map/ppermute | solution.py:299
  31.7 11.2 %collective-permute-start.7 = (bf16[2,272,128]{2,1,0:T(8,128)(2,1)}, bf16[2,272,128]{2,1,0:T(8,128)(2,1)S(1)}, u32[]{:S(2)}, u32[]{:S(2)}) collective-permute-start(bf16[2,272,128]{2,1,0:T(8,128)(2,1)} %get-tuple-element.21), channel_id=1, source_target_pairs={{0,4},{2,6},{4,0},{6,2},{1,5},{3,7},{5,1},{7,3},{8,12},{10,14},{12... | collective-permute-start | bytes 417800 | tf_op jit(solution)/shard_map/ppermute | solution.py:299
  33.3 12.6 %collective-permute-start.8 = (bf16[2,272,128]{2,1,0:T(8,128)(2,1)}, bf16[2,272,128]{2,1,0:T(8,128)(2,1)S(1)}, u32[]{:S(2)}, u32[]{:S(2)}) collective-permute-start(bf16[2,272,128]{2,1,0:T(8,128)(2,1)} %get-tuple-element.22), channel_id=1, source_target_pairs={{0,6},{2,0},{4,2},{6,4},{1,7},{3,1},{5,3},{7,5},{8,14},{10,8},{12,... | collective-permute-start | bytes 417800 | tf_op jit(solution)/shard_map/ppermute | solution.py:299
  36.2 39.4 %collective-permute-start.24 = (bf16[1,256,8,128]{3,2,1,0:T(8,128)(2,1)S(1)}, bf16[1,256,8,128]{3,2,1,0:T(8,128)(2,1)S(1)}, u32[]{:S(2)}, u32[]{:S(2)}) collective-permute-start(bf16[1,256,8,128]{3,2,1,0:T(8,128)(2,1)S(1)} %get-tuple-element.25), channel_id=1, source_target_pairs={{0,8},{8,24},{16,0},{24,16},{1,9},{9,25},{17,1},{25,17},{2,10},{10... | collective-permute-start | bytes 1572872 | tf_op jit(solution)/shard_map/ppermute | solution.py:296
  39.0 11.2 %collective-permute-start.18 = (bf16[1,272,128]{2,1,0:T(8,128)(2,1)S(1)}, bf16[1,272,128]{2,1,0:T(8,128)(2,1)S(1)}, u32[]{:S(2)}, u32[]{:S(2)}) collective-permute-start(bf16[1,272,128]{2,1,0:T(8,128)(2,1)S(1)} %get-tuple-element.27), channel_id=1, source_target_pairs={{0,6},{2,0},{4,2},{6,4},{1,7},{3,1},{5,3},{7,5},{8,14},{10,8},{12,... | collective-permute-start | bytes 208904 | tf_op jit(solution)/shard_map/ppermute | solution.py:299
  42.9 7.4 %collective-permute-start.17 = (bf16[1,272,128]{2,1,0:T(8,128)(2,1)S(1)}, bf16[1,272,128]{2,1,0:T(8,128)(2,1)S(1)}, u32[]{:S(2)}, u32[]{:S(2)}) collective-permute-start(bf16[1,272,128]{2,1,0:T(8,128)(2,1)S(1)} %get-tuple-element.28), channel_id=1, source_target_pairs={{0,4},{2,6},{4,0},{6,2},{1,5},{3,7},{5,1},{7,3},{8,12},{10,14},{12... | collective-permute-start | bytes 208904 | tf_op jit(solution)/shard_map/ppermute | solution.py:299
  50.3 7.7 %collective-permute-start.9 = (bf16[272,128]{1,0:T(8,128)(2,1)S(1)}, bf16[272,128]{1,0:T(8,128)(2,1)S(1)}, u32[]{:S(2)}, u32[]{:S(2)}) collective-permute-start(bf16[272,128]{1,0:T(8,128)(2,1)S(1)} %get-tuple-element.23), channel_id=1, source_target_pairs={{0,16},{8,0},{16,24},{24,8},{1,17},{9,1},{17,25},{25,9},{2,18},{10... | collective-permute-start | bytes 208904 | tf_op jit(solution)/shard_map/ppermute | solution.py:296
  56.4 20.9 %collective-permute-start.14 = (bf16[1,256,8,128]{3,2,1,0:T(8,128)(2,1)S(1)}, bf16[1,256,8,128]{3,2,1,0:T(8,128)(2,1)S(1)}, u32[]{:S(2)}, u32[]{:S(2)}) collective-permute-start(bf16[1,256,8,128]{3,2,1,0:T(8,128)(2,1)S(1)} %get-tuple-element.26), channel_id=1, source_target_pairs={{0,16},{8,0},{16,24},{24,8},{1,17},{9,1},{17,25},{25,9},{2,18},{10... | collective-permute-start | bytes 1572872 | tf_op jit(solution)/shard_map/ppermute | solution.py:296
  59.2 8.4 %collective-permute-start.20 = (bf16[1,272,128]{2,1,0:T(8,128)(2,1)S(1)}, bf16[1,272,128]{2,1,0:T(8,128)(2,1)S(1)}, u32[]{:S(2)}, u32[]{:S(2)}) collective-permute-start(bf16[1,272,128]{2,1,0:T(8,128)(2,1)S(1)} %bitcast.26), channel_id=1, source_target_pairs={{0,4},{2,6},{4,0},{6,2},{1,5},{3,7},{5,1},{7,3},{8,12},{10,14},{12... | collective-permute-start | bytes 208904 | tf_op jit(solution)/shard_map/ppermute | solution.py:299
  59.2 8.4 %collective-permute-start.19 = (bf16[1,272,128]{2,1,0:T(8,128)(2,1)S(1)}, bf16[1,272,128]{2,1,0:T(8,128)(2,1)S(1)}, u32[]{:S(2)}, u32[]{:S(2)}) collective-permute-start(bf16[1,272,128]{2,1,0:T(8,128)(2,1)S(1)} %bitcast.27), channel_id=1, source_target_pairs={{0,2},{2,4},{4,6},{6,0},{1,3},{3,5},{5,7},{7,1},{8,10},{10,12},{12... | collective-permute-start | bytes 208904 | tf_op jit(solution)/shard_map/ppermute | solution.py:299
  62.4 13.1 %collective-permute-start.13 = (bf16[2,272,128]{2,1,0:T(8,128)(2,1)S(1)}, bf16[2,272,128]{2,1,0:T(8,128)(2,1)S(1)}, u32[]{:S(2)}, u32[]{:S(2)}) collective-permute-start(bf16[2,272,128]{2,1,0:T(8,128)(2,1)S(1)} %pad_maximum_fusion.refs_0_), channel_id=1, source_target_pairs={{0,6},{2,0},{4,2},{6,4},{1,7},{3,1},{5,3},{7,5},{8,14},{10,8},{12,... | collective-permute-start | bytes 417800 | tf_op jit(solution)/shard_map/ppermute | solution.py:299
  67.6 8.0 %collective-permute-start.12 = (bf16[2,272,128]{2,1,0:T(8,128)(2,1)S(1)}, bf16[2,272,128]{2,1,0:T(8,128)(2,1)S(1)}, u32[]{:S(2)}, u32[]{:S(2)}) collective-permute-start(bf16[2,272,128]{2,1,0:T(8,128)(2,1)S(1)} %pad_maximum_fusion.refs_0_), channel_id=1, source_target_pairs={{0,4},{2,6},{4,0},{6,2},{1,5},{3,7},{5,1},{7,3},{8,12},{10,14},{12... | collective-permute-start | bytes 417800 | tf_op jit(solution)/shard_map/ppermute | solution.py:299
  67.6 8.0 %collective-permute-start.11 = (bf16[2,272,128]{2,1,0:T(8,128)(2,1)S(1)}, bf16[2,272,128]{2,1,0:T(8,128)(2,1)S(1)}, u32[]{:S(2)}, u32[]{:S(2)}) collective-permute-start(bf16[2,272,128]{2,1,0:T(8,128)(2,1)S(1)} %pad_maximum_fusion.refs_0_), channel_id=1, source_target_pairs={{0,2},{2,4},{4,6},{6,0},{1,3},{3,5},{5,7},{7,1},{8,10},{10,12},{12... | collective-permute-start | bytes 417800 | tf_op jit(solution)/shard_map/ppermute | solution.py:299
  79.0 14.8 %collective-permute-start.34 = (bf16[256,1024]{1,0:T(8,128)(2,1)S(1)}, bf16[256,1024]{1,0:T(8,128)(2,1)S(1)}, u32[]{:S(2)}, u32[]{:S(2)}) collective-permute-start(bf16[256,1024]{1,0:T(8,128)(2,1)S(1)} %fusion.61), channel_id=1, source_target_pairs={{0,16},{8,0},{16,24},{24,8},{1,17},{9,1},{17,25},{25,9},{2,18},{10... | collective-permute-start | bytes 1572872 | tf_op jit(solution)/shard_map/ppermute | solution.py:296
  80.5 15.6 %collective-permute-start.31 = (bf16[256,1024]{1,0:T(8,128)(2,1)S(1)}, bf16[256,1024]{1,0:T(8,128)(2,1)S(1)}, u32[]{:S(2)}, u32[]{:S(2)}) collective-permute-start(bf16[256,1024]{1,0:T(8,128)(2,1)S(1)} %fusion.58), channel_id=1, source_target_pairs={{0,8},{8,24},{16,0},{24,16},{1,9},{9,25},{17,1},{25,17},{2,10},{10... | collective-permute-start | bytes 1572872 | tf_op jit(solution)/shard_map/ppermute | solution.py:296
  81.8 23.3 %collective-permute-start.28 = (bf16[256,1024]{1,0:T(8,128)(2,1)S(1)}, bf16[256,1024]{1,0:T(8,128)(2,1)S(1)}, u32[]{:S(2)}, u32[]{:S(2)}) collective-permute-start(bf16[256,1024]{1,0:T(8,128)(2,1)S(1)} %fusion.55), channel_id=1, source_target_pairs={{0,16},{8,0},{16,24},{24,8},{1,17},{9,1},{17,25},{25,9},{2,18},{10... | collective-permute-start | bytes 1572872 | tf_op jit(solution)/shard_map/ppermute | solution.py:296
  84.0 23.3 %collective-permute-start.25 = (bf16[256,1024]{1,0:T(8,128)(2,1)S(1)}, bf16[256,1024]{1,0:T(8,128)(2,1)S(1)}, u32[]{:S(2)}, u32[]{:S(2)}) collective-permute-start(bf16[256,1024]{1,0:T(8,128)(2,1)S(1)} %fusion.52), channel_id=1, source_target_pairs={{0,8},{8,24},{16,0},{24,16},{1,9},{9,25},{17,1},{25,17},{2,10},{10... | collective-permute-start | bytes 1572872 | tf_op jit(solution)/shard_map/ppermute | solution.py:296
  94.6 21.7 %collective-permute-start.35 = (bf16[256,1024]{1,0:T(8,128)(2,1)S(1)}, bf16[256,1024]{1,0:T(8,128)(2,1)S(1)}, u32[]{:S(2)}, u32[]{:S(2)}) collective-permute-start(bf16[256,1024]{1,0:T(8,128)(2,1)S(1)} %fusion.64), channel_id=1, source_target_pairs={{0,16},{8,0},{16,24},{24,8},{1,17},{9,1},{17,25},{25,9},{2,18},{10... | collective-permute-start | bytes 1572872 | tf_op jit(solution)/shard_map/ppermute | solution.py:296
  96.8 21.7 %collective-permute-start.32 = (bf16[256,1024]{1,0:T(8,128)(2,1)S(1)}, bf16[256,1024]{1,0:T(8,128)(2,1)S(1)}, u32[]{:S(2)}, u32[]{:S(2)}) collective-permute-start(bf16[256,1024]{1,0:T(8,128)(2,1)S(1)} %fusion.70), channel_id=1, source_target_pairs={{0,8},{8,24},{16,0},{24,16},{1,9},{9,25},{17,1},{25,17},{2,10},{10... | collective-permute-start | bytes 1572872 | tf_op jit(solution)/shard_map/ppermute | solution.py:296
  105.8 21.7 %collective-permute-start.29 = (bf16[256,1024]{1,0:T(8,128)(2,1)S(1)}, bf16[256,1024]{1,0:T(8,128)(2,1)S(1)}, u32[]{:S(2)}, u32[]{:S(2)}) collective-permute-start(bf16[256,1024]{1,0:T(8,128)(2,1)S(1)} %fusion.76), channel_id=1, source_target_pairs={{0,16},{8,0},{16,24},{24,8},{1,17},{9,1},{17,25},{25,9},{2,18},{10... | collective-permute-start | bytes 1572872 | tf_op jit(solution)/shard_map/ppermute | solution.py:296
  108.1 21.7 %collective-permute-start.26 = (bf16[256,1024]{1,0:T(8,128)(2,1)S(1)}, bf16[256,1024]{1,0:T(8,128)(2,1)S(1)}, u32[]{:S(2)}, u32[]{:S(2)}) collective-permute-start(bf16[256,1024]{1,0:T(8,128)(2,1)S(1)} %fusion.82), channel_id=1, source_target_pairs={{0,8},{8,24},{16,0},{24,16},{1,9},{9,25},{17,1},{25,17},{2,10},{10... | collective-permute-start | bytes 1572872 | tf_op jit(solution)/shard_map/ppermute | solution.py:296
  117.0 27.4 %collective-permute-start.36 = (bf16[256,1024]{1,0:T(8,128)(2,1)S(1)}, bf16[256,1024]{1,0:T(8,128)(2,1)S(1)}, u32[]{:S(2)}, u32[]{:S(2)}) collective-permute-start(bf16[256,1024]{1,0:T(8,128)(2,1)S(1)} %fusion.67), channel_id=1, source_target_pairs={{0,16},{8,0},{16,24},{24,8},{1,17},{9,1},{17,25},{25,9},{2,18},{10... | collective-permute-start | bytes 1572872 | tf_op jit(solution)/shard_map/ppermute | solution.py:296
  119.3 25.2 %collective-permute-start.33 = (bf16[256,1024]{1,0:T(8,128)(2,1)S(1)}, bf16[256,1024]{1,0:T(8,128)(2,1)S(1)}, u32[]{:S(2)}, u32[]{:S(2)}) collective-permute-start(bf16[256,1024]{1,0:T(8,128)(2,1)S(1)} %fusion.73), channel_id=1, source_target_pairs={{0,8},{8,24},{16,0},{24,16},{1,9},{9,25},{17,1},{25,17},{2,10},{10... | collective-permute-start | bytes 1572872 | tf_op jit(solution)/shard_map/ppermute | solution.py:296
  128.3 13.8 %collective-permute-start.30 = (bf16[256,1024]{1,0:T(8,128)(2,1)S(1)}, bf16[256,1024]{1,0:T(8,128)(2,1)S(1)}, u32[]{:S(2)}, u32[]{:S(2)}) collective-permute-start(bf16[256,1024]{1,0:T(8,128)(2,1)S(1)} %fusion.79), channel_id=1, source_target_pairs={{0,16},{8,0},{16,24},{24,8},{1,17},{9,1},{17,25},{25,9},{2,18},{10... | collective-permute-start | bytes 1572872 | tf_op jit(solution)/shard_map/ppermute | solution.py:296
  130.5 12.8 %collective-permute-start.27 = (bf16[256,1024]{1,0:T(8,128)(2,1)S(1)}, bf16[256,1024]{1,0:T(8,128)(2,1)S(1)}, u32[]{:S(2)}, u32[]{:S(2)}) collective-permute-start(bf16[256,1024]{1,0:T(8,128)(2,1)S(1)} %fusion.85), channel_id=1, source_target_pairs={{0,8},{8,24},{16,0},{24,16},{1,9},{9,25},{17,1},{25,17},{2,10},{10... | collective-permute-start | bytes 1572872 | tf_op jit(solution)/shard_map/ppermute | solution.py:296
  (12 other events, 40.5 us)

commit v4 on v3

--- a/solution.py
+++ b/solution.py
@@ -161,7 +161,7 @@
             num_scalar_prefetch=2,
             grid=(1,),
             in_specs=[pl.BlockSpec((2 * heads, size), lambda i, b, p: (rows // (2 * heads) - 1, 0))]
-            + [pl.BlockSpec((1, rows, size), lambda i, b, p: (slot, 0, 0))] * parts
+            + [pl.BlockSpec((1, pieces[0].shape[1], size), lambda i, b, p: (slot, 0, 0))] * parts
             + [
                 pl.BlockSpec((1, query.shape[1], heads, size), lambda i, b, p: (0, 0, b[0], 0))
                 for query in queries
@@ -256,7 +256,7 @@
     tokens, _, size = query.shape
     query = lax.dynamic_slice_in_dim(query, block[0] * heads, heads, 1)
     mass = own[-2 * heads :].astype(F32)
-    stack = jnp.stack([piece[slot, : -2 * heads] for piece in pieces])
+    stack = jnp.stack([piece[slot, : heads * size // parts] for piece in pieces])
     order = lax.rem(place[0] + parts - jnp.arange(parts), parts)
     state = stack[order].reshape(heads, size, size)
     feature = feature_map(query)
@@ -322,7 +322,7 @@
         owns = list(make_total(take, heads, count))
         if g == 0:
             owns = [around(own, o) if o else own for own, o in zip(owns, group)]
-        stack = jnp.stack(owns) if len(owns) > 1 else owns[0][None]
+        stack = jnp.stack([own[: -2 * heads] for own in owns]) if group[0] else owns[0][None]
         pieces = [stack] + [along(stack, j) for j in range(1, parts)]
         for i, o in enumerate(group):
             slot = -o % n

time: 146 us -> 171 us (1.17)
  waiting for transfers between devices: 51.5 us -> 83.1 us
  local copies, waits for them, and re-layouts: 12.4 us -> 7.8 us
  starting transfers between devices: 55.3 us -> 53 us
    ppermute x19, waiting for transfers between devices: 41.5 us -> 65.1 us  [around(): return lax.ppermute(x, 'dp', [(d, to[d][offset % n]) for d in range(n)])]
    ppermute x18, waiting for transfers between devices: 10.1 us -> 18 us  [along(): lax.ppermute(x, 'sp', [(i, (i + offset) % parts) for i in range(parts)])]
    ppermute x19, starting transfers between devices: 25.8 us -> 21.1 us  [around(): return lax.ppermute(x, 'dp', [(d, to[d][offset % n]) for d in range(n)])]
    unnamed x14 -> x18, local copies, waits for them, and re-layouts: 9.14 us -> 6.59 us
    ppermute x18, starting transfers between devices: 29.5 us -> 32 us  [along(): lax.ppermute(x, 'sp', [(i, (i + offset) % parts) for i in range(parts)])]
    split x2, local copies, waits for them, and re-layouts: 1.93 us -> 0.07 us  [layer(): cuts = jnp.split(piece, halves, axis=1)]
  transfers between devices with their start and end apart: 37 -> 37, of which waited for: 13 -> 15; matrix products, arithmetic and copies ran while one was open for 9% -> 7% of each run, Pallas kernels for 9% -> 6%
where the time goes in v4:
time: 171 us; the launch traced here: 170 us
  waiting for transfers between devices  83.1 us (49%)
  starting transfers between devices  53 us (31%)
  Pallas kernels  14.8 us (9%)
  matrix products  11.3 us (7%)
  local copies, waits for them, and re-layouts  7.8 us (5%)
    ppermute x19, waiting for transfers between devices, around(): return lax.ppermute(x, 'dp', [(d, to[d][offset % n]) for d in range(n)])  65.1 us
    ppermute x18, starting transfers between devices, along(): lax.ppermute(x, 'sp', [(i, (i + offset) % parts) for i in range(parts)])  32 us
    ppermute x19, starting transfers between devices, around(): return lax.ppermute(x, 'dp', [(d, to[d][offset % n]) for d in range(n)])  21.1 us
    ppermute x18, waiting for transfers between devices, along(): lax.ppermute(x, 'sp', [(i, (i + offset) % parts) for i in range(parts)])  18 us
    pallas_call x3, Pallas kernels, partial_states(): pl.pallas_call(functools.partial(state_kernel, parts), grid_spec=pltpu.Pr...  7.84 us
    unnamed x18, local copies, waits for them, and re-layouts  6.59 us
    dot_general x8, matrix products, layer(): jnp.dot(mixed[-way * (k + 1) % n], weight, preferred_element_type=F32)  5.85 us
    pallas_call x4, Pallas kernels, read_states(): pl.pallas_call(functools.partial(read_kernel, parts, scale), grid_spec=pl...  3.79 us
  transfers between devices with their start and end apart: 37, of which 15 were waited for; matrix products, arithmetic and copies ran while one was open for 7% of the time, Pallas kernels for 6%

profile of v4, /device:TPU:0, one launch (start us, length us, event | category | flops | bytes accessed | tf_op | source)
XLA Modules:
  0.0 170.3 jit_solution(4859151317780742428)
XLA Ops:
  0.0 1.6 copy-done
  3.2 1.6 partial_states.3
  4.8 3.1 %collective-permute-start = (bf16[1,272,128]{2,1,0:T(8,128)(2,1)S(1)}, bf16[1,272,128]{2,1,0:T(8,128)(2,1)S(1)}, u32[]{:S(2)}, u32[]{:S(2)}) collective-permute-start(bf16[1,272,128]{2,1,0:T(8,128)(2,1)S(1)} %get-tuple-element.16), channel_id=1, source_target_pairs={{0,2},{2,4},{4,6},{6,0},{1,3},{3,5},{5,7},{7,1},{8,10},{10,12},{12... | collective-permute-start | bytes 208904 | tf_op jit(solution)/shard_map/ppermute | solution.py:299
  7.9 2.6 %collective-permute-start.1 = (bf16[1,272,128]{2,1,0:T(8,128)(2,1)S(1)}, bf16[1,272,128]{2,1,0:T(8,128)(2,1)S(1)}, u32[]{:S(2)}, u32[]{:S(2)}) collective-permute-start(bf16[1,272,128]{2,1,0:T(8,128)(2,1)S(1)} %get-tuple-element.17), channel_id=1, source_target_pairs={{0,4},{2,6},{4,0},{6,2},{1,5},{3,7},{5,1},{7,3},{8,12},{10,14},{12... | collective-permute-start | bytes 208904 | tf_op jit(solution)/shard_map/ppermute | solution.py:299
  10.5 1.7 partial_states.5
  12.2 2.5 %collective-permute-start.15 = (bf16[4,272,128]{2,1,0:T(8,128)(2,1)S(1)}, bf16[4,272,128]{2,1,0:T(8,128)(2,1)S(1)}, u32[]{:S(2)}, u32[]{:S(2)}) collective-permute-start(bf16[4,272,128]{2,1,0:T(8,128)(2,1)S(1)} %bitcast.28), channel_id=1, source_target_pairs={{0,24},{8,16},{16,8},{24,0},{1,25},{9,17},{17,9},{25,1},{2,26},{10... | collective-permute-start | bytes 835592 | tf_op jit(solution)/shard_map/ppermute | solution.py:296
  14.7 4.6 %partial_states.4 = (bf16[2,272,128]{2,1,0:T(8,128)(2,1)}, bf16[2,272,128]{2,1,0:T(8,128)(2,1)}, bf16[2,272,128]{2,1,0:T(8,128)(2,1)}, bf16[2,272,128]{2,1,0:T(8,128)(2,1)}) custom-call(s32[8]{0:T(128)} %constant.29.clone.table, s32[1]{0:T(128)} %bitcast.here.block, s32[1]{0:T(128)} %bitcast.1.place, bf16[1,256,32,128]{3,2,1,0:T(8,128)(2,1)} %key.5, ...), custom_call_target="tpu_custom_call" | custom-call | flops 134217728 | bytes 2097152 | tf_op jit(solution)/shard_map/partial_states/pallas_call | solution.py:80
  19.5 1.7 collective-permute-start.7
  22.3 1.9 %collective-permute-start.8 = (bf16[2,272,128]{2,1,0:T(8,128)(2,1)}, bf16[2,272,128]{2,1,0:T(8,128)(2,1)S(1)}, u32[]{:S(2)}, u32[]{:S(2)}) collective-permute-start(bf16[2,272,128]{2,1,0:T(8,128)(2,1)} %get-tuple-element.22), channel_id=1, source_target_pairs={{0,6},{2,0},{4,2},{6,4},{1,7},{3,1},{5,3},{7,5},{8,14},{10,8},{12,... | collective-permute-start | bytes 417800 | tf_op jit(solution)/shard_map/ppermute | solution.py:299
  25.2 7.4 %collective-permute-done.2.refs_3_ = bf16[1,272,128]{2,1,0:T(8,128)(2,1)S(1)} collective-permute-done((bf16[1,272,128]{2,1,0:T(8,128)(2,1)S(1)}, bf16[1,272,128]{2,1,0:T(8,128)(2,1)S(1)}, u32[]{:S(2)}, u32[]{:S(2)}) %collective-permute-start.2) | collective-permute-done | bytes 69664 | tf_op jit(solution)/shard_map/ppermute | solution.py:299
  33.2 2.4 %collective-permute-start.23 = (bf16[1,192,8,128]{3,2,1,0:T(8,128)(2,1)S(1)}, bf16[1,192,8,128]{3,2,1,0:T(8,128)(2,1)S(1)}, u32[]{:S(2)}, u32[]{:S(2)}) collective-permute-start(bf16[1,192,8,128]{3,2,1,0:T(8,128)(2,1)S(1)} %constant_dynamic-slice_fusion.2), channel_id=1, source_target_pairs={{0,24},{8,16},{16,8},{24,0},{1,25},{9,17},{17,9},{25,1},{2,26},{10... | collective-permute-start | bytes 1179656 | tf_op jit(solution)/shard_map/ppermute | solution.py:296
  38.3 7.8 %collective-permute-done.9.mass = bf16[272,128]{1,0:T(8,128)(2,1)S(1)} collective-permute-done((bf16[272,128]{1,0:T(8,128)(2,1)S(1)}, bf16[272,128]{1,0:T(8,128)(2,1)S(1)}, u32[]{:S(2)}, u32[]{:S(2)}) %collective-permute-start.9) | collective-permute-done | bytes 69664 | tf_op jit(solution)/shard_map/ppermute | solution.py:296
  47.5 10.8 %collective-permute-done.10.mass = bf16[272,128]{1,0:T(8,128)(2,1)S(1)} collective-permute-done((bf16[272,128]{1,0:T(8,128)(2,1)S(1)}, bf16[272,128]{1,0:T(8,128)(2,1)S(1)}, u32[]{:S(2)}, u32[]{:S(2)}) %collective-permute-start.10) | collective-permute-done | bytes 69664 | tf_op jit(solution)/shard_map/ppermute | solution.py:296
  58.3 3.5 %collective-permute-start.17 = (bf16[1,272,128]{2,1,0:T(8,128)(2,1)S(1)}, bf16[1,272,128]{2,1,0:T(8,128)(2,1)S(1)}, u32[]{:S(2)}, u32[]{:S(2)}) collective-permute-start(bf16[1,272,128]{2,1,0:T(8,128)(2,1)S(1)} %get-tuple-element.28), channel_id=1, source_target_pairs={{0,4},{2,6},{4,0},{6,2},{1,5},{3,7},{5,1},{7,3},{8,12},{10,14},{12... | collective-permute-start | bytes 208904 | tf_op jit(solution)/shard_map/ppermute | solution.py:299
  64.2 5.0 %collective-permute-start.5 = (bf16[1,272,128]{2,1,0:T(8,128)(2,1)S(1)}, bf16[1,272,128]{2,1,0:T(8,128)(2,1)S(1)}, u32[]{:S(2)}, u32[]{:S(2)}) collective-permute-start(bf16[1,272,128]{2,1,0:T(8,128)(2,1)S(1)} %bitcast.24), channel_id=1, source_target_pairs={{0,6},{2,0},{4,2},{6,4},{1,7},{3,1},{5,3},{7,5},{8,14},{10,8},{12,... | collective-permute-start | bytes 208904 | tf_op jit(solution)/shard_map/ppermute | solution.py:299
  71.9 3.4 %collective-permute-done.4.refs_2_ = bf16[1,272,128]{2,1,0:T(8,128)(2,1)S(1)} collective-permute-done((bf16[1,272,128]{2,1,0:T(8,128)(2,1)S(1)}, bf16[1,272,128]{2,1,0:T(8,128)(2,1)S(1)}, u32[]{:S(2)}, u32[]{:S(2)}) %collective-permute-start.4) | collective-permute-done | bytes 69664 | tf_op jit(solution)/shard_map/ppermute | solution.py:299
  75.3 2.4 %collective-permute-start.21 = (bf16[1,256,128]{2,1,0:T(8,128)(2,1)S(1)}, bf16[1,256,128]{2,1,0:T(8,128)(2,1)S(1)}, u32[]{:S(2)}, u32[]{:S(2)}) collective-permute-start(bf16[1,256,128]{2,1,0:T(8,128)(2,1)S(1)} %slice_bitcast_fusion.refs_0_), channel_id=1, source_target_pairs={{0,6},{2,0},{4,2},{6,4},{1,7},{3,1},{5,3},{7,5},{8,14},{10,8},{12,... | collective-permute-start | bytes 196616 | tf_op jit(solution)/shard_map/ppermute | solution.py:299
  79.9 4.4 %collective-permute-start.13 = (bf16[2,256,128]{2,1,0:T(8,128)(2,1)S(1)}, bf16[2,256,128]{2,1,0:T(8,128)(2,1)S(1)}, u32[]{:S(2)}, u32[]{:S(2)}) collective-permute-start(bf16[2,256,128]{2,1,0:T(8,128)(2,1)S(1)} %pad_maximum_fusion.refs_0_), channel_id=1, source_target_pairs={{0,6},{2,0},{4,2},{6,4},{1,7},{3,1},{5,3},{7,5},{8,14},{10,8},{12,... | collective-permute-start | bytes 393224 | tf_op jit(solution)/shard_map/ppermute | solution.py:299
  84.9 2.1 %collective-permute-start.11 = (bf16[2,256,128]{2,1,0:T(8,128)(2,1)S(1)}, bf16[2,256,128]{2,1,0:T(8,128)(2,1)S(1)}, u32[]{:S(2)}, u32[]{:S(2)}) collective-permute-start(bf16[2,256,128]{2,1,0:T(8,128)(2,1)S(1)} %pad_maximum_fusion.refs_0_), channel_id=1, source_target_pairs={{0,2},{2,4},{4,6},{6,0},{1,3},{3,5},{5,7},{7,1},{8,10},{10,12},{12... | collective-permute-start | bytes 393224 | tf_op jit(solution)/shard_map/ppermute | solution.py:299
  87.0 3.4 %copy-done.4 = bf16[1024,4096]{1,0:T(8,128)(2,1)S(1)} copy-done((bf16[1024,4096]{1,0:T(8,128)(2,1)S(1)}, bf16[1024,4096]{1,0:T(8,128)(2,1)}, u32[]{:S(2)}) %copy-start.4) | copy-done | bytes 8388632
  92.9 2.4 %collective-permute-done.12.refs_2_ = bf16[2,256,128]{2,1,0:T(8,128)(2,1)S(1)} collective-permute-done((bf16[2,256,128]{2,1,0:T(8,128)(2,1)S(1)}, bf16[2,256,128]{2,1,0:T(8,128)(2,1)S(1)}, u32[]{:S(2)}, u32[]{:S(2)}) %collective-permute-start.12) | collective-permute-done | bytes 131104 | tf_op jit(solution)/shard_map/ppermute | solution.py:299
  98.7 2.0 %collective-permute-start.31 = (bf16[256,1024]{1,0:T(8,128)(2,1)S(1)}, bf16[256,1024]{1,0:T(8,128)(2,1)S(1)}, u32[]{:S(2)}, u32[]{:S(2)}) collective-permute-start(bf16[256,1024]{1,0:T(8,128)(2,1)S(1)} %fusion.58), channel_id=1, source_target_pairs={{0,8},{8,24},{16,0},{24,16},{1,9},{9,25},{17,1},{25,17},{2,10},{10... | collective-permute-start | bytes 1572872 | tf_op jit(solution)/shard_map/ppermute | solution.py:296
  102.3 2.2 %collective-permute-start.25 = (bf16[256,1024]{1,0:T(8,128)(2,1)S(1)}, bf16[256,1024]{1,0:T(8,128)(2,1)S(1)}, u32[]{:S(2)}, u32[]{:S(2)}) collective-permute-start(bf16[256,1024]{1,0:T(8,128)(2,1)S(1)} %fusion.52), channel_id=1, source_target_pairs={{0,8},{8,24},{16,0},{24,16},{1,9},{9,25},{17,1},{25,17},{2,10},{10... | collective-permute-start | bytes 1572872 | tf_op jit(solution)/shard_map/ppermute | solution.py:296
  104.5 9.0 %collective-permute-done.34 = bf16[256,1024]{1,0:T(8,128)(2,1)S(1)} collective-permute-done((bf16[256,1024]{1,0:T(8,128)(2,1)S(1)}, bf16[256,1024]{1,0:T(8,128)(2,1)S(1)}, u32[]{:S(2)}, u32[]{:S(2)}) %collective-permute-start.34) | collective-permute-done | bytes 524320 | tf_op jit(solution)/shard_map/ppermute | solution.py:296
  115.0 2.1 %collective-permute-start.32 = (bf16[256,1024]{1,0:T(8,128)(2,1)S(1)}, bf16[256,1024]{1,0:T(8,128)(2,1)S(1)}, u32[]{:S(2)}, u32[]{:S(2)}) collective-permute-start(bf16[256,1024]{1,0:T(8,128)(2,1)S(1)} %fusion.70), channel_id=1, source_target_pairs={{0,8},{8,24},{16,0},{24,16},{1,9},{9,25},{17,1},{25,17},{2,10},{10... | collective-permute-start | bytes 1572872 | tf_op jit(solution)/shard_map/ppermute | solution.py:296
  117.1 7.6 %collective-permute-done.28 = bf16[256,1024]{1,0:T(8,128)(2,1)S(1)} collective-permute-done((bf16[256,1024]{1,0:T(8,128)(2,1)S(1)}, bf16[256,1024]{1,0:T(8,128)(2,1)S(1)}, u32[]{:S(2)}, u32[]{:S(2)}) %collective-permute-start.28) | collective-permute-done | bytes 524320 | tf_op jit(solution)/shard_map/ppermute | solution.py:296
  126.3 2.1 %collective-permute-start.26 = (bf16[256,1024]{1,0:T(8,128)(2,1)S(1)}, bf16[256,1024]{1,0:T(8,128)(2,1)S(1)}, u32[]{:S(2)}, u32[]{:S(2)}) collective-permute-start(bf16[256,1024]{1,0:T(8,128)(2,1)S(1)} %fusion.82), channel_id=1, source_target_pairs={{0,8},{8,24},{16,0},{24,16},{1,9},{9,25},{17,1},{25,17},{2,10},{10... | collective-permute-start | bytes 1572872 | tf_op jit(solution)/shard_map/ppermute | solution.py:296
  128.3 7.6 %collective-permute-done.35 = bf16[256,1024]{1,0:T(8,128)(2,1)S(1)} collective-permute-done((bf16[256,1024]{1,0:T(8,128)(2,1)S(1)}, bf16[256,1024]{1,0:T(8,128)(2,1)S(1)}, u32[]{:S(2)}, u32[]{:S(2)}) %collective-permute-start.35) | collective-permute-done | bytes 524320 | tf_op jit(solution)/shard_map/ppermute | solution.py:296
  137.5 2.1 %collective-permute-start.33 = (bf16[256,1024]{1,0:T(8,128)(2,1)S(1)}, bf16[256,1024]{1,0:T(8,128)(2,1)S(1)}, u32[]{:S(2)}, u32[]{:S(2)}) collective-permute-start(bf16[256,1024]{1,0:T(8,128)(2,1)S(1)} %fusion.73), channel_id=1, source_target_pairs={{0,8},{8,24},{16,0},{24,16},{1,9},{9,25},{17,1},{25,17},{2,10},{10... | collective-permute-start | bytes 1572872 | tf_op jit(solution)/shard_map/ppermute | solution.py:296
  139.5 7.6 %collective-permute-done.29 = bf16[256,1024]{1,0:T(8,128)(2,1)S(1)} collective-permute-done((bf16[256,1024]{1,0:T(8,128)(2,1)S(1)}, bf16[256,1024]{1,0:T(8,128)(2,1)S(1)}, u32[]{:S(2)}, u32[]{:S(2)}) %collective-permute-start.29) | collective-permute-done | bytes 524320 | tf_op jit(solution)/shard_map/ppermute | solution.py:296
  148.7 2.1 %collective-permute-start.27 = (bf16[256,1024]{1,0:T(8,128)(2,1)S(1)}, bf16[256,1024]{1,0:T(8,128)(2,1)S(1)}, u32[]{:S(2)}, u32[]{:S(2)}) collective-permute-start(bf16[256,1024]{1,0:T(8,128)(2,1)S(1)} %fusion.85), channel_id=1, source_target_pairs={{0,8},{8,24},{16,0},{24,16},{1,9},{9,25},{17,1},{25,17},{2,10},{10... | collective-permute-start | bytes 1572872 | tf_op jit(solution)/shard_map/ppermute | solution.py:296
  153.3 14.6 %collective-permute-done.30.refs_1_ = bf16[256,1024]{1,0:T(8,128)(2,1)S(1)} collective-permute-done((bf16[256,1024]{1,0:T(8,128)(2,1)S(1)}, bf16[256,1024]{1,0:T(8,128)(2,1)S(1)}, u32[]{:S(2)}, u32[]{:S(2)}) %collective-permute-start.30) | collective-permute-done | bytes 524320 | tf_op jit(solution)/shard_map/ppermute | solution.py:296
  (96 shorter events, 35.1 us)
Async XLA Ops:
  4.8 17.5 %collective-permute-start = (bf16[1,272,128]{2,1,0:T(8,128)(2,1)S(1)}, bf16[1,272,128]{2,1,0:T(8,128)(2,1)S(1)}, u32[]{:S(2)}, u32[]{:S(2)}) collective-permute-start(bf16[1,272,128]{2,1,0:T(8,128)(2,1)S(1)} %get-tuple-element.16), channel_id=1, source_target_pairs={{0,2},{2,4},{4,6},{6,0},{1,3},{3,5},{5,7},{7,1},{8,10},{10,12},{12... | collective-permute-start | bytes 208904 | tf_op jit(solution)/shard_map/ppermute | solution.py:299
  7.9 16.4 %collective-permute-start.1 = (bf16[1,272,128]{2,1,0:T(8,128)(2,1)S(1)}, bf16[1,272,128]{2,1,0:T(8,128)(2,1)S(1)}, u32[]{:S(2)}, u32[]{:S(2)}) collective-permute-start(bf16[1,272,128]{2,1,0:T(8,128)(2,1)S(1)} %get-tuple-element.17), channel_id=1, source_target_pairs={{0,4},{2,6},{4,0},{6,2},{1,5},{3,7},{5,1},{7,3},{8,12},{10,14},{12... | collective-permute-start | bytes 208904 | tf_op jit(solution)/shard_map/ppermute | solution.py:299
  12.2 25.6 %collective-permute-start.15 = (bf16[4,272,128]{2,1,0:T(8,128)(2,1)S(1)}, bf16[4,272,128]{2,1,0:T(8,128)(2,1)S(1)}, u32[]{:S(2)}, u32[]{:S(2)}) collective-permute-start(bf16[4,272,128]{2,1,0:T(8,128)(2,1)S(1)} %bitcast.28), channel_id=1, source_target_pairs={{0,24},{8,16},{16,8},{24,0},{1,25},{9,17},{17,9},{25,1},{2,26},{10... | collective-permute-start | bytes 835592 | tf_op jit(solution)/shard_map/ppermute | solution.py:296
  19.3 13.9 %collective-permute-start.6 = (bf16[2,272,128]{2,1,0:T(8,128)(2,1)}, bf16[2,272,128]{2,1,0:T(8,128)(2,1)S(1)}, u32[]{:S(2)}, u32[]{:S(2)}) collective-permute-start(bf16[2,272,128]{2,1,0:T(8,128)(2,1)} %get-tuple-element.20), channel_id=1, source_target_pairs={{0,2},{2,4},{4,6},{6,0},{1,3},{3,5},{5,7},{7,1},{8,10},{10,12},{12... | collective-permute-start | bytes 417800 | tf_op jit(solution)/shard_map/ppermute | solution.py:299
  19.5 16.1 %collective-permute-start.7 = (bf16[2,272,128]{2,1,0:T(8,128)(2,1)}, bf16[2,272,128]{2,1,0:T(8,128)(2,1)S(1)}, u32[]{:S(2)}, u32[]{:S(2)}) collective-permute-start(bf16[2,272,128]{2,1,0:T(8,128)(2,1)} %get-tuple-element.21), channel_id=1, source_target_pairs={{0,4},{2,6},{4,0},{6,2},{1,5},{3,7},{5,1},{7,3},{8,12},{10,14},{12... | collective-permute-start | bytes 417800 | tf_op jit(solution)/shard_map/ppermute | solution.py:299
  22.3 13.8 %collective-permute-start.8 = (bf16[2,272,128]{2,1,0:T(8,128)(2,1)}, bf16[2,272,128]{2,1,0:T(8,128)(2,1)S(1)}, u32[]{:S(2)}, u32[]{:S(2)}) collective-permute-start(bf16[2,272,128]{2,1,0:T(8,128)(2,1)} %get-tuple-element.22), channel_id=1, source_target_pairs={{0,6},{2,0},{4,2},{6,4},{1,7},{3,1},{5,3},{7,5},{8,14},{10,8},{12,... | collective-permute-start | bytes 417800 | tf_op jit(solution)/shard_map/ppermute | solution.py:299
  24.3 8.2 %collective-permute-start.2 = (bf16[1,272,128]{2,1,0:T(8,128)(2,1)S(1)}, bf16[1,272,128]{2,1,0:T(8,128)(2,1)S(1)}, u32[]{:S(2)}, u32[]{:S(2)}) collective-permute-start(bf16[1,272,128]{2,1,0:T(8,128)(2,1)S(1)} %get-tuple-element.18), channel_id=1, source_target_pairs={{0,6},{2,0},{4,2},{6,4},{1,7},{3,1},{5,3},{7,5},{8,14},{10,8},{12,... | collective-permute-start | bytes 208904 | tf_op jit(solution)/shard_map/ppermute | solution.py:299
  32.5 37.5 %collective-permute-start.22 = (bf16[1,64,8,128]{3,2,1,0:T(8,128)(2,1)S(1)}, bf16[1,64,8,128]{3,2,1,0:T(8,128)(2,1)S(1)}, u32[]{:S(2)}, u32[]{:S(2)}) collective-permute-start(bf16[1,64,8,128]{3,2,1,0:T(8,128)(2,1)S(1)} %constant_dynamic-slice_fusion), channel_id=1, source_target_pairs={{0,24},{8,16},{16,8},{24,0},{1,25},{9,17},{17,9},{25,1},{2,26},{10... | collective-permute-start | bytes 393224 | tf_op jit(solution)/shard_map/ppermute | solution.py:296
  33.2 44.7 %collective-permute-start.23 = (bf16[1,192,8,128]{3,2,1,0:T(8,128)(2,1)S(1)}, bf16[1,192,8,128]{3,2,1,0:T(8,128)(2,1)S(1)}, u32[]{:S(2)}, u32[]{:S(2)}) collective-permute-start(bf16[1,192,8,128]{3,2,1,0:T(8,128)(2,1)S(1)} %constant_dynamic-slice_fusion.2), channel_id=1, source_target_pairs={{0,24},{8,16},{16,8},{24,0},{1,25},{9,17},{17,9},{25,1},{2,26},{10... | collective-permute-start | bytes 1179656 | tf_op jit(solution)/shard_map/ppermute | solution.py:296
  35.6 59.7 %collective-permute-start.24 = (bf16[1,256,8,128]{3,2,1,0:T(8,128)(2,1)}, bf16[1,256,8,128]{3,2,1,0:T(8,128)(2,1)S(1)}, u32[]{:S(2)}, u32[]{:S(2)}) collective-permute-start(bf16[1,256,8,128]{3,2,1,0:T(8,128)(2,1)} %get-tuple-element.25), channel_id=1, source_target_pairs={{0,8},{8,24},{16,0},{24,16},{1,9},{9,25},{17,1},{25,17},{2,10},{10... | collective-permute-start | bytes 1572872 | tf_op jit(solution)/shard_map/ppermute | solution.py:296
  36.2 9.9 %collective-permute-start.9 = (bf16[272,128]{1,0:T(8,128)(2,1)S(1)}, bf16[272,128]{1,0:T(8,128)(2,1)S(1)}, u32[]{:S(2)}, u32[]{:S(2)}) collective-permute-start(bf16[272,128]{1,0:T(8,128)(2,1)S(1)} %get-tuple-element.23), channel_id=1, source_target_pairs={{0,16},{8,0},{16,24},{24,8},{1,17},{9,1},{17,25},{25,9},{2,18},{10... | collective-permute-start | bytes 208904 | tf_op jit(solution)/shard_map/ppermute | solution.py:296
  37.8 20.5 %collective-permute-start.10 = (bf16[272,128]{1,0:T(8,128)(2,1)S(1)}, bf16[272,128]{1,0:T(8,128)(2,1)S(1)}, u32[]{:S(2)}, u32[]{:S(2)}) collective-permute-start(bf16[272,128]{1,0:T(8,128)(2,1)S(1)} %get-tuple-element.24), channel_id=1, source_target_pairs={{0,8},{8,24},{16,0},{24,16},{1,9},{9,25},{17,1},{25,17},{2,10},{10... | collective-permute-start | bytes 208904 | tf_op jit(solution)/shard_map/ppermute | solution.py:296
  46.1 15.6 %collective-permute-start.18 = (bf16[1,272,128]{2,1,0:T(8,128)(2,1)S(1)}, bf16[1,272,128]{2,1,0:T(8,128)(2,1)S(1)}, u32[]{:S(2)}, u32[]{:S(2)}) collective-permute-start(bf16[1,272,128]{2,1,0:T(8,128)(2,1)S(1)} %get-tuple-element.27), channel_id=1, source_target_pairs={{0,6},{2,0},{4,2},{6,4},{1,7},{3,1},{5,3},{7,5},{8,14},{10,8},{12,... | collective-permute-start | bytes 208904 | tf_op jit(solution)/shard_map/ppermute | solution.py:299
  61.7 7.5 %collective-permute-start.16 = (bf16[1,272,128]{2,1,0:T(8,128)(2,1)S(1)}, bf16[1,272,128]{2,1,0:T(8,128)(2,1)S(1)}, u32[]{:S(2)}, u32[]{:S(2)}) collective-permute-start(bf16[1,272,128]{2,1,0:T(8,128)(2,1)S(1)} %get-tuple-element.29), channel_id=1, source_target_pairs={{0,2},{2,4},{4,6},{6,0},{1,3},{3,5},{5,7},{7,1},{8,10},{10,12},{12... | collective-permute-start | bytes 208904 | tf_op jit(solution)/shard_map/ppermute | solution.py:299
  64.2 7.6 %collective-permute-start.5 = (bf16[1,272,128]{2,1,0:T(8,128)(2,1)S(1)}, bf16[1,272,128]{2,1,0:T(8,128)(2,1)S(1)}, u32[]{:S(2)}, u32[]{:S(2)}) collective-permute-start(bf16[1,272,128]{2,1,0:T(8,128)(2,1)S(1)} %bitcast.24), channel_id=1, source_target_pairs={{0,6},{2,0},{4,2},{6,4},{1,7},{3,1},{5,3},{7,5},{8,14},{10,8},{12,... | collective-permute-start | bytes 208904 | tf_op jit(solution)/shard_map/ppermute | solution.py:299
  70.0 7.8 %collective-permute-start.3 = (bf16[1,272,128]{2,1,0:T(8,128)(2,1)S(1)}, bf16[1,272,128]{2,1,0:T(8,128)(2,1)S(1)}, u32[]{:S(2)}, u32[]{:S(2)}) collective-permute-start(bf16[1,272,128]{2,1,0:T(8,128)(2,1)S(1)} %bitcast.26), channel_id=1, source_target_pairs={{0,2},{2,4},{4,6},{6,0},{1,3},{3,5},{5,7},{7,1},{8,10},{10,12},{12... | collective-permute-start | bytes 208904 | tf_op jit(solution)/shard_map/ppermute | solution.py:299
  71.8 25.1 %collective-permute-start.14 = (bf16[1,256,8,128]{3,2,1,0:T(8,128)(2,1)S(1)}, bf16[1,256,8,128]{3,2,1,0:T(8,128)(2,1)S(1)}, u32[]{:S(2)}, u32[]{:S(2)}) collective-permute-start(bf16[1,256,8,128]{3,2,1,0:T(8,128)(2,1)S(1)} %copy-done.8), channel_id=1, source_target_pairs={{0,16},{8,0},{16,24},{24,8},{1,17},{9,1},{17,25},{25,9},{2,18},{10... | collective-permute-start | bytes 1572872 | tf_op jit(solution)/shard_map/ppermute | solution.py:296
  79.9 13.0 %collective-permute-start.13 = (bf16[2,256,128]{2,1,0:T(8,128)(2,1)S(1)}, bf16[2,256,128]{2,1,0:T(8,128)(2,1)S(1)}, u32[]{:S(2)}, u32[]{:S(2)}) collective-permute-start(bf16[2,256,128]{2,1,0:T(8,128)(2,1)S(1)} %pad_maximum_fusion.refs_0_), channel_id=1, source_target_pairs={{0,6},{2,0},{4,2},{6,4},{1,7},{3,1},{5,3},{7,5},{8,14},{10,8},{12,... | collective-permute-start | bytes 393224 | tf_op jit(solution)/shard_map/ppermute | solution.py:299
  84.9 10.4 %collective-permute-start.12 = (bf16[2,256,128]{2,1,0:T(8,128)(2,1)S(1)}, bf16[2,256,128]{2,1,0:T(8,128)(2,1)S(1)}, u32[]{:S(2)}, u32[]{:S(2)}) collective-permute-start(bf16[2,256,128]{2,1,0:T(8,128)(2,1)S(1)} %pad_maximum_fusion.refs_0_), channel_id=1, source_target_pairs={{0,4},{2,6},{4,0},{6,2},{1,5},{3,7},{5,1},{7,3},{8,12},{10,14},{12... | collective-permute-start | bytes 393224 | tf_op jit(solution)/shard_map/ppermute | solution.py:299
  84.9 10.3 %collective-permute-start.11 = (bf16[2,256,128]{2,1,0:T(8,128)(2,1)S(1)}, bf16[2,256,128]{2,1,0:T(8,128)(2,1)S(1)}, u32[]{:S(2)}, u32[]{:S(2)}) collective-permute-start(bf16[2,256,128]{2,1,0:T(8,128)(2,1)S(1)} %pad_maximum_fusion.refs_0_), channel_id=1, source_target_pairs={{0,2},{2,4},{4,6},{6,0},{1,3},{3,5},{5,7},{7,1},{8,10},{10,12},{12... | collective-permute-start | bytes 393224 | tf_op jit(solution)/shard_map/ppermute | solution.py:299
  98.6 14.8 %collective-permute-start.34 = (bf16[256,1024]{1,0:T(8,128)(2,1)S(1)}, bf16[256,1024]{1,0:T(8,128)(2,1)S(1)}, u32[]{:S(2)}, u32[]{:S(2)}) collective-permute-start(bf16[256,1024]{1,0:T(8,128)(2,1)S(1)} %fusion.61), channel_id=1, source_target_pairs={{0,16},{8,0},{16,24},{24,8},{1,17},{9,1},{17,25},{25,9},{2,18},{10... | collective-permute-start | bytes 1572872 | tf_op jit(solution)/shard_map/ppermute | solution.py:296
  98.7 15.6 %collective-permute-start.31 = (bf16[256,1024]{1,0:T(8,128)(2,1)S(1)}, bf16[256,1024]{1,0:T(8,128)(2,1)S(1)}, u32[]{:S(2)}, u32[]{:S(2)}) collective-permute-start(bf16[256,1024]{1,0:T(8,128)(2,1)S(1)} %fusion.58), channel_id=1, source_target_pairs={{0,8},{8,24},{16,0},{24,16},{1,9},{9,25},{17,1},{25,17},{2,10},{10... | collective-permute-start | bytes 1572872 | tf_op jit(solution)/shard_map/ppermute | solution.py:296
  101.4 23.3 %collective-permute-start.28 = (bf16[256,1024]{1,0:T(8,128)(2,1)S(1)}, bf16[256,1024]{1,0:T(8,128)(2,1)S(1)}, u32[]{:S(2)}, u32[]{:S(2)}) collective-permute-start(bf16[256,1024]{1,0:T(8,128)(2,1)S(1)} %fusion.55), channel_id=1, source_target_pairs={{0,16},{8,0},{16,24},{24,8},{1,17},{9,1},{17,25},{25,9},{2,18},{10... | collective-permute-start | bytes 1572872 | tf_op jit(solution)/shard_map/ppermute | solution.py:296
  102.3 23.2 %collective-permute-start.25 = (bf16[256,1024]{1,0:T(8,128)(2,1)S(1)}, bf16[256,1024]{1,0:T(8,128)(2,1)S(1)}, u32[]{:S(2)}, u32[]{:S(2)}) collective-permute-start(bf16[256,1024]{1,0:T(8,128)(2,1)S(1)} %fusion.52), channel_id=1, source_target_pairs={{0,8},{8,24},{16,0},{24,16},{1,9},{9,25},{17,1},{25,17},{2,10},{10... | collective-permute-start | bytes 1572872 | tf_op jit(solution)/shard_map/ppermute | solution.py:296
  114.2 21.7 %collective-permute-start.35 = (bf16[256,1024]{1,0:T(8,128)(2,1)S(1)}, bf16[256,1024]{1,0:T(8,128)(2,1)S(1)}, u32[]{:S(2)}, u32[]{:S(2)}) collective-permute-start(bf16[256,1024]{1,0:T(8,128)(2,1)S(1)} %fusion.64), channel_id=1, source_target_pairs={{0,16},{8,0},{16,24},{24,8},{1,17},{9,1},{17,25},{25,9},{2,18},{10... | collective-permute-start | bytes 1572872 | tf_op jit(solution)/shard_map/ppermute | solution.py:296
  115.0 21.7 %collective-permute-start.32 = (bf16[256,1024]{1,0:T(8,128)(2,1)S(1)}, bf16[256,1024]{1,0:T(8,128)(2,1)S(1)}, u32[]{:S(2)}, u32[]{:S(2)}) collective-permute-start(bf16[256,1024]{1,0:T(8,128)(2,1)S(1)} %fusion.70), channel_id=1, source_target_pairs={{0,8},{8,24},{16,0},{24,16},{1,9},{9,25},{17,1},{25,17},{2,10},{10... | collective-permute-start | bytes 1572872 | tf_op jit(solution)/shard_map/ppermute | solution.py:296
  125.4 21.7 %collective-permute-start.29 = (bf16[256,1024]{1,0:T(8,128)(2,1)S(1)}, bf16[256,1024]{1,0:T(8,128)(2,1)S(1)}, u32[]{:S(2)}, u32[]{:S(2)}) collective-permute-start(bf16[256,1024]{1,0:T(8,128)(2,1)S(1)} %fusion.76), channel_id=1, source_target_pairs={{0,16},{8,0},{16,24},{24,8},{1,17},{9,1},{17,25},{25,9},{2,18},{10... | collective-permute-start | bytes 1572872 | tf_op jit(solution)/shard_map/ppermute | solution.py:296
  126.3 21.7 %collective-permute-start.26 = (bf16[256,1024]{1,0:T(8,128)(2,1)S(1)}, bf16[256,1024]{1,0:T(8,128)(2,1)S(1)}, u32[]{:S(2)}, u32[]{:S(2)}) collective-permute-start(bf16[256,1024]{1,0:T(8,128)(2,1)S(1)} %fusion.82), channel_id=1, source_target_pairs={{0,8},{8,24},{16,0},{24,16},{1,9},{9,25},{17,1},{25,17},{2,10},{10... | collective-permute-start | bytes 1572872 | tf_op jit(solution)/shard_map/ppermute | solution.py:296
  136.7 32.5 %collective-permute-start.36 = (bf16[256,1024]{1,0:T(8,128)(2,1)S(1)}, bf16[256,1024]{1,0:T(8,128)(2,1)S(1)}, u32[]{:S(2)}, u32[]{:S(2)}) collective-permute-start(bf16[256,1024]{1,0:T(8,128)(2,1)S(1)} %fusion.67), channel_id=1, source_target_pairs={{0,16},{8,0},{16,24},{24,8},{1,17},{9,1},{17,25},{25,9},{2,18},{10... | collective-permute-start | bytes 1572872 | tf_op jit(solution)/shard_map/ppermute | solution.py:296
  137.5 31.7 %collective-permute-start.33 = (bf16[256,1024]{1,0:T(8,128)(2,1)S(1)}, bf16[256,1024]{1,0:T(8,128)(2,1)S(1)}, u32[]{:S(2)}, u32[]{:S(2)}) collective-permute-start(bf16[256,1024]{1,0:T(8,128)(2,1)S(1)} %fusion.73), channel_id=1, source_target_pairs={{0,8},{8,24},{16,0},{24,16},{1,9},{9,25},{17,1},{25,17},{2,10},{10... | collective-permute-start | bytes 1572872 | tf_op jit(solution)/shard_map/ppermute | solution.py:296
  147.9 20.0 %collective-permute-start.30 = (bf16[256,1024]{1,0:T(8,128)(2,1)S(1)}, bf16[256,1024]{1,0:T(8,128)(2,1)S(1)}, u32[]{:S(2)}, u32[]{:S(2)}) collective-permute-start(bf16[256,1024]{1,0:T(8,128)(2,1)S(1)} %fusion.79), channel_id=1, source_target_pairs={{0,16},{8,0},{16,24},{24,8},{1,17},{9,1},{17,25},{25,9},{2,18},{10... | collective-permute-start | bytes 1572872 | tf_op jit(solution)/shard_map/ppermute | solution.py:296
  148.7 19.2 %collective-permute-start.27 = (bf16[256,1024]{1,0:T(8,128)(2,1)S(1)}, bf16[256,1024]{1,0:T(8,128)(2,1)S(1)}, u32[]{:S(2)}, u32[]{:S(2)}) collective-permute-start(bf16[256,1024]{1,0:T(8,128)(2,1)S(1)} %fusion.85), channel_id=1, source_target_pairs={{0,8},{8,24},{16,0},{24,16},{1,9},{9,25},{17,1},{25,17},{2,10},{10... | collective-permute-start | bytes 1572872 | tf_op jit(solution)/shard_map/ppermute | solution.py:296
  (14 other events, 134.6 us)
